TPU v7x, 8 devices: a whole 2x2x1 slice. The times are simulated.
8 devices in a mesh: dp: 2 (over z, y), emb: 4 (over x, core).
Axes of the slice: x: 2, y: 2, z: 1, core: 2. Of those that a mesh axis runs over, the one named last changes fastest.
Arguments:
- tok_ids: int32 [4096], P(('dp', 'emb'))
- resid_in: bfloat16 [4096, 3072], P(('dp', 'emb'))
- cot_out: bfloat16 [4096, 3072], P(('dp', 'emb'))
- tables: bfloat16 [4, 128256, 256], P(None, 'emb')
- w_up: bfloat16 [4, 3072, 8192], replicated
- w_down: bfloat16 [4, 8192, 3072], replicated
- w_gate: bfloat16 [4, 3072, 256], replicated
- w_proj: bfloat16 [4, 256, 3072], replicated
Outputs:
- output 1: bfloat16 [4096, 3072], P(('dp', 'emb'))
- output 2: float32 [4, 128256, 256], P(None, 'emb')
All inputs are finite; a program needn't handle non-finite values.
Results may differ from a plain program's by a relative error of at most 0.0110832.
Values are sent between devices in bfloat16 or wider.
A program may use at most 2.5 GiB of HBM per device.

v0:
```python
import jax
import jax.numpy as jnp
from jax import lax
from jax.sharding import PartitionSpec as P

NORM_EPS = 1e-6


def rms_norm(x_f32):
    return x_f32 * lax.rsqrt(jnp.mean(x_f32 * x_f32, axis=-1, keepdims=True) + NORM_EPS)


def layer_forward(resid_cur, fetched, w_up_l, w_down_l, w_gate_l, w_proj_l):
    x_f32 = resid_cur.astype(jnp.float32)
    normed = rms_norm(x_f32).astype(jnp.bfloat16)
    up_pre = jnp.dot(normed, w_up_l, preferred_element_type=jnp.float32)
    hidden = jax.nn.gelu(up_pre).astype(jnp.bfloat16)
    mlp_out = jnp.dot(hidden, w_down_l, preferred_element_type=jnp.float32)
    gate_pre = jnp.dot(normed, w_gate_l, preferred_element_type=jnp.float32)
    gate_act = jax.nn.gelu(gate_pre)
    mixed_in = (gate_act * fetched.astype(jnp.float32)).astype(jnp.bfloat16)
    proj_out = jnp.dot(mixed_in, w_proj_l, preferred_element_type=jnp.float32)
    resid_next = (x_f32 + mlp_out + proj_out).astype(jnp.bfloat16)
    return resid_next, (resid_cur, up_pre, gate_pre, gate_act, fetched)


def layer_backward(cot_next, layer_saved, w_up_l, w_down_l, w_gate_l, w_proj_l):
    resid_cur, up_pre, gate_pre, gate_act, fetched = layer_saved
    d_mixed = jnp.einsum('td,ed->te', cot_next, w_proj_l, preferred_element_type=jnp.float32).astype(jnp.bfloat16).astype(jnp.float32)
    grad_rows = gate_act * d_mixed
    d_gate_act = d_mixed * fetched.astype(jnp.float32)
    d_gate_pre = jax.vjp(jax.nn.gelu, gate_pre)[1](d_gate_act)[0]
    d_hidden = jnp.einsum('td,fd->tf', cot_next, w_down_l, preferred_element_type=jnp.float32).astype(jnp.bfloat16)
    d_up_pre = jax.vjp(jax.nn.gelu, up_pre)[1](d_hidden.astype(jnp.float32))[0]
    d_norm_mlp = jnp.einsum('tf,df->td', d_up_pre.astype(jnp.bfloat16), w_up_l, preferred_element_type=jnp.float32).astype(jnp.bfloat16)
    d_norm_gate = jnp.einsum('te,de->td', d_gate_pre.astype(jnp.bfloat16), w_gate_l, preferred_element_type=jnp.float32).astype(jnp.bfloat16)
    d_normed = (d_norm_mlp + d_norm_gate).astype(jnp.float32)
    d_x_norm = jax.vjp(rms_norm, resid_cur.astype(jnp.float32))[1](d_normed)[0]
    cot_cur = (cot_next.astype(jnp.float32) + d_x_norm).astype(jnp.bfloat16)
    return cot_cur, grad_rows


def route_plan(tok_ids, range_rows, n_emb, cap_rows):
    owner_ids = tok_ids // range_rows
    local_off = tok_ids - owner_ids * range_rows
    one_hot = (owner_ids[:, None] == jnp.arange(n_emb, dtype=jnp.int32)[None, :]).astype(jnp.int32)
    rank_in = jnp.sum((jnp.cumsum(one_hot, axis=0) - one_hot) * one_hot, axis=1)
    slot_of = owner_ids * cap_rows + rank_in
    tok_count = tok_ids.shape[0]
    slot_token = jnp.zeros((n_emb * cap_rows,), jnp.int32).at[slot_of].set(jnp.arange(tok_count, dtype=jnp.int32))
    slot_mask = jnp.zeros((n_emb * cap_rows,), jnp.float32).at[slot_of].set(1.0)
    send_ids = jnp.where(slot_mask > 0, jnp.take(local_off, slot_token), 0)
    return slot_of, slot_token, slot_mask, send_ids


def solution(mesh):
    n_emb = mesh.shape['emb']
    tok_spec = P(('dp', 'emb'))
    act_spec = P(('dp', 'emb'), None)
    table_spec = P(None, 'emb', None)
    full_spec = P(None, None, None)

    def device_body(tok_ids, resid_in, cot_out, tables, w_up, w_down, w_gate, w_proj):
        n_layers = tables.shape[0]
        range_rows = tables.shape[1]
        tok_count = tok_ids.shape[0]
        cap_rows = min(2 * tok_count // n_emb, 3 * tok_count // 4)
        slot_of, slot_token, slot_mask, send_ids = route_plan(tok_ids, range_rows, n_emb, cap_rows)
        recv_ids = lax.all_to_all(send_ids, 'emb', 0, 0, tiled=True)
        resid_cur = resid_in
        saved_acts = []
        for l_idx in range(n_layers):
            served = jnp.take(tables[l_idx], recv_ids, axis=0)
            returned = lax.all_to_all(served, 'emb', 0, 0, tiled=True)
            fetched = jnp.take(returned, slot_of, axis=0)
            resid_cur, layer_saved = layer_forward(resid_cur, fetched, w_up[l_idx], w_down[l_idx], w_gate[l_idx], w_proj[l_idx])
            saved_acts.append(layer_saved)
        cot_cur = cot_out
        grad_list = [None] * n_layers
        for l_idx in reversed(range(n_layers)):
            cot_cur, grad_rows = layer_backward(cot_cur, saved_acts[l_idx], w_up[l_idx], w_down[l_idx], w_gate[l_idx], w_proj[l_idx])
            outgoing = jnp.take(grad_rows, slot_token, axis=0) * slot_mask[:, None]
            incoming = lax.all_to_all(outgoing, 'emb', 0, 0, tiled=True)
            shard_grad = jax.ops.segment_sum(incoming, recv_ids, num_segments=range_rows)
            grad_list[l_idx] = lax.psum(shard_grad, 'dp')
        return resid_cur, jnp.stack(grad_list)

    return jax.shard_map(device_body, mesh=mesh, in_specs=(tok_spec, act_spec, act_spec, table_spec, full_spec, full_spec, full_spec, full_spec), out_specs=(act_spec, table_spec), check_vma=False)
```

profile of v0, /device:TPU:0, one launch (start us, length us, event | category | flops | bytes accessed | tf_op | source)
XLA Modules:
  0.0 3690.8 jit_solution(18064345364236410452)
XLA Ops:
  29.8 43.5 %slice_bitcast_fusion = (bf16[32064,256]{1,0:T(8,128)(2,1)}, bf16[32064,256]{1,0:T(8,128)(2,1)}, bf16[32064,256]{1,0:T(8,128)(2,1)}, bf16[32064,256]{1,0:T(8,128)(2,1)}) fusion(bf16[4,32064,256]{2,1,0:T(8,128)(2,1)} %param.17), kind=kLoop, calls=%fused_computation.124 | loop fusion | bytes 131334144 | tf_op jit(solution)/shard_map/squeeze | solution.py:73
  73.3 35.9 fusion.79.clone.5
  109.2 35.0 fusion.24
  215.4 34.3 fusion.22
  260.2 32.7 fusion.18
  297.0 33.8 fusion.14
  341.4 32.7 fusion.10
  378.3 33.9 fusion.6
  422.7 44.7 %fusion.44.clone.7 = bf16[512,8192]{1,0:T(8,128)(2,1)} fusion(f32[512,8192]{1,0:T(8,128)} %fusion.6, bf16[512,3072]{1,0:T(8,128)(2,1)} %param.16, bf16[4,8192,3072]{2,1,0:T(8,128)(2,1)} %param.19), kind=kOutput, calls=%fused_computation.77.clone.clone.clone.clone.clone.2 | convolution fusion | flops 25862078464 | bytes 78643200 | tf_op jit(solution)/shard_map/td,fd->tf/dot_general | solution.py:33
  467.4 33.1 fusion.182
  508.4 44.7 %fusion.49.clone.7 = bf16[512,8192]{1,0:T(8,128)(2,1)} fusion(f32[512,8192]{1,0:T(8,128)} %fusion.14, bf16[512,3072]{1,0:T(8,128)(2,1)} %fusion.152, bf16[4,8192,3072]{2,1,0:T(8,128)(2,1)} %param.19), kind=kOutput, calls=%fused_computation.82.clone.clone.clone.clone.clone.2 | convolution fusion | flops 25862078464 | bytes 78643200 | tf_op jit(solution)/shard_map/td,fd->tf/dot_general | solution.py:33
  556.6 34.0 fusion.177
  598.9 44.7 %fusion.54.clone.7 = bf16[512,8192]{1,0:T(8,128)(2,1)} fusion(f32[512,8192]{1,0:T(8,128)} %fusion.22, bf16[512,3072]{1,0:T(8,128)(2,1)} %fusion.154, bf16[4,8192,3072]{2,1,0:T(8,128)(2,1)} %param.19), kind=kOutput, calls=%fused_computation.87.clone.clone.clone.clone.clone.2 | convolution fusion | flops 25862078464 | bytes 78643200 | tf_op jit(solution)/shard_map/td,fd->tf/dot_general | solution.py:33
  651.4 33.8 fusion.172
  710.7 17.5 all_to_all.108
  728.2 19.3 scatter_custom_fusion.2
  748.7 17.2 all_to_all.109
  786.4 20.1 scatter_custom_fusion.5
  806.5 19.3 scatter_custom_fusion.4
  825.8 19.5 scatter_custom_fusion.3
  845.4 32.7 fusion.2
  882.3 582.7 %all-reduce.4.cloned.1.call-done = f32[1,32064,256]{2,1,0:T(8,128)} async-done(((f32[1,32064,256]{2,1,0:T(8,128)}), f32[1,32064,256]{2,1,0:T(8,128)}) %all-reduce.4.cloned.1.call-update) | async-done | bytes 32833552 | tf_op jit(solution)/shard_map/psum | solution.py:85
  1465.0 2132.6 %all-reduce.6.cloned.1.call-done = (f32[1,32064,256]{2,1,0:T(8,128)}, f32[1,32064,256]{2,1,0:T(8,128)}, f32[1,32064,256]{2,1,0:T(8,128)}) async-done(((f32[1,32064,256]{2,1,0:T(8,128)}, f32[1,32064,256]{2,1,0:T(8,128)}, f32[1,32064,256]{2,1,0:T(8,128)}), (f32[1,32064,256]{2,1,0:T(8,128)}, f32[1,32064,256]{2,1,0:T(8,128)}, f32[1,32064,256]{2,1,0:T(8,128)})) %all-reduce.6.cloned.1.call-update) | async-done | bytes 98500624 | tf_op jit(solution)/shard_map/psum | solution.py:85
  3597.7 86.0 %pad_maximum_fusion = f32[4,32064,256]{2,1,0:T(8,128)} fusion(f32[1,32064,256]{2,1,0:T(8,128)} %get-tuple-element.4, f32[1,32064,256]{2,1,0:T(8,128)} %get-tuple-element.6, f32[1,32064,256]{2,1,0:T(8,128)} %get-tuple-element.7, f32[1,32064,256]{2,1,0:T(8,128)} %all-reduce.4.cloned.1.call-done), kind=kLoop, calls=%fused_computation.19 | loop fusion | flops 98500608 | bytes 262668288 | tf_op jit(solution)/shard_map/stack | solution.py:86
  (170 shorter events, 211.9 us)
Async XLA Ops:
  22.6 121.6 %all-to-all-start = ((s32[4,256,1]{1,2,0:T(1,128)}), s32[4,256,1]{1,2,0:T(1,128)S(1)}, u32[]{:S(2)}, u32[]{:S(2)}) async-start(s32[4,256,1]{1,2,0:T(1,128)} %bitcast.5), calls=%async_computation | async-start | bytes 8192 | tf_op jit(solution)/shard_map/all_to_all | solution.py:69
  29.8 43.5 %copy-start.7 = (bf16[512,3072]{1,0:T(8,128)(2,1)S(1)}, bf16[512,3072]{1,0:T(8,128)(2,1)}, u32[]{:S(2)}) copy-start(bf16[512,3072]{1,0:T(8,128)(2,1)} %param.15) | copy-start | bytes 9437188
  109.2 35.0 copy-start.43
  144.2 45.6 %copy-start.31 = (s32[4,256,1]{1,2,0:T(1,128)}, s32[4,256,1]{1,2,0:T(1,128)S(1)}, u32[]{:S(2)}) copy-start(s32[4,256,1]{1,2,0:T(1,128)S(1)} %all-to-all-done) | copy-start | bytes 12292
  191.4 12.1 all-to-all-start.1
  203.4 50.4 %all-to-all-start.2 = ((bf16[4,256,256]{2,1,0:T(8,128)(2,1)}), bf16[4,256,256]{2,1,0:T(8,128)(2,1)S(1)}, u32[]{:S(2)}, u32[]{:S(2)}) async-start(bf16[4,256,256]{2,1,0:T(8,128)(2,1)} %bitcast.15), calls=%async_computation.2 | async-start | bytes 1048576 | tf_op jit(solution)/shard_map/all_to_all | solution.py:74
  215.3 34.3 copy-start.32
  215.4 34.3 copy-start.45
  253.8 80.3 %all-to-all-start.3 = ((bf16[4,256,256]{2,1,0:T(8,128)(2,1)}), bf16[4,256,256]{2,1,0:T(8,128)(2,1)}, u32[]{:S(2)}, u32[]{:S(2)}) async-start(bf16[4,256,256]{2,1,0:T(8,128)(2,1)} %bitcast.22), calls=%async_computation.3 | async-start | bytes 1048576 | tf_op jit(solution)/shard_map/all_to_all | solution.py:74
  296.4 34.4 copy-start.4
  297.0 33.8 copy-start.40
  334.1 81.3 %all-to-all-start.4 = ((bf16[4,256,256]{2,1,0:T(8,128)(2,1)}), bf16[4,256,256]{2,1,0:T(8,128)(2,1)}, u32[]{:S(2)}, u32[]{:S(2)}) async-start(bf16[4,256,256]{2,1,0:T(8,128)(2,1)} %bitcast.257), calls=%async_computation.4 | async-start | bytes 1048576 | tf_op jit(solution)/shard_map/all_to_all | solution.py:74
  338.3 1126.7 %all-reduce.4.cloned.1.call-start = ((), (), s32[]{:S(2)}) async-start(), calls=%async_computation.9 | async-start | bytes 65667072 | tf_op jit(solution)/shard_map/psum | solution.py:85
  377.7 126.6 %copy-start.2 = (bf16[512,3072]{1,0:T(8,128)(2,1)}, bf16[512,3072]{1,0:T(8,128)(2,1)S(1)}, u32[]{:S(2)}) copy-start(bf16[512,3072]{1,0:T(8,128)(2,1)S(1)} %get-tuple-element.31) | copy-start | bytes 9437188
  418.1 82.4 %copy-start.14 = (bf16[512,256]{1,0:T(8,128)(2,1)}, bf16[512,256]{1,0:T(8,128)(2,1)S(1)}, u32[]{:S(2)}) copy-start(bf16[512,256]{1,0:T(8,128)(2,1)S(1)} %gather_fusion.8) | copy-start | bytes 786436
  467.4 33.1 copy-start.47
  508.4 44.7 %copy-start.10 = (bf16[512,3072]{1,0:T(8,128)(2,1)S(1)}, bf16[512,3072]{1,0:T(8,128)(2,1)}, u32[]{:S(2)}) copy-start(bf16[512,3072]{1,0:T(8,128)(2,1)} %fusion.152) | copy-start | bytes 9437188
  556.6 34.0 copy-start.6
  556.6 34.0 copy-start.19
  598.9 44.7 %copy-start.25 = (f32[512,256]{1,0:T(8,128)S(1)}, f32[512,256]{1,0:T(8,128)}, u32[]{:S(2)}) copy-start(f32[512,256]{1,0:T(8,128)} %fusion.208) | copy-start | bytes 1572868
  598.9 49.0 %copy-start.28 = (s32[1024]{0:T(1024)S(1)}, s32[1024]{0:T(1024)}, u32[]{:S(2)}) copy-start(s32[1024]{0:T(1024)} %copy-done.27) | copy-start | bytes 12292
  651.4 33.8 copy-start.1
  782.8 43.0 %all-to-all-start.6 = ((f32[4,256,256]{2,1,0:T(8,128)}), f32[4,256,256]{2,1,0:T(8,128)S(1)}, u32[]{:S(2)}, u32[]{:S(2)}) async-start(f32[4,256,256]{2,1,0:T(8,128)} %bitcast.35), calls=%async_computation.6 | async-start | bytes 2097152 | tf_op jit(solution)/shard_map/all_to_all | solution.py:83
  786.3 2811.3 %all-reduce.6.cloned.1.call-start = ((), (), s32[]{:S(2)}) async-start(), calls=%async_computation.10 | async-start | bytes 197001216 | tf_op jit(solution)/shard_map/psum | solution.py:85
  (32 other events, 507.8 us)
Sparse Core Ops, SparseCore 0:
  747.6 717.3 all-reduce.3
  1468.2 2129.4 all-reduce.5
where the time goes:
time: 3700 us; the launch traced here: 3690 us
  waiting for transfers between devices  2720 us (74%)
  matrix products  567 us (15%)
  other arithmetic  183 us (5%)
  local copies, waits for them, and re-layouts  130 us (4%)
  blocking collectives  51.6 us (1%)
    psum x2, waiting for transfers between devices, device_body(): grad_list[l_idx] = lax.psum(shard_grad, 'dp')  2720 us
    dot_general x4, matrix products, layer_forward(): up_pre = jnp.dot(normed, w_up_l, preferred_element_type=jnp.float32)  138 us
    dot_general x3, matrix products, layer_backward(): jnp.einsum('td,fd->tf', cot_next, w_down_l, preferred_element_type=jnp.fl...  134 us
    dot_general x4, matrix products, layer_forward(): mlp_out = jnp.dot(hidden, w_down_l, preferred_element_type=jnp.float32)  133 us
    dot_general x3, matrix products, layer_backward(): jnp.einsum('tf,df->td', d_up_pre.astype(jnp.bfloat16), w_up_l, preferred_...  101 us
    another operation x1, other arithmetic, device_body(): return (resid_cur, jnp.stack(grad_list))  86 us
    scatter-add x4, other arithmetic, device_body(): jax.ops.segment_sum(incoming, recv_ids, num_segments=range_rows)  78.2 us
  transfers between devices with their start and end apart: 8, of which 3 were waited for; matrix products, arithmetic and copies ran while one was open for 11% of the time, Pallas kernels for 0%

commit v1 on v0

v1 whole, which is shorter than its diff:
```python
import functools

import jax
import jax.numpy as jnp
from jax import lax
from jax.experimental import pallas as pl
from jax.experimental.pallas import tpu as pltpu
from jax.sharding import PartitionSpec as P

NORM_EPS = 1e-6
BF = jnp.bfloat16
F32 = jnp.float32
I32 = jnp.int32
VMEM_BYTES = 67043328
GELU_C = 0.7978845608028654
GELU_A = 0.044715

MESH_AXES = ('dp', 'emb')
CAP = 256


def gelu(x):
    return 0.5 * x * (1.0 + jnp.tanh(GELU_C * (x + GELU_A * (x * x * x))))


def gelu_slope(x):
    sq = x * x
    th = jnp.tanh(GELU_C * (x + GELU_A * (x * sq)))
    return 0.5 * (1.0 + th) + (0.5 * GELU_C) * x * (1.0 - th * th) * (1.0 + (3 * GELU_A) * sq)


def dot(a, b):
    return jnp.dot(a, b, preferred_element_type=F32)


def dot_t(a, b):
    return lax.dot_general(a, b, (((1,), (1,)), ((), ())), preferred_element_type=F32)


def row_loop(rows, slab, unroll=2):
    def run(body):
        def step(i, carry):
            body(pl.ds(pl.multiple_of(i * slab, slab), slab))
            return carry

        lax.fori_loop(0, rows // slab, step, 0, unroll=unroll)

    return run


def forward_kernel(cfg, x_hbm, cot_hbm, fet_ref, wg_ref, wp_ref, wu_ref, wd_ref,
                   out_hbm, saved_hbm, up_ref, gate_ref, rows_ref, dgp_ref, dtab_hbm,
                   x_s, u_s, acc_s, h_s, zero_s, in_sem, out_sem, z_sem):
    n_layers, n_blk, cw, nw, slab, z_per, z_chunks = cfg
    layer, blk = pl.program_id(0), pl.program_id(1)
    tok, dim = x_s.shape
    fb = wu_ref.shape[2]
    step = layer * n_blk + blk
    z_rows = zero_s.shape[0]

    def z_copy(j):
        c = step * z_per + j
        zl = c // z_chunks
        zc = c - zl * z_chunks
        return pltpu.make_async_copy(zero_s, dtab_hbm.at[zl, pl.ds(pl.multiple_of(zc * z_rows, 8), z_rows), :], z_sem.at[j])

    def norm_rows(sl, x):
        scale = lax.rsqrt(jnp.mean(x * x, axis=-1, keepdims=True) + NORM_EPS)
        u_s[sl, :] = (x * scale).astype(BF)
        acc_s[sl, :] = x

    @pl.when(step == 0)
    def _():
        fetch = pltpu.make_async_copy(x_hbm, x_s, in_sem)
        fetch.start()
        row_loop(z_rows, 8, 1)(lambda sl: zero_s.__setitem__((sl, slice(None)), jnp.zeros((8, zero_s.shape[1]), F32)))
        fetch.wait()
        row_loop(tok, slab)(lambda sl: norm_rows(sl, x_s[sl, :].astype(F32)))

    for j in range(z_per):
        @pl.when(step > 0)
        def _():
            z_copy(j).wait()

        z_copy(j).start()

    @pl.when(blk == 0)
    def _():
        gate_ref[0] = dot(u_s[...], wg_ref[0])

    for c in range(fb // cw):
        cs = slice(c * cw, (c + 1) * cw)
        up = dot(u_s[...], wu_ref[0, :, cs])
        up_ref[0, :, cs] = up
        h_s[:, cs] = gelu(up).astype(BF)
    for n in range(dim // nw):
        ns = slice(n * nw, (n + 1) * nw)
        acc_s[:, ns] += dot(h_s[...], wd_ref[0, :, ns])

    @pl.when(blk == n_blk - 1)
    def _():
        mixed = (gelu(gate_ref[0]) * fet_ref[0].astype(F32)).astype(BF)
        for n in range(dim // nw):
            ns = slice(n * nw, (n + 1) * nw)
            acc_s[:, ns] += dot(mixed, wp_ref[0, :, ns])

        @pl.when(layer > 0)
        def _():
            pltpu.make_async_copy(x_s, saved_hbm.at[layer - 1], out_sem).wait()

        def next_rows(sl):
            x_new = acc_s[sl, :].astype(BF)
            x_s[sl, :] = x_new
            norm_rows(sl, x_new.astype(F32))

        row_loop(tok, slab)(next_rows)

        @pl.when(layer < n_layers - 1)
        def _():
            pltpu.make_async_copy(x_s, saved_hbm.at[layer], out_sem).start()

        @pl.when(layer == n_layers - 1)
        def _():
            put = pltpu.make_async_copy(x_s, out_hbm, out_sem)
            put.start()
            get = pltpu.make_async_copy(cot_hbm, u_s, in_sem)
            get.start()
            for j in range(z_per):
                z_copy(j).wait()
            get.wait()
            d_mixed = dot_t(u_s[...], wp_ref[0]).astype(BF).astype(F32)
            gate_grads(gate_ref[0], fet_ref[0], d_mixed, rows_ref, dgp_ref)
            put.wait()


def gate_grads(gate_pre, fetched, d_mixed, rows_ref, dgp_ref):
    rows_ref[...] = gelu(gate_pre) * d_mixed
    dgp_ref[...] = (d_mixed * fetched.astype(F32) * gelu_slope(gate_pre)).astype(BF)


def backward_kernel(cfg, cot_ref, x_ref, up_ref, wu_ref, wd_ref, wg_ref, wp_ref, gate_ref, fet_ref, dgp_in_ref,
                    cot_out_ref, rows_ref, dgp_ref, acc_s, dup_s, dng_s):
    n_blk, cw, nw, slab = cfg
    blk = pl.program_id(0)
    tok, dim = cot_ref.shape
    fb = wu_ref.shape[2]

    @pl.when(blk == 0)
    def _():
        for n in range(dim // nw):
            ns = slice(n * nw, (n + 1) * nw)
            dng_s[:, ns] = dot_t(dgp_in_ref[...], wg_ref[0, ns, :]).astype(BF)

        def clear(sl):
            acc_s[sl, :] = jnp.zeros((slab, dim), F32)

        row_loop(tok, slab)(clear)

    for c in range(fb // cw):
        cs = slice(c * cw, (c + 1) * cw)
        d_hid = dot_t(cot_ref[...], wd_ref[0, cs, :]).astype(BF).astype(F32)
        dup_s[:, cs] = (d_hid * gelu_slope(up_ref[0, :, cs])).astype(BF)
    for n in range(dim // nw):
        ns = slice(n * nw, (n + 1) * nw)
        acc_s[:, ns] += dot_t(dup_s[...], wu_ref[0, ns, :])

    @pl.when(blk == n_blk - 1)
    def _():
        def rows_back(sl):
            x = x_ref[0, sl, :].astype(F32)
            scale = lax.rsqrt(jnp.mean(x * x, axis=-1, keepdims=True) + NORM_EPS)
            d_n = (acc_s[sl, :].astype(BF).astype(F32) + dng_s[sl, :].astype(F32)).astype(BF).astype(F32)
            proj = jnp.mean(d_n * x, axis=-1, keepdims=True)
            d_x = d_n * scale - x * (proj * (scale * scale * scale))
            cot_out_ref[sl, :] = (cot_ref[sl, :].astype(F32) + d_x).astype(BF)

        row_loop(tok, slab)(rows_back)
        d_mixed = dot_t(cot_out_ref[...], wp_ref[0]).astype(BF).astype(F32)
        gate_grads(gate_ref[0], fet_ref[0], d_mixed, rows_ref, dgp_ref)


def gather_kernel(cfg, loc_ref, pick_ref, tables_hbm, out_ref, buf, sems):
    n_layers, n_slots, per_sem, per_dot, group = cfg

    def issue(s, carry):
        base = pl.multiple_of(jnp.left_shift(jnp.right_shift(loc_ref[s], 3), 3), 8)
        pltpu.make_async_copy(
            tables_hbm.at[:, pl.ds(base, 8), :], buf.at[:, pl.ds(pl.multiple_of(s * 8, 8), 8), :], sems.at[s // per_sem]
        ).start()
        return carry

    lax.fori_loop(0, n_slots, issue, 0, unroll=8)
    per_trip = per_dot * group

    def pick(g, carry):
        @pl.when(lax.rem(g * per_trip, per_sem) == 0)
        def _():
            part = buf.at[:, pl.ds(pl.multiple_of(g * per_trip * 8, 8), per_sem * 8), :]
            pltpu.make_async_copy(part, part, sems.at[g * per_trip // per_sem]).wait()

        for k in range(group):
            s0 = pl.multiple_of(g * per_trip + k * per_dot, per_dot)
            want = pick_ref[pl.ds(s0, per_dot), :]
            sel = (lax.broadcasted_iota(I32, (per_dot, per_dot * 8), 1) == want).astype(BF)
            for l in range(n_layers):
                rows = buf[l, pl.ds(pl.multiple_of(s0 * 8, 8), per_dot * 8), :]
                out_ref[l, pl.ds(s0, per_dot), :] = dot(sel, rows).astype(BF)
        return carry

    lax.fori_loop(0, n_slots // per_trip, pick, 0)


def scatter_kernel(cfg, keys_ref, meta_ref, rows_ref, dt_in, dt_out, sums, sem):
    first_layer, slot_bits = cfg
    layer = first_layer - pl.program_id(0)
    count = meta_ref[0]

    def add(j, carry):
        acc, prev = carry
        key = keys_ref[j]
        slot = jnp.bitwise_and(key, (1 << slot_bits) - 1)
        row = jnp.right_shift(key, slot_bits)
        acc = jnp.where(row == prev, acc, 0.0) + rows_ref[0, pl.ds(slot, 1), :]
        sums[pl.ds(j, 1), :] = acc
        return acc, row

    lax.fori_loop(0, count, add, (jnp.zeros((1, rows_ref.shape[2]), F32), jnp.int32(-1)))

    def put(j, n):
        row = jnp.right_shift(keys_ref[j], slot_bits)
        last = row != jnp.right_shift(keys_ref[j + 1], slot_bits)

        @pl.when(last)
        def _():
            pltpu.make_async_copy(sums.at[pl.ds(j, 1), :], dt_out.at[layer, pl.ds(row, 1), :], sem).start()

        return n + last.astype(I32)

    n_rows = lax.fori_loop(0, count, put, jnp.int32(0))

    def drain(j, carry):
        pltpu.make_async_copy(sums.at[pl.ds(0, 1), :], dt_out.at[layer, pl.ds(0, 1), :], sem).wait()
        return carry

    lax.fori_loop(0, n_rows, drain, 0)


def solution(mesh):
    n_emb, n_dp = mesh.shape['emb'], mesh.shape['dp']
    n_dev = n_emb * n_dp
    tok_spec = P(('dp', 'emb'))
    act_spec = P(('dp', 'emb'), None)
    table_spec = P(None, 'emb', None)
    full_spec = P(None, None, None)
    hbm = pl.BlockSpec(memory_space=pl.ANY)
    vm = pl.BlockSpec(memory_space=pltpu.VMEM)
    sm = pl.BlockSpec(memory_space=pltpu.SMEM)

    def device_body(tok_ids, resid_in, cot_out, tables, w_up, w_down, w_gate, w_proj):
        n_layers, range_rows, e_dim = tables.shape
        tok = tok_ids.shape[0]
        dim, ffn = w_up.shape[1:]
        n_slots = n_dev * CAP
        my_emb, my_dp = lax.axis_index('emb'), lax.axis_index('dp')

        ids8 = lax.all_gather(tok_ids, MESH_AXES, tiled=True).reshape(n_dev, tok)
        mine = (ids8 // range_rows) == my_emb
        t_iota = jnp.arange(tok, dtype=I32)
        before = t_iota[None, :] < t_iota[:, None]
        rank8 = jnp.sum((mine[:, None, :] & before[None]).astype(I32), axis=-1)
        c_iota = jnp.arange(CAP, dtype=I32)
        hit = mine[:, None, :] & (rank8[:, None, :] == c_iota[None, :, None])
        recv_loc = jnp.sum(jnp.where(hit, (ids8 - my_emb * range_rows)[:, None, :], 0), axis=-1)
        counts = jnp.sum(mine.astype(I32), axis=-1)
        valid = c_iota[None, :] < counts[:, None]
        slot_bits = (n_slots - 1).bit_length()
        keys = jnp.where(valid, recv_loc * n_slots + jnp.arange(n_slots, dtype=I32).reshape(n_dev, CAP), jnp.iinfo(jnp.int32).max)
        skeys = jnp.concatenate([lax.sort(keys.reshape(-1)), jnp.full((8,), jnp.iinfo(jnp.int32).max, I32)])
        total = jnp.sum(counts).reshape(1)

        my_owner = tok_ids // range_rows
        rank = jnp.sum(((my_owner[None, :] == my_owner[:, None]) & before).astype(I32), axis=-1)
        slot_of = my_owner * CAP + rank
        sel_in = slot_of[:, None] == jnp.arange(n_emb * CAP, dtype=I32)[None, :]

        want = lax.dynamic_slice_in_dim(recv_loc, my_dp * n_emb, n_emb, 0).reshape(-1)
        n_serve = n_emb * CAP
        per_dot, group, per_sem = 32, 4, 128
        pick = (jnp.bitwise_and(want, 7) + 8 * (jnp.arange(n_serve, dtype=I32) % per_dot))[:, None]
        served = pl.pallas_call(
            functools.partial(gather_kernel, (n_layers, n_serve, per_sem, per_dot, group)),
            out_shape=jax.ShapeDtypeStruct((n_layers, n_serve, e_dim), BF),
            in_specs=[sm, vm, hbm],
            out_specs=vm,
            scratch_shapes=[pltpu.VMEM((n_layers, n_serve * 8, e_dim), BF), pltpu.SemaphoreType.DMA((n_serve // per_sem,))],
            compiler_params=pltpu.CompilerParams(vmem_limit_bytes=VMEM_BYTES),
            name='table_rows',
        )(want, pick, tables)
        returned = lax.all_to_all(served.reshape(n_layers, n_emb, CAP, e_dim), 'emb', 1, 1, tiled=True)
        fetched = jnp.einsum('tc,lce->lte', sel_in.astype(BF), returned.reshape(n_layers, n_serve, e_dim),
                             preferred_element_type=F32).astype(BF)

        fb = 1024
        n_blk = ffn // fb
        cw, nw, slab = 512, 512, 16
        z_rows = 1336
        z_chunks = range_rows // z_rows
        z_per = n_layers * z_chunks // (n_layers * n_blk)
        assert z_chunks * z_rows == range_rows and z_per * n_blk == z_chunks

        def lsp(*shape):
            return pl.BlockSpec((1,) + shape, lambda l, f: (l, 0, 0))

        matmul_flops = 4 * tok * dim * ffn
        out, saved, ups, gates, rows, dgp, dtab = pl.pallas_call(
            functools.partial(forward_kernel, (n_layers, n_blk, cw, nw, slab, z_per, z_chunks)),
            grid=(n_layers, n_blk),
            out_shape=[
                jax.ShapeDtypeStruct((tok, dim), BF),
                jax.ShapeDtypeStruct((n_layers - 1, tok, dim), BF),
                jax.ShapeDtypeStruct((n_layers - 1, tok, ffn), F32),
                jax.ShapeDtypeStruct((n_layers, tok, e_dim), F32),
                jax.ShapeDtypeStruct((tok, e_dim), F32),
                jax.ShapeDtypeStruct((tok, e_dim), BF),
                jax.ShapeDtypeStruct((n_layers, range_rows, e_dim), F32),
            ],
            in_specs=[hbm, hbm, lsp(tok, e_dim), lsp(dim, e_dim), lsp(e_dim, dim),
                      pl.BlockSpec((1, dim, fb), lambda l, f: (l, 0, f)), pl.BlockSpec((1, fb, dim), lambda l, f: (l, f, 0))],
            out_specs=[hbm, hbm,
                       pl.BlockSpec((1, tok, fb), lambda l, f: (jnp.maximum(l - 1, 0), 0, jnp.where(l > 0, f, 0))),
                       lsp(tok, e_dim),
                       pl.BlockSpec((tok, e_dim), lambda l, f: (0, 0)), pl.BlockSpec((tok, e_dim), lambda l, f: (0, 0)), hbm],
            scratch_shapes=[
                pltpu.VMEM((tok, dim), BF), pltpu.VMEM((tok, dim), BF), pltpu.VMEM((tok, dim), F32), pltpu.VMEM((tok, fb), BF),
                pltpu.VMEM((z_rows, e_dim), F32), pltpu.SemaphoreType.DMA, pltpu.SemaphoreType.DMA, pltpu.SemaphoreType.DMA((z_per,)),
            ],
            compiler_params=pltpu.CompilerParams(vmem_limit_bytes=VMEM_BYTES, dimension_semantics=('arbitrary', 'arbitrary')),
            cost_estimate=pl.CostEstimate(flops=n_layers * matmul_flops, bytes_accessed=400 << 20, transcendentals=0),
            name='forward',
        )(resid_in, cot_out, fetched, w_gate, w_proj, w_up, w_down)

        sel_out = (jnp.arange(n_serve, dtype=I32)[:, None] == slot_of[None, :]).astype(F32)

        def exchange(grad_rows):
            slots = jnp.dot(sel_out, grad_rows, precision=lax.Precision.HIGHEST, preferred_element_type=F32)
            slots = jnp.broadcast_to(slots.reshape(1, n_emb, CAP, e_dim), (n_dp, n_emb, CAP, e_dim)).reshape(n_dev, CAP, e_dim)
            return lax.all_to_all(slots, MESH_AXES, 0, 0, tiled=True).reshape(n_slots, e_dim)

        def backward(layer, cot, dgp):
            def at(l, *shape):
                return pl.BlockSpec((1,) + shape, lambda f: (l, 0, 0), pipeline_mode=pl.Buffered(1))

            def flat(*shape):
                return pl.BlockSpec(shape, lambda f: (0, 0), pipeline_mode=pl.Buffered(1))

            return pl.pallas_call(
                functools.partial(backward_kernel, (n_blk, cw, nw, slab)),
                grid=(n_blk,),
                out_shape=[jax.ShapeDtypeStruct((tok, dim), BF), jax.ShapeDtypeStruct((tok, e_dim), F32), jax.ShapeDtypeStruct((tok, e_dim), BF)],
                in_specs=[flat(tok, dim), at(layer - 1, tok, dim),
                          pl.BlockSpec((1, tok, fb), lambda f: (layer - 1, 0, f)),
                          pl.BlockSpec((1, dim, fb), lambda f: (layer, 0, f)), pl.BlockSpec((1, fb, dim), lambda f: (layer, f, 0)),
                          at(layer, dim, e_dim), at(layer - 1, e_dim, dim), at(layer - 1, tok, e_dim), at(layer - 1, tok, e_dim),
                          flat(tok, e_dim)],
                out_specs=[flat(tok, dim), flat(tok, e_dim), flat(tok, e_dim)],
                scratch_shapes=[pltpu.VMEM((tok, dim), F32), pltpu.VMEM((tok, fb), BF), pltpu.VMEM((tok, dim), BF)],
                compiler_params=pltpu.CompilerParams(vmem_limit_bytes=VMEM_BYTES, dimension_semantics=('arbitrary',)),
                cost_estimate=pl.CostEstimate(flops=matmul_flops, bytes_accessed=100 << 20, transcendentals=0),
                name=f'backward_{layer}',
            )(cot, saved, ups, w_up, w_down, w_gate, w_proj, gates, fetched, dgp)

        def scatter(first_layer, rows_in, dtab):
            n = rows_in.shape[0]
            return pl.pallas_call(
                functools.partial(scatter_kernel, (first_layer, slot_bits)),
                grid=(n,),
                out_shape=jax.ShapeDtypeStruct(dtab.shape, F32),
                in_specs=[sm, sm, pl.BlockSpec((1, n_slots, e_dim), lambda i: (i, 0, 0)), hbm],
                out_specs=hbm,
                input_output_aliases={3: 0},
                scratch_shapes=[pltpu.VMEM((n_slots, e_dim), F32), pltpu.SemaphoreType.DMA],
                compiler_params=pltpu.CompilerParams(vmem_limit_bytes=VMEM_BYTES, dimension_semantics=('arbitrary',)),
                cost_estimate=pl.CostEstimate(flops=n * 20_000_000_000, bytes_accessed=n << 22, transcendentals=0),
                name=f'scatter_{first_layer}',
            )(skeys, total, rows_in, dtab)

        cot = cot_out
        for layer in reversed(range(1, n_layers)):
            got = exchange(rows)
            cot, rows, dgp = backward(layer, cot, dgp)
            dtab = scatter(layer, got[None], dtab)
        dtab = scatter(0, exchange(rows)[None], dtab)
        return out, dtab

    return jax.shard_map(device_body, mesh=mesh, in_specs=(tok_spec, act_spec, act_spec, table_spec, full_spec, full_spec, full_spec, full_spec), out_specs=(act_spec, table_spec), check_vma=False)
```

time: 3700 us -> 793 us (0.21)
  waiting for transfers between devices: 2720 us -> 18.7 us
  Pallas kernels: 0 us -> 682 us
  matrix products: 567 us -> 11.9 us
  other arithmetic: 183 us -> 10.1 us
  local copies, waits for them, and re-layouts: 130 us -> 19.4 us
  blocking collectives: 51.6 us -> 13.6 us
    psum x2 -> x0, waiting for transfers between devices: 2720 us -> none  [device_body(): grad_list[l_idx] = lax.psum(shard_grad, 'dp')]
    pallas_call x0 -> x9, Pallas kernels: none -> 682 us  [the longest x1 269 us: device_body(): pl.pallas_call(functools.partial(forward_kernel, (n_layers, n_blk, cw, nw...]
    dot_general x29 -> x5, matrix products: 567 us -> 11.9 us  [the longest x4 9.59 us: exchange(): jnp.dot(sel_out, grad_rows, precision=lax.Precision.HIGHEST, preferred_el...]
    another operation x3 -> x0, other arithmetic: 87.4 us -> none  [the longest x1 86 us: device_body(): return (resid_cur, jnp.stack(grad_list))]
    gather x13 -> x0, local copies, waits for them, and re-layouts: 78.5 us -> none  [the longest x4 45.5 us: device_body(): served = jnp.take(tables[l_idx], recv_ids, axis=0)]
    scatter-add x4 -> x0, other arithmetic: 78.2 us -> none  [device_body(): jax.ops.segment_sum(incoming, recv_ids, num_segments=range_rows)]
    all_to_all x3 -> x0, blocking collectives: 51.6 us -> none  [device_body(): incoming = lax.all_to_all(outgoing, 'emb', 0, 0, tiled=True)]
    squeeze x1 -> x0, local copies, waits for them, and re-layouts: 43.5 us -> none  [device_body(): served = jnp.take(tables[l_idx], recv_ids, axis=0)]
  transfers between devices with their start and end apart: 8 -> 5, of which waited for: 3 -> 1; matrix products, arithmetic and copies ran while one was open for 11% -> 2% of each run, Pallas kernels for 0% -> 42%
where the time goes in v1:
time: 793 us; the launch traced here: 795 us
  Pallas kernels  682 us (86%)
  starting transfers between devices  37.6 us (5%)
  local copies, waits for them, and re-layouts  19.4 us (2%)
  waiting for transfers between devices  18.7 us (2%)
  blocking collectives  13.6 us (2%)
  matrix products  11.9 us (2%)
  other arithmetic  10.1 us (1%)
    pallas_call x1, Pallas kernels, device_body(): pl.pallas_call(functools.partial(forward_kernel, (n_layers, n_blk, cw, nw...  269 us
    pallas_call x3, Pallas kernels, backward(): pl.pallas_call(functools.partial(backward_kernel, (n_blk, cw, nw, slab)),...  230 us
    pallas_call x4, Pallas kernels, scatter(): pl.pallas_call(functools.partial(scatter_kernel, (first_layer, slot_bits)...  138 us
    pallas_call x1, Pallas kernels, device_body(): pl.pallas_call(functools.partial(gather_kernel, (n_layers, n_serve, per_s...  46.1 us
    all_to_all x4, starting transfers between devices, exchange(): lax.all_to_all(slots, MESH_AXES, 0, 0, tiled=True).reshape(n_slots, e_dim)  23.4 us
    all_to_all x1, waiting for transfers between devices, device_body(): lax.all_to_all(served.reshape(n_layers, n_emb, CAP, e_dim), 'emb', 1, 1,...  18.7 us
  transfers between devices with their start and end apart: 5, of which 1 were waited for; matrix products, arithmetic and copies ran while one was open for 2% of the time, Pallas kernels for 42%

profile of v1, /device:TPU:0, one launch (start us, length us, event | category | flops | bytes accessed | tf_op | source)
XLA Modules:
  0.0 794.7 jit_solution(2550022278358930635)
XLA Ops:
  0.7 13.6 %all-gather = s32[8,1,512]{2,1,0:T(1,128)S(1)} all-gather(s32[1,1,512]{2,1,0:T(1,128)} %bitcast.64), channel_id=1, replica_groups=mesh['dp'=2,'emb'=4] {'dp','emb'}, dimensions={0}, use_global_device_ids=true | all-gather | bytes 18432 | tf_op jit(solution)/shard_map/all_gather | solution.py:266
  19.6 46.1 %table_rows.1 = bf16[4,1024,256]{2,1,0:T(8,128)(2,1)} custom-call(s32[1024]{0:T(1024)} %bitcast.65, s32[1024,1]{1,0:T(8,128)} %fusion.20.pick_ref, bf16[4,32064,256]{2,1,0:T(8,128)(2,1)} %tables_hbm.1), custom_call_target="tpu_custom_call" | custom-call | tf_op jit(solution)/shard_map/table_rows/pallas_call | solution.py:290
  65.8 3.1 copy.44
  68.9 14.2 %all-to-all-start = ((bf16[4,4,256,256]{3,2,0,1:T(8,128)(2,1)}), bf16[4,4,256,256]{3,2,0,1:T(8,128)(2,1)S(1)}, u32[]{:S(2)}, u32[]{:S(2)}) async-start(bf16[4,4,256,256]{3,2,0,1:T(8,128)(2,1)} %copy.44), calls=%async_computation | async-start | bytes 4194304 | tf_op jit(solution)/shard_map/all_to_all | solution.py:299
  83.3 5.0 sort.14
  89.9 18.7 %all-to-all-done = bf16[4,4,256,256]{3,2,0,1:T(8,128)(2,1)S(1)} async-done(((bf16[4,4,256,256]{3,2,0,1:T(8,128)(2,1)}), bf16[4,4,256,256]{3,2,0,1:T(8,128)(2,1)S(1)}, u32[]{:S(2)}, u32[]{:S(2)}) %all-to-all-start) | async-done | bytes 2097184 | tf_op jit(solution)/shard_map/all_to_all | solution.py:299
  108.6 2.5 copy.45
  111.1 3.2 reshape.155
  116.6 268.7 %forward.1 = (bf16[512,3072]{1,0:T(8,128)(2,1)}, bf16[3,512,3072]{2,1,0:T(8,128)(2,1)}, f32[3,512,8192]{2,1,0:T(8,128)}, f32[4,512,256]{2,1,0:T(8,128)}, f32[512...) custom-call(bf16[512,3072]{1,0:T(8,128)(2,1)} %x_hbm.1, bf16[512,3072]{1,0:T(8,128)(2,1)} %cot_ref.1, ...), custom_call_target="tpu_custom_call" | custom-call | flops 206158430208 | bytes 419430400 | tf_op jit(solution)/shard_map/forward/pallas_call | solution.py:315
  389.0 14.2 %all-to-all-start.4 = ((f32[8,256,256]{2,1,0:T(8,128)}), f32[8,256,256]{2,1,0:T(8,128)}, u32[]{:S(2)}, u32[]{:S(2)}) async-start(f32[8,256,256]{2,1,0:T(8,128)} %bitcast.17), calls=%async_computation.4 | async-start | bytes 4194304 | tf_op jit(solution)/shard_map/all_to_all | solution.py:347
  403.2 76.5 %backward_3.1 = (bf16[512,3072]{1,0:T(8,128)(2,1)}, f32[512,256]{1,0:T(8,128)}, bf16[512,256]{1,0:T(8,128)(2,1)}) custom-call(bf16[512,3072]{1,0:T(8,128)(2,1)} %cot_ref.1, bf16[3,512,3072]{2,1,0:T(8,128)(2,1)} %get-tuple-element.20.x_ref, f32[3,512,8192]{2,1,0:T(8,128)} %get-tuple-element.21.up_ref, bf16[4,3072,8192]{2,1,0:T(8,128)(2,1)} %wu_ref.7, ...), custom_call_target="tpu_custom_call" | custom-call | flops 51539607552 | bytes 104857600 | tf_op jit(solution)/shard_map/backward_3/pallas_call | solution.py:356
  479.7 76.4 %backward_2.1 = (bf16[512,3072]{1,0:T(8,128)(2,1)}, f32[512,256]{1,0:T(8,128)}, bf16[512,256]{1,0:T(8,128)(2,1)}) custom-call(bf16[512,3072]{1,0:T(8,128)(2,1)} %get-tuple-element.24.cot_ref, bf16[3,512,3072]{2,1,0:T(8,128)(2,1)} %get-tuple-element.20.x_ref, f32[3,512,8192]{2,1,0:T(8,128)} %get-tuple-element.21.up_ref, bf16[4,3072,8192]{2,1,0:T(8,128)(2,1)} %wu_ref.7, ...), custom_call_target="tpu_custom_call" | custom-call | flops 51539607552 | bytes 104857600 | tf_op jit(solution)/shard_map/backward_2/pallas_call | solution.py:356
  556.1 76.7 %backward_1.1 = (bf16[512,3072]{1,0:T(8,128)(2,1)}, f32[512,256]{1,0:T(8,128)}, bf16[512,256]{1,0:T(8,128)(2,1)}) custom-call(bf16[512,3072]{1,0:T(8,128)(2,1)} %get-tuple-element.26.cot_ref, bf16[3,512,3072]{2,1,0:T(8,128)(2,1)} %get-tuple-element.20.x_ref, f32[3,512,8192]{2,1,0:T(8,128)} %get-tuple-element.21.up_ref, bf16[4,3072,8192]{2,1,0:T(8,128)(2,1)} %wu_ref.7, ...), custom_call_target="tpu_custom_call" | custom-call | flops 51539607552 | bytes 104857600 | tf_op jit(solution)/shard_map/backward_1/pallas_call | solution.py:356
  632.8 3.2 fusion.4
  636.0 3.1 fusion.3
  641.8 3.1 all-to-all-start.3
  644.9 34.4 %scatter_3.1.dt_in = f32[4,32064,256]{2,1,0:T(8,128)} custom-call(s32[2056]{0:T(1024)} %concatenate.3.keys_ref, s32[1]{0:T(128)} %bitcast.6.meta_ref, f32[1,2048,256]{2,1,0:T(8,128)} %bitcast.18.rows_ref, f32[4,32064,256]{2,1,0:T(8,128)} %get-tuple-element.32.dt_in), custom_call_target="tpu_custom_call", output_to_operand_aliasing={{}: (3, {})} | custom-call | flops 20000000000 | bytes 4194304 | tf_op jit(solution)/shard_map/scatter_3/pallas_call | solution.py:374
  679.4 2.7 broadcast_in_dim.38
  682.1 3.1 all-to-all-start.2
  685.2 34.4 %scatter_2.1.dt_in = f32[4,32064,256]{2,1,0:T(8,128)} custom-call(s32[2056]{0:T(1024)} %concatenate.3.keys_ref, s32[1]{0:T(128)} %bitcast.6.meta_ref, f32[1,2048,256]{2,1,0:T(8,128)} %bitcast.15.rows_ref, f32[4,32064,256]{2,1,0:T(8,128)} %scatter_3.1.dt_in), custom_call_target="tpu_custom_call", output_to_operand_aliasing={{}: (3, {})} | custom-call | flops 20000000000 | bytes 4194304 | tf_op jit(solution)/shard_map/scatter_2/pallas_call | solution.py:374
  719.7 2.7 broadcast_in_dim.36
  722.4 3.1 all-to-all-start.1
  725.5 34.4 %scatter_1.1.dt_in = f32[4,32064,256]{2,1,0:T(8,128)} custom-call(s32[2056]{0:T(1024)} %concatenate.3.keys_ref, s32[1]{0:T(128)} %bitcast.6.meta_ref, f32[1,2048,256]{2,1,0:T(8,128)} %bitcast.12.rows_ref, f32[4,32064,256]{2,1,0:T(8,128)} %scatter_2.1.dt_in), custom_call_target="tpu_custom_call", output_to_operand_aliasing={{}: (3, {})} | custom-call | flops 20000000000 | bytes 4194304 | tf_op jit(solution)/shard_map/scatter_1/pallas_call | solution.py:374
  760.0 34.4 %scatter_0.1 = f32[4,32064,256]{2,1,0:T(8,128)} custom-call(s32[2056]{0:T(1024)} %concatenate.3.keys_ref, s32[1]{0:T(128)} %bitcast.6.meta_ref, f32[1,2048,256]{2,1,0:T(8,128)} %bitcast.9.rows_ref, f32[4,32064,256]{2,1,0:T(8,128)} %scatter_1.1.dt_in), custom_call_target="tpu_custom_call", output_to_operand_aliasing={{}: (3, {})} | custom-call | flops 20000000000 | bytes 4194304 | tf_op jit(solution)/shard_map/scatter_0/pallas_call | solution.py:374
  (49 shorter events, 15.7 us)
Async XLA Ops:
  14.3 0.6 copy-start.1
  17.9 0.6 copy-start.5
  68.9 14.3 %copy-start.6 = (s32[8,256]{1,0:T(8,128)S(1)}, s32[8,256]{1,0:T(8,128)}, u32[]{:S(2)}) copy-start(s32[8,256]{1,0:T(8,128)} %copy-done.5) | copy-start | bytes 24580
  68.9 14.3 %copy-start.9 = (s32[8]{0:T(128)S(1)}, s32[8]{0:T(128)}, u32[]{:S(2)}) copy-start(s32[8]{0:T(128)} %get-tuple-element.33) | copy-start | bytes 100
  68.9 14.4 %copy-start.8 = (pred[8,1,512]{2,0,1:T(8,128)(4,1)S(1)}, pred[8,1,512]{2,0,1:T(8,128)(4,1)}, u32[]{:S(2)}) copy-start(pred[8,1,512]{2,0,1:T(8,128)(4,1)} %get-tuple-element.35) | copy-start | bytes 12292
  68.9 20.0 %copy-start.2 = (s32[8,1,512]{2,1,0:T(1,128)S(1)}, s32[8,1,512]{2,1,0:T(1,128)}, u32[]{:S(2)}) copy-start(s32[8,1,512]{2,1,0:T(1,128)} %copy-done.1) | copy-start | bytes 49156
  68.9 20.7 %copy-start.7 = (s32[512]{0:T(512)S(1)}, s32[512]{0:T(512)}, u32[]{:S(2)}) copy-start(s32[512]{0:T(512)} %param.8) | copy-start | bytes 6148
  68.9 39.7 %all-to-all-start = ((bf16[4,4,256,256]{3,2,0,1:T(8,128)(2,1)}), bf16[4,4,256,256]{3,2,0,1:T(8,128)(2,1)S(1)}, u32[]{:S(2)}, u32[]{:S(2)}) async-start(bf16[4,4,256,256]{3,2,0,1:T(8,128)(2,1)} %copy.44), calls=%async_computation | async-start | bytes 4194304 | tf_op jit(solution)/shard_map/all_to_all | solution.py:299
  89.9 24.4 %copy-start.3 = (s32[512]{0:T(512)}, s32[512]{0:T(512)S(1)}, u32[]{:S(2)}) copy-start(s32[512]{0:T(512)S(1)} %multiply_add_fusion) | copy-start | bytes 6148
  389.0 251.2 %all-to-all-start.4 = ((f32[8,256,256]{2,1,0:T(8,128)}), f32[8,256,256]{2,1,0:T(8,128)}, u32[]{:S(2)}, u32[]{:S(2)}) async-start(f32[8,256,256]{2,1,0:T(8,128)} %bitcast.17), calls=%async_computation.4 | async-start | bytes 4194304 | tf_op jit(solution)/shard_map/all_to_all | solution.py:347
  632.8 6.3 copy-start
  632.8 6.3 copy-start.4
  641.8 37.6 %all-to-all-start.3 = ((f32[8,256,256]{2,1,0:T(8,128)}), f32[8,256,256]{2,1,0:T(8,128)}, u32[]{:S(2)}, u32[]{:S(2)}) async-start(f32[8,256,256]{2,1,0:T(8,128)} %bitcast.14), calls=%async_computation.3 | async-start | bytes 4194304 | tf_op jit(solution)/shard_map/all_to_all | solution.py:347
  682.1 37.5 %all-to-all-start.2 = ((f32[8,256,256]{2,1,0:T(8,128)}), f32[8,256,256]{2,1,0:T(8,128)}, u32[]{:S(2)}, u32[]{:S(2)}) async-start(f32[8,256,256]{2,1,0:T(8,128)} %bitcast.11), calls=%async_computation.2 | async-start | bytes 4194304 | tf_op jit(solution)/shard_map/all_to_all | solution.py:347
  722.4 37.6 %all-to-all-start.1 = ((f32[8,256,256]{2,1,0:T(8,128)}), f32[8,256,256]{2,1,0:T(8,128)}, u32[]{:S(2)}, u32[]{:S(2)}) async-start(f32[8,256,256]{2,1,0:T(8,128)} %bitcast.8), calls=%async_computation.1 | async-start | bytes 4194304 | tf_op jit(solution)/shard_map/all_to_all | solution.py:347

commit v2 on v1

v2 whole, which is shorter than its diff:
```python
import functools

import jax
import jax.numpy as jnp
from jax import lax
from jax.experimental import pallas as pl
from jax.experimental.pallas import tpu as pltpu
from jax.sharding import PartitionSpec as P

NORM_EPS = 1e-6
BF = jnp.bfloat16
F32 = jnp.float32
I32 = jnp.int32
VMEM_BYTES = 67043328
GELU_C = 0.7978845608028654
GELU_A = 0.044715

MESH_AXES = ('dp', 'emb')
CAP = 256


def gelu(x):
    return 0.5 * x * (1.0 + jnp.tanh(GELU_C * (x + GELU_A * (x * x * x))))


def gelu_slope(x):
    sq = x * x
    th = jnp.tanh(GELU_C * (x + GELU_A * (x * sq)))
    return 0.5 * (1.0 + th) + (0.5 * GELU_C) * x * (1.0 - th * th) * (1.0 + (3 * GELU_A) * sq)


def dot(a, b):
    return jnp.dot(a, b, preferred_element_type=F32)


def dot_t(a, b):
    return lax.dot_general(a, b, (((1,), (1,)), ((), ())), preferred_element_type=F32)


def row_loop(rows, slab, unroll=2):
    def run(body):
        def step(i, carry):
            body(pl.ds(pl.multiple_of(i * slab, slab), slab))
            return carry

        lax.fori_loop(0, rows // slab, step, 0, unroll=unroll)

    return run


def peer_of(n_emb, index):
    dp = index // n_emb
    return {'dp': dp, 'emb': index - dp * n_emb}


def remote(src, dst, send_sem, recv_sem, device):
    return pltpu.make_async_remote_copy(src_ref=src, dst_ref=dst, send_sem=send_sem, recv_sem=recv_sem,
                                        device_id=device, device_id_type=pl.DeviceIdType.MESH)


def meet(devices):
    barrier = pltpu.get_barrier_semaphore()
    for device in devices:
        pl.semaphore_signal(barrier, inc=1, device_id=device, device_id_type=pl.DeviceIdType.MESH)
    pl.semaphore_wait(barrier, len(devices))


def ids_kernel(cfg, in_ref, out_ref, send_sem, recv_sem):
    n_dp, n_emb = cfg
    n_dev = n_dp * n_emb
    me = lax.axis_index('dp') * n_emb + lax.axis_index('emb')
    peers = [peer_of(n_emb, lax.rem(me + k, n_dev)) for k in range(1, n_dev)]
    meet(peers)
    copies = [remote(in_ref, out_ref.at[me], send_sem.at[k], recv_sem.at[k], peer) for k, peer in enumerate(peers)]
    for copy in copies:
        copy.start()
    out_ref[me] = in_ref[...]
    for copy in copies:
        copy.wait()


def gather_kernel(cfg, loc_ref, counts_ref, pick_ref, tables_hbm, out_ref, buf, sems):
    n_layers, n_dest, cap, per_dot, group = cfg
    trip = per_dot * group
    n_trips = [(counts_ref[d] + (trip - 1)) // trip for d in range(n_dest)]

    def row_copy(d, s):
        base = pl.multiple_of(jnp.left_shift(jnp.right_shift(loc_ref[s], 3), 3), 8)
        return pltpu.make_async_copy(
            tables_hbm.at[:, pl.ds(base, 8), :], buf.at[:, pl.ds(pl.multiple_of(s * 8, 8), 8), :], sems.at[d])

    for d in range(n_dest):
        def issue(i, carry, d=d):
            for k in range(8):
                row_copy(d, d * cap + i * 8 + k).start()
            return carry

        lax.fori_loop(0, n_trips[d] * (trip // 8), issue, 0)

    for d in range(n_dest):
        def drain(i, carry, d=d):
            part = buf.at[:, pl.ds(pl.multiple_of((d * cap + i * trip) * 8, 8), trip * 8), :]
            pltpu.make_async_copy(part, part, sems.at[d]).wait()
            return carry

        lax.fori_loop(0, n_trips[d], drain, 0)

        def pick(i, carry, d=d):
            for k in range(group):
                s0 = pl.multiple_of(d * cap + i * trip + k * per_dot, per_dot)
                want = pick_ref[pl.ds(s0, per_dot), :]
                sel = (lax.broadcasted_iota(I32, (per_dot, per_dot * 8), 1) == want).astype(BF)
                for l in range(n_layers):
                    rows = buf[l, pl.ds(pl.multiple_of(s0 * 8, 8), per_dot * 8), :]
                    out_ref[l, pl.ds(s0, per_dot), :] = dot(sel, rows).astype(BF)
            return carry

        lax.fori_loop(0, n_trips[d], pick, 0)

        def blank(i, carry, d=d):
            s0 = pl.multiple_of(d * cap + i * trip, trip)
            for l in range(n_layers):
                out_ref[l, pl.ds(s0, trip), :] = jnp.zeros((trip, out_ref.shape[2]), BF)
            return carry

        lax.fori_loop(n_trips[d], cap // trip, blank, 0)


def mlp_block(cfg, u_s, h_s, acc_s, wu_ref, wd_ref, up_ref):
    cw, nw = cfg
    for c in range(wu_ref.shape[2] // cw):
        cs = slice(c * cw, (c + 1) * cw)
        up = dot(u_s[...], wu_ref[0, :, cs])
        if up_ref is not None:
            up_ref[0, :, cs] = up
        h_s[:, cs] = gelu(up).astype(BF)
    for n in range(acc_s.shape[1] // nw):
        ns = slice(n * nw, (n + 1) * nw)
        acc_s[:, ns] += dot(h_s[...], wd_ref[0, :, ns])


def norm_rows(x, sl, u_s, acc_s):
    scale = lax.rsqrt(jnp.mean(x * x, axis=-1, keepdims=True) + NORM_EPS)
    u_s[sl, :] = (x * scale).astype(BF)
    acc_s[sl, :] = x


def add_proj(nw, acc_s, mixed, wp_ref):
    for n in range(acc_s.shape[1] // nw):
        ns = slice(n * nw, (n + 1) * nw)
        acc_s[:, ns] += dot(mixed, wp_ref[0, :, ns])


def first_kernel(cfg, x_hbm, slot_ref, served_hbm, wg_ref, wp_ref, wu_ref, wd_ref,
                 x_out_ref, gate_ref, fet_ref,
                 u_s, acc_s, h_s, ret_s, in_sem, self_sem, send_sem, recv_sem):
    n_dp, n_emb, cap, cw, nw, slab = cfg
    n_blk = pl.num_programs(0)
    blk = pl.program_id(0)
    tok, dim = u_s.shape
    my_emb = lax.axis_index('emb')
    my_dp = lax.axis_index('dp')
    here = ret_s.at[:, pl.ds(pl.multiple_of(my_emb * cap, cap), cap), :]
    own = pltpu.make_async_copy(served_hbm.at[:, pl.ds(pl.multiple_of(my_emb * cap, cap), cap), :], here, self_sem)
    peers = [lax.rem(my_emb + k, n_emb) for k in range(1, n_emb)]
    copies = [remote(served_hbm.at[:, pl.ds(pl.multiple_of(p * cap, cap), cap), :], here,
                     send_sem.at[k], recv_sem.at[k], {'dp': my_dp, 'emb': p}) for k, p in enumerate(peers)]

    @pl.when(blk == 0)
    def _():
        fetch = pltpu.make_async_copy(x_hbm, x_out_ref, in_sem)
        fetch.start()
        meet([{'dp': my_dp, 'emb': p} for p in peers])
        own.start()
        for copy in copies:
            copy.start()
        fetch.wait()
        row_loop(tok, slab)(lambda sl: norm_rows(x_out_ref[sl, :].astype(F32), sl, u_s, acc_s))
        gate_ref[0] = dot(u_s[...], wg_ref[0])

    mlp_block((cw, nw), u_s, h_s, acc_s, wu_ref, wd_ref, None)

    @pl.when(blk == n_blk - 1)
    def _():
        own.wait()
        for copy in copies:
            copy.wait()
        sel = (lax.broadcasted_iota(I32, (tok, n_emb * cap), 1) == slot_ref[...]).astype(BF)
        for l in range(fet_ref.shape[0]):
            fet_ref[l] = dot(sel, ret_s[l]).astype(BF)
        add_proj(nw, acc_s, (gelu(gate_ref[0]) * fet_ref[0].astype(F32)).astype(BF), wp_ref)

        def finish(sl):
            x_out_ref[sl, :] = acc_s[sl, :].astype(BF)

        row_loop(tok, slab)(finish)


def forward_kernel(cfg, x_hbm, cot_hbm, fet_ref, wg_ref, wp_ref, wu_ref, wd_ref,
                   out_hbm, saved_hbm, up_ref, gate_ref, rows_ref, dgp_ref, dtab_hbm,
                   x_s, u_s, acc_s, h_s, zero_s, in_sem, out_sem, z_sem):
    n_layers, n_blk, cw, nw, slab, z_per, z_chunks = cfg
    layer, blk = pl.program_id(0), pl.program_id(1)
    tok, dim = x_s.shape
    step = layer * n_blk + blk
    z_rows = zero_s.shape[0]

    def z_copy(j):
        c = step * z_per + j
        zl = c // z_chunks
        zc = c - zl * z_chunks
        return pltpu.make_async_copy(zero_s, dtab_hbm.at[zl, pl.ds(pl.multiple_of(zc * z_rows, 8), z_rows), :], z_sem.at[j])

    @pl.when(step == 0)
    def _():
        fetch = pltpu.make_async_copy(x_hbm, x_s, in_sem)
        fetch.start()
        row_loop(z_rows, 8, 1)(lambda sl: zero_s.__setitem__((sl, slice(None)), jnp.zeros((8, zero_s.shape[1]), F32)))
        fetch.wait()
        row_loop(tok, slab)(lambda sl: norm_rows(x_s[sl, :].astype(F32), sl, u_s, acc_s))

    for j in range(z_per):
        @pl.when(step > 0)
        def _():
            z_copy(j).wait()

        z_copy(j).start()

    @pl.when(blk == 0)
    def _():
        gate_ref[0] = dot(u_s[...], wg_ref[0])

    mlp_block((cw, nw), u_s, h_s, acc_s, wu_ref, wd_ref, up_ref)

    @pl.when(blk == n_blk - 1)
    def _():
        add_proj(nw, acc_s, (gelu(gate_ref[0]) * fet_ref[0].astype(F32)).astype(BF), wp_ref)

        @pl.when(layer > 0)
        def _():
            pltpu.make_async_copy(x_s, saved_hbm.at[layer - 1], out_sem).wait()

        def next_rows(sl):
            x_new = acc_s[sl, :].astype(BF)
            x_s[sl, :] = x_new
            norm_rows(x_new.astype(F32), sl, u_s, acc_s)

        row_loop(tok, slab)(next_rows)

        @pl.when(layer < n_layers - 1)
        def _():
            pltpu.make_async_copy(x_s, saved_hbm.at[layer], out_sem).start()

        @pl.when(layer == n_layers - 1)
        def _():
            put = pltpu.make_async_copy(x_s, out_hbm, out_sem)
            put.start()
            get = pltpu.make_async_copy(cot_hbm, u_s, in_sem)
            get.start()
            for j in range(z_per):
                z_copy(j).wait()
            get.wait()
            d_mixed = dot_t(u_s[...], wp_ref[0]).astype(BF).astype(F32)
            gate_grads(gate_ref[0], fet_ref[0], d_mixed, rows_ref, dgp_ref)
            put.wait()


def gate_grads(gate_pre, fetched, d_mixed, rows_ref, dgp_ref):
    rows_ref[...] = gelu(gate_pre) * d_mixed
    dgp_ref[...] = (d_mixed * fetched.astype(F32) * gelu_slope(gate_pre)).astype(BF)


def to_slots(rows, slot_ref, slots_s):
    hi = rows.astype(BF)
    rest = rows - hi.astype(F32)
    mid = rest.astype(BF)
    low = (rest - mid.astype(F32)).astype(BF)
    n, tok = slots_s.shape[0], rows.shape[0]
    sel = (lax.broadcasted_iota(I32, (n, tok), 0) == slot_ref[...]).astype(BF)
    slots_s[...] = (dot(sel, hi) + dot(sel, mid)) + dot(sel, low)


def backward_kernel(cfg, cot_hbm, x1_hbm, saved_hbm, rows_in_ref, dgp_in_ref, slot_ref, gate0_ref,
                    up_ref, wu_ref, wd_ref, wg_ref, wp_ref, gate_ref, fet_ref,
                    got_hbm, slots0_hbm,
                    cot_s, x_s, acc_s, dup_s, dng_s, slots_s, rows_s, dgp_s, in_sem, x_sem, put_sem, send_sem, self_sem, recv_sem):
    n_layers, n_blk, n_dp, n_emb, cap, cw, nw, slab = cfg
    i, blk = pl.program_id(0), pl.program_id(1)
    layer = n_layers - i
    tok, dim = cot_s.shape
    fb = wu_ref.shape[2]
    n_dev = n_dp * n_emb
    me = lax.axis_index('dp') * n_emb + lax.axis_index('emb')
    peers = [peer_of(n_emb, lax.rem(me + k, n_dev)) for k in range(1, n_dev)]
    here = got_hbm.at[layer - 1, pl.ds(pl.multiple_of(me * cap, cap), cap), :]

    def part(emb):
        return slots_s.at[pl.ds(pl.multiple_of(emb * cap, cap), cap), :]

    own = pltpu.make_async_copy(part(lax.axis_index('emb')), here, self_sem)
    copies = [remote(part(peer['emb']), here, send_sem.at[k], recv_sem.at[i, k], peer) for k, peer in enumerate(peers)]

    @pl.when(blk == 0)
    def _():
        @pl.when(i == 0)
        def _():
            fetch = pltpu.make_async_copy(cot_hbm, cot_s, in_sem)
            fetch.start()
            rows_s[...] = rows_in_ref[...]
            dgp_s[...] = dgp_in_ref[...]
            meet(peers)
            fetch.wait()

        @pl.when(i < n_layers - 1)
        def _():
            pltpu.make_async_copy(saved_hbm.at[n_layers - 2 - i], x_s, x_sem).start()

        @pl.when(i == n_layers - 1)
        def _():
            pltpu.make_async_copy(x1_hbm, x_s, x_sem).start()

        to_slots(rows_s[...], slot_ref, slots_s)
        for n in range(dim // nw):
            ns = slice(n * nw, (n + 1) * nw)
            dng_s[:, ns] = dot_t(dgp_s[...], wg_ref[0, ns, :]).astype(BF)

        def clear(sl):
            acc_s[sl, :] = jnp.zeros((slab, dim), F32)

        row_loop(tok, slab)(clear)

    @pl.when(blk == 1)
    def _():
        own.start()
        for copy in copies:
            copy.start()

    for c in range(fb // cw):
        cs = slice(c * cw, (c + 1) * cw)
        d_hid = dot_t(cot_s[...], wd_ref[0, cs, :]).astype(BF).astype(F32)
        dup_s[:, cs] = (d_hid * gelu_slope(up_ref[0, :, cs])).astype(BF)
    for n in range(dim // nw):
        ns = slice(n * nw, (n + 1) * nw)
        acc_s[:, ns] += dot_t(dup_s[...], wu_ref[0, ns, :])

    @pl.when(blk == n_blk - 1)
    def _():
        pltpu.make_async_copy(x1_hbm, x_s, x_sem).wait()

        def rows_back(sl):
            x = x_s[sl, :].astype(F32)
            scale = lax.rsqrt(jnp.mean(x * x, axis=-1, keepdims=True) + NORM_EPS)
            d_n = (acc_s[sl, :].astype(BF).astype(F32) + dng_s[sl, :].astype(F32)).astype(BF).astype(F32)
            proj = jnp.mean(d_n * x, axis=-1, keepdims=True)
            d_x = d_n * scale - x * (proj * (scale * scale * scale))
            cot_s[sl, :] = (cot_s[sl, :].astype(F32) + d_x).astype(BF)

        row_loop(tok, slab)(rows_back)
        d_mixed = dot_t(cot_s[...], wp_ref[0]).astype(BF).astype(F32)
        gate = jnp.where(i < n_layers - 1, gate_ref[0], gate0_ref[0])
        gate_grads(gate, fet_ref[0], d_mixed, rows_s, dgp_s)
        own.wait()
        for copy in copies:
            copy.wait()

        @pl.when(i == n_layers - 1)
        def _():
            to_slots(rows_s[...], slot_ref, slots_s)
            puts = [pltpu.make_async_copy(slots_s, slots0_hbm.at[d], put_sem.at[d]) for d in range(n_dp)]
            for put in puts:
                put.start()
            for put in puts:
                put.wait()


def scatter_kernel(cfg, keys_ref, meta_ref, rows_ref, dt_in, dt_out, sums, sem):
    first_layer, slot_bits, unroll, bulk = cfg
    count = meta_ref[0]
    n_layers, _, e_dim = rows_ref.shape
    trips = (count + (unroll - 1)) // unroll

    def add(t, carry):
        prev, accs = carry
        for k in range(unroll):
            j = t * unroll + k
            key = keys_ref[j]
            slot = jnp.bitwise_and(key, (1 << slot_bits) - 1)
            row = jnp.right_shift(key, slot_bits)
            same = row == prev
            accs = tuple(jnp.where(same, acc, 0.0) + rows_ref[l, pl.ds(slot, 1), :] for l, acc in enumerate(accs))
            for l in range(n_layers):
                sums[l, pl.ds(j, 1), :] = accs[l]
            prev = row
        return prev, accs

    lax.fori_loop(0, trips, add, (jnp.int32(-1), tuple(jnp.zeros((1, e_dim), F32) for _ in range(n_layers))))

    def move(j, row, n):
        return pltpu.make_async_copy(sums.at[:, pl.ds(j, n), :], dt_out.at[pl.ds(first_layer, n_layers), pl.ds(row, n), :], sem)

    def put(t, carry):
        n, row = carry
        for k in range(unroll):
            j = t * unroll + k
            follow = jnp.right_shift(keys_ref[j + 1], slot_bits)
            last = jnp.logical_and(row != follow, j < count)

            @pl.when(last)
            def _(j=j, row=row):
                move(j, row, 1).start()

            n = n + last.astype(I32)
            row = follow
        return n, row

    n_rows, _ = lax.fori_loop(0, trips, put, (jnp.int32(0), jnp.right_shift(keys_ref[0], slot_bits)))

    def drain_bulk(j, carry):
        move(0, 0, bulk).wait()
        return carry

    def drain(j, carry):
        move(0, 0, 1).wait()
        return carry

    lax.fori_loop(0, n_rows // bulk, drain_bulk, 0)
    lax.fori_loop(0, lax.rem(n_rows, bulk), drain, 0)


def solution(mesh):
    n_emb, n_dp = mesh.shape['emb'], mesh.shape['dp']
    n_dev = n_emb * n_dp
    tok_spec = P(('dp', 'emb'))
    act_spec = P(('dp', 'emb'), None)
    table_spec = P(None, 'emb', None)
    full_spec = P(None, None, None)
    hbm = pl.BlockSpec(memory_space=pl.ANY)
    vm = pl.BlockSpec(memory_space=pltpu.VMEM)
    sm = pl.BlockSpec(memory_space=pltpu.SMEM)
    big = jnp.iinfo(jnp.int32).max

    def params(n_grid, **kw):
        return pltpu.CompilerParams(vmem_limit_bytes=VMEM_BYTES, dimension_semantics=('arbitrary',) * n_grid if n_grid else None, **kw)

    def device_body(tok_ids, resid_in, cot_out, tables, w_up, w_down, w_gate, w_proj):
        n_layers, range_rows, e_dim = tables.shape
        tok = tok_ids.shape[0]
        dim, ffn = w_up.shape[1:]
        n_slots, n_serve = n_dev * CAP, n_emb * CAP
        my_emb, my_dp = lax.axis_index('emb'), lax.axis_index('dp')

        lanes = 128
        ids8 = pl.pallas_call(
            functools.partial(ids_kernel, (n_dp, n_emb)),
            out_shape=jax.ShapeDtypeStruct((n_dev, tok // lanes, lanes), I32),
            in_specs=[vm], out_specs=vm,
            scratch_shapes=[pltpu.SemaphoreType.DMA((n_dev - 1,)), pltpu.SemaphoreType.DMA((n_dev - 1,))],
            compiler_params=pltpu.CompilerParams(collective_id=0, has_side_effects=True),
            name='all_ids',
        )(tok_ids.reshape(tok // lanes, lanes)).reshape(n_dev, tok)
        mine = (ids8 // range_rows) == my_emb
        t_iota = jnp.arange(tok, dtype=I32)
        before = t_iota[None, :] < t_iota[:, None]
        rank8 = jnp.sum((mine[:, None, :] & before[None]).astype(I32), axis=-1)
        c_iota = jnp.arange(CAP, dtype=I32)
        hit = mine[:, None, :] & (rank8[:, None, :] == c_iota[None, :, None])
        recv_loc = jnp.sum(jnp.where(hit, (ids8 - my_emb * range_rows)[:, None, :], 0), axis=-1)
        counts = jnp.sum(mine.astype(I32), axis=-1)
        valid = c_iota[None, :] < counts[:, None]
        slot_bits = (n_slots - 1).bit_length()
        slot_ids = jnp.arange(n_slots, dtype=I32).reshape(n_dev, CAP)
        keys = jnp.where(valid, recv_loc * (1 << slot_bits) + slot_ids, big)
        skeys = jnp.concatenate([lax.sort(keys.reshape(-1)), jnp.full((16,), big, I32)])
        total = jnp.sum(counts).reshape(1)

        my_owner = tok_ids // range_rows
        rank = jnp.sum(((my_owner[None, :] == my_owner[:, None]) & before).astype(I32), axis=-1)
        slot_of = my_owner * CAP + rank

        spread = jnp.where(valid, recv_loc, lax.rem(slot_ids * 8, range_rows))
        want = lax.dynamic_slice_in_dim(spread, my_dp * n_emb, n_emb, 0).reshape(-1)
        n_want = lax.dynamic_slice_in_dim(counts, my_dp * n_emb, n_emb, 0)
        per_dot, group = 32, 2
        pick = (jnp.bitwise_and(want, 7) + 8 * (jnp.arange(n_serve, dtype=I32) % per_dot))[:, None]
        served = pl.pallas_call(
            functools.partial(gather_kernel, (n_layers, n_emb, CAP, per_dot, group)),
            out_shape=jax.ShapeDtypeStruct((n_layers, n_serve, e_dim), BF),
            in_specs=[sm, sm, vm, hbm],
            out_specs=vm,
            scratch_shapes=[pltpu.VMEM((n_layers, n_serve * 8, e_dim), BF), pltpu.SemaphoreType.DMA((n_emb,))],
            compiler_params=params(0),
            name='table_rows',
        )(want, n_want, pick, tables)

        fb = 1024
        n_blk = ffn // fb
        cw, nw, slab = 512, 512, 16
        n_back = n_layers - 1
        z_rows = 1336
        z_chunks = range_rows // z_rows
        z_per = n_layers * z_chunks // (n_back * n_blk)
        assert z_chunks * z_rows == range_rows and z_per * n_blk * n_back == z_chunks * n_layers

        def flat(*shape):
            return pl.BlockSpec(shape, lambda *_: (0,) * len(shape), pipeline_mode=pl.Buffered(1))

        matmul_flops = 4 * tok * dim * ffn
        x1, gate0, fetched = pl.pallas_call(
            functools.partial(first_kernel, (n_dp, n_emb, CAP, cw, nw, slab)),
            grid=(n_blk,),
            out_shape=[
                jax.ShapeDtypeStruct((tok, dim), BF),
                jax.ShapeDtypeStruct((1, tok, e_dim), F32),
                jax.ShapeDtypeStruct((n_layers, tok, e_dim), BF),
            ],
            in_specs=[hbm, flat(tok, 1), hbm, flat(1, dim, e_dim), flat(1, e_dim, dim),
                      pl.BlockSpec((1, dim, fb), lambda f: (0, 0, f)), pl.BlockSpec((1, fb, dim), lambda f: (0, f, 0))],
            out_specs=[flat(tok, dim), flat(1, tok, e_dim), flat(n_layers, tok, e_dim)],
            scratch_shapes=[
                pltpu.VMEM((tok, dim), BF), pltpu.VMEM((tok, dim), F32), pltpu.VMEM((tok, fb), BF),
                pltpu.VMEM((n_layers, n_serve, e_dim), BF), pltpu.SemaphoreType.DMA, pltpu.SemaphoreType.DMA,
                pltpu.SemaphoreType.DMA((n_emb - 1,)), pltpu.SemaphoreType.DMA((n_emb - 1,)),
            ],
            compiler_params=params(1, collective_id=1, has_side_effects=True),
            cost_estimate=pl.CostEstimate(flops=matmul_flops, bytes_accessed=100 << 20, transcendentals=0),
            name='first_layer',
        )(resid_in, slot_of[:, None], served, w_gate, w_proj, w_up, w_down)

        def lsp(*shape):
            return pl.BlockSpec((1,) + shape, lambda l, f: (l + 1, 0, 0))

        out, saved, ups, gates, rows, dgp, dtab = pl.pallas_call(
            functools.partial(forward_kernel, (n_back, n_blk, cw, nw, slab, z_per, z_chunks)),
            grid=(n_back, n_blk),
            out_shape=[
                jax.ShapeDtypeStruct((tok, dim), BF),
                jax.ShapeDtypeStruct((n_back - 1, tok, dim), BF),
                jax.ShapeDtypeStruct((n_back, tok, ffn), F32),
                jax.ShapeDtypeStruct((n_back, tok, e_dim), F32),
                jax.ShapeDtypeStruct((tok, e_dim), F32),
                jax.ShapeDtypeStruct((tok, e_dim), BF),
                jax.ShapeDtypeStruct((n_layers, range_rows, e_dim), F32),
            ],
            in_specs=[hbm, hbm, lsp(tok, e_dim), lsp(dim, e_dim), lsp(e_dim, dim),
                      pl.BlockSpec((1, dim, fb), lambda l, f: (l + 1, 0, f)), pl.BlockSpec((1, fb, dim), lambda l, f: (l + 1, f, 0))],
            out_specs=[hbm, hbm,
                       pl.BlockSpec((1, tok, fb), lambda l, f: (l, 0, f)),
                       pl.BlockSpec((1, tok, e_dim), lambda l, f: (l, 0, 0)),
                       flat(tok, e_dim), flat(tok, e_dim), hbm],
            scratch_shapes=[
                pltpu.VMEM((tok, dim), BF), pltpu.VMEM((tok, dim), BF), pltpu.VMEM((tok, dim), F32), pltpu.VMEM((tok, fb), BF),
                pltpu.VMEM((z_rows, e_dim), F32), pltpu.SemaphoreType.DMA, pltpu.SemaphoreType.DMA, pltpu.SemaphoreType.DMA((z_per,)),
            ],
            compiler_params=params(2),
            cost_estimate=pl.CostEstimate(flops=n_back * matmul_flops, bytes_accessed=400 << 20, transcendentals=0),
            name='forward',
        )(x1, cot_out, fetched, w_gate, w_proj, w_up, w_down)

        def of_layer(off, *shape):
            return pl.BlockSpec((1,) + shape, lambda i, f: (jnp.maximum(n_back - i + off, 0), 0, 0))

        got, slots0 = pl.pallas_call(
            functools.partial(backward_kernel, (n_back, n_blk, n_dp, n_emb, CAP, cw, nw, slab)),
            grid=(n_back, n_blk),
            out_shape=[jax.ShapeDtypeStruct((n_back, n_slots, e_dim), F32), jax.ShapeDtypeStruct((n_dp, n_serve, e_dim), F32)],
            in_specs=[hbm, hbm, hbm, flat(tok, e_dim), flat(tok, e_dim), flat(1, tok), flat(1, tok, e_dim),
                      pl.BlockSpec((1, tok, fb), lambda i, f: (n_back - 1 - i, 0, f)),
                      pl.BlockSpec((1, dim, fb), lambda i, f: (n_back - i, 0, f)), pl.BlockSpec((1, fb, dim), lambda i, f: (n_back - i, f, 0)),
                      of_layer(0, dim, e_dim), of_layer(-1, e_dim, dim), of_layer(-2, tok, e_dim), of_layer(-1, tok, e_dim)],
            out_specs=[hbm, hbm],
            scratch_shapes=[
                pltpu.VMEM((tok, dim), BF), pltpu.VMEM((tok, dim), BF), pltpu.VMEM((tok, dim), F32), pltpu.VMEM((tok, fb), BF),
                pltpu.VMEM((tok, dim), BF), pltpu.VMEM((n_serve, e_dim), F32), pltpu.VMEM((tok, e_dim), F32), pltpu.VMEM((tok, e_dim), BF),
                pltpu.SemaphoreType.DMA, pltpu.SemaphoreType.DMA, pltpu.SemaphoreType.DMA((n_dp,)),
                pltpu.SemaphoreType.DMA((n_dev - 1,)), pltpu.SemaphoreType.DMA, pltpu.SemaphoreType.DMA((n_back, n_dev - 1)),
            ],
            compiler_params=params(2, collective_id=2, has_side_effects=True),
            cost_estimate=pl.CostEstimate(flops=n_back * matmul_flops, bytes_accessed=400 << 20, transcendentals=0),
            name='backward',
        )(cot_out, x1, saved, rows, dgp, slot_of[None, :], gate0, ups, w_up, w_down, w_gate, w_proj, gates, fetched)

        def scatter(first_layer, rows_in, dtab):
            n = rows_in.shape[0]
            return pl.pallas_call(
                functools.partial(scatter_kernel, (first_layer, slot_bits, 8, 64)),
                out_shape=jax.ShapeDtypeStruct(dtab.shape, F32),
                in_specs=[sm, sm, vm, hbm],
                out_specs=hbm,
                input_output_aliases={3: 0},
                scratch_shapes=[pltpu.VMEM((n, n_slots + 8, e_dim), F32), pltpu.SemaphoreType.DMA],
                compiler_params=params(0),
                cost_estimate=pl.CostEstimate(flops=n * 20_000_000_000, bytes_accessed=n << 22, transcendentals=0),
                name=f'scatter_{first_layer}',
            )(skeys, total, rows_in, dtab)

        got0 = lax.all_to_all(slots0.reshape(n_dev, CAP, e_dim), MESH_AXES, 0, 0, tiled=True).reshape(1, n_slots, e_dim)
        dtab = scatter(1, got, dtab)
        dtab = scatter(0, got0, dtab)
        return out, dtab

    return jax.shard_map(device_body, mesh=mesh, in_specs=(tok_spec, act_spec, act_spec, table_spec, full_spec, full_spec, full_spec, full_spec), out_specs=(act_spec, table_spec), check_vma=False)
```

time: 793 us -> 601 us (0.76)
  Pallas kernels: 682 us -> 579 us
  starting transfers between devices: 37.6 us -> 3.55 us
  waiting for transfers between devices: 18.7 us -> 0.01 us
  local copies, waits for them, and re-layouts: 19.4 us -> 3.37 us
  blocking collectives: 13.6 us -> 0 us
  matrix products: 11.9 us -> 0 us
    pallas_call x9 -> x7, Pallas kernels: 682 us -> 579 us  [the longest x1 221 us: device_body(): pl.pallas_call(functools.partial(backward_kernel, (n_back, n_blk, n_dp, n...]
    all_to_all x5 -> x1, starting transfers between devices: 37.6 us -> 3.55 us  [device_body(): lax.all_to_all(slots0.reshape(n_dev, CAP, e_dim), MESH_AXES, 0, 0, tiled=...]
    all_to_all x5 -> x1, waiting for transfers between devices: 18.7 us -> 0.01 us  [device_body(): lax.all_to_all(slots0.reshape(n_dev, CAP, e_dim), MESH_AXES, 0, 0, tiled=...]
    all_gather x1 -> x0, blocking collectives: 13.6 us -> none  [device_body(): ids8 = lax.all_gather(tok_ids, MESH_AXES, tiled=True).reshape(n_dev, tok)]
    dot_general x5 -> x0, matrix products: 11.9 us -> none  [the longest x4 9.59 us: exchange(): jnp.dot(sel_out, grad_rows, precision=lax.Precision.HIGHEST, preferred_el...]
  transfers between devices with their start and end apart: 5 -> 1, of which waited for: 1 -> 0; matrix products, arithmetic and copies ran while one was open for 2% -> 1% of each run, Pallas kernels for 42% -> 6%
where the time goes in v2:
time: 601 us; the launch traced here: 599 us
  Pallas kernels  579 us (96%)
  other arithmetic  11.7 us (2%)
    pallas_call x1, Pallas kernels, device_body(): pl.pallas_call(functools.partial(backward_kernel, (n_back, n_blk, n_dp, n...  221 us
    pallas_call x1, Pallas kernels, device_body(): pl.pallas_call(functools.partial(forward_kernel, (n_back, n_blk, cw, nw,...  207 us
    pallas_call x1, Pallas kernels, device_body(): pl.pallas_call(functools.partial(first_kernel, (n_dp, n_emb, CAP, cw, nw,...  75.4 us
    pallas_call x2, Pallas kernels, scatter(): pl.pallas_call(functools.partial(scatter_kernel, (first_layer, slot_bits,...  57.3 us
  transfers between devices with their start and end apart: 1, of which 0 were waited for; matrix products, arithmetic and copies ran while one was open for 1% of the time, Pallas kernels for 6%

profile of v2, /device:TPU:0, one launch (start us, length us, event | category | flops | bytes accessed | tf_op | source)
XLA Modules:
  0.0 599.1 jit_solution(8606970416346763279)
XLA Ops:
  0.7 0.7 add_select_fusion.3
  1.4 0.2 convert_reduce_fusion.1
  1.7 0.7 multiply_add_fusion.1
  2.4 7.9 %all_ids.1 = s32[8,4,128]{2,1,0:T(4,128)} custom-call(s32[4,128]{1,0:T(4,128)} %bitcast.33), custom_call_target="tpu_custom_call" | custom-call | tf_op jit(solution)/shard_map/all_ids/pallas_call | solution.py:453
  10.3 0.8 fusion.6
  11.0 0.8 convert_reduce_fusion.2
  11.9 0.5 copy-done.3
  12.4 0.6 dynamic_slice.7.counts_ref
  12.9 0.7 fusion.12
  13.7 0.9 copy.18.slot_ref
  14.5 0.7 convert_reduce_fusion
  15.3 0.9 select_reduce_fusion
  16.3 0.6 copy.23
  16.9 0.2 copy.25
  17.1 0.9 fusion.2.pick_ref
  18.0 10.6 %table_rows.1.served_hbm = bf16[4,1024,256]{2,1,0:T(8,128)(2,1)} custom-call(s32[1024]{0:T(1024)} %bitcast.36, s32[4]{0:T(128)} %dynamic_slice.7.counts_ref, s32[1024,1]{1,0:T(8,128)} %fusion.2.pick_ref, bf16[4,32064,256]{2,1,0:T(8,128)(2,1)} %tables_hbm.1), custom_call_target="tpu_custom_call" | custom-call | tf_op jit(solution)/shard_map/table_rows/pallas_call | solution.py:485
  28.6 75.4 %first_layer.1 = (bf16[512,3072]{1,0:T(8,128)(2,1)}, f32[1,512,256]{2,1,0:T(8,128)}, bf16[4,512,256]{2,1,0:T(8,128)(2,1)}) custom-call(bf16[512,3072]{1,0:T(8,128)(2,1)} %x_hbm.1, s32[512,1]{1,0:T(8,128)} %copy.18.slot_ref, bf16[4,1024,256]{2,1,0:T(8,128)(2,1)} %table_rows.1.served_hbm, bf16[4,3072,256]{2,1,0:T(8,128)(2,1)} %wg_ref.5, ...), custom_call_target="tpu_custom_call" | custom-call | flops 51539607552 | bytes 104857600 | tf_op jit(solution)/shard_map/first_layer/pallas_call | solution.py:508
  104.0 207.0 %forward.1 = (bf16[512,3072]{1,0:T(8,128)(2,1)}, bf16[2,512,3072]{2,1,0:T(8,128)(2,1)}, f32[3,512,8192]{2,1,0:T(8,128)}, f32[3,512,256]{2,1,0:T(8,128)}, f32[512...) custom-call(bf16[512,3072]{1,0:T(8,128)(2,1)} %get-tuple-element.16.x_hbm.x1_hbm, ...), custom_call_target="tpu_custom_call" | custom-call | flops 154618822656 | bytes 419430400 | tf_op jit(solution)/shard_map/forward/pallas_call | solution.py:532
  311.0 221.2 %backward.1 = (f32[3,2048,256]{2,1,0:T(8,128)}, f32[2,1024,256]{2,1,0:T(8,128)}) custom-call(bf16[512,3072]{1,0:T(8,128)(2,1)} %cot_hbm.3, bf16[512,3072]{1,0:T(8,128)(2,1)} %get-tuple-element.16.x_hbm.x1_hbm, bf16[2,512,3072]{2,1,0:T(8,128)(2,1)} %get-tuple-element.20.saved_hbm, f32[512,256]{1,0:T(8,128)} %get-tuple-element.21.rows_in_ref, ...), custom_call_target="tpu_custom_call" | custom-call | flops 154618822656 | bytes 419430400 | tf_op jit(solution)/shard_map/backward/pallas_call | solution.py:562
  532.3 3.6 all-to-all-start
  536.0 5.0 sort.14
  541.0 0.6 concatenate.3.keys_ref
  541.6 35.2 %scatter_1.1.dt_in = f32[4,32064,256]{2,1,0:T(8,128)} custom-call(s32[2064]{0:T(1024)} %concatenate.3.keys_ref, s32[1]{0:T(128)} %bitcast.2.meta_ref, f32[3,2048,256]{2,1,0:T(8,128)} %get-tuple-element.27.rows_ref, f32[4,32064,256]{2,1,0:T(8,128)} %get-tuple-element.28.dt_in), custom_call_target="tpu_custom_call", output_to_operand_aliasing={{}: (3, {})} | custom-call | flops 60000002048 | bytes 12582912 | tf_op jit(solution)/shard_map/scatter_1/pallas_call | solution.py:584
  576.8 22.1 %scatter_0.1 = f32[4,32064,256]{2,1,0:T(8,128)} custom-call(s32[2064]{0:T(1024)} %concatenate.3.keys_ref, s32[1]{0:T(128)} %bitcast.2.meta_ref, f32[1,2048,256]{2,1,0:T(8,128)} %bitcast.5.rows_ref, f32[4,32064,256]{2,1,0:T(8,128)} %scatter_1.1.dt_in), custom_call_target="tpu_custom_call", output_to_operand_aliasing={{}: (3, {})} | custom-call | flops 20000000000 | bytes 4194304 | tf_op jit(solution)/shard_map/scatter_0/pallas_call | solution.py:584
  (20 shorter events, 0.3 us)
Async XLA Ops:
  2.4 12.9 %copy-start.2 = (s32[512]{0:T(512)}, s32[512]{0:T(512)S(1)}, u32[]{:S(2)}) copy-start(s32[512]{0:T(512)S(1)} %multiply_add_fusion.1) | copy-start | bytes 6148
  11.8 0.6 copy-start.3
  16.2 0.6 copy-start
  532.3 3.6 copy-start.1
  532.3 3.6 copy-start.4
  532.3 44.5 %all-to-all-start = ((f32[8,256,256]{2,1,0:T(8,128)}), f32[8,256,256]{2,1,0:T(8,128)}, u32[]{:S(2)}, u32[]{:S(2)}) async-start(f32[8,256,256]{2,1,0:T(8,128)} %bitcast.30), calls=%async_computation | async-start | bytes 4194304 | tf_op jit(solution)/shard_map/all_to_all | solution.py:596

commit v3 on v2

--- a/solution.py
+++ b/solution.py
@@ -128,15 +128,27 @@
 
 def mlp_block(cfg, u_s, h_s, acc_s, wu_ref, wd_ref, up_ref):
     cw, nw = cfg
-    for c in range(wu_ref.shape[2] // cw):
+    gw = 128
+    fb = wu_ref.shape[2]
+
+    def act(c):
+        for g in range(cw // gw):
+            gs = slice(c * cw + g * gw, c * cw + (g + 1) * gw)
+            h_s[:, gs] = gelu(up_ref[0, :, gs]).astype(BF)
+
+    n_c = fb // cw
+    for c in range(n_c):
         cs = slice(c * cw, (c + 1) * cw)
-        up = dot(u_s[...], wu_ref[0, :, cs])
-        if up_ref is not None:
-            up_ref[0, :, cs] = up
-        h_s[:, cs] = gelu(up).astype(BF)
-    for n in range(acc_s.shape[1] // nw):
-        ns = slice(n * nw, (n + 1) * nw)
-        acc_s[:, ns] += dot(h_s[...], wd_ref[0, :, ns])
+        up_ref[0, :, cs] = dot(u_s[...], wu_ref[0, :, cs])
+        if c > 0:
+            act(c - 1)
+    for c in range(n_c):
+        cs = slice(c * cw, (c + 1) * cw)
+        for n in range(acc_s.shape[1] // nw):
+            ns = slice(n * nw, (n + 1) * nw)
+            acc_s[:, ns] += dot(h_s[:, cs], wd_ref[0, cs, ns])
+        if c == 0:
+            act(n_c - 1)
 
 
 def norm_rows(x, sl, u_s, acc_s):
@@ -153,7 +165,7 @@
 
 def first_kernel(cfg, x_hbm, slot_ref, served_hbm, wg_ref, wp_ref, wu_ref, wd_ref,
                  x_out_ref, gate_ref, fet_ref,
-                 u_s, acc_s, h_s, ret_s, in_sem, self_sem, send_sem, recv_sem):
+                 u_s, acc_s, h_s, up_s, ret_s, in_sem, self_sem, send_sem, recv_sem):
     n_dp, n_emb, cap, cw, nw, slab = cfg
     n_blk = pl.num_programs(0)
     blk = pl.program_id(0)
@@ -178,7 +190,7 @@
         row_loop(tok, slab)(lambda sl: norm_rows(x_out_ref[sl, :].astype(F32), sl, u_s, acc_s))
         gate_ref[0] = dot(u_s[...], wg_ref[0])
 
-    mlp_block((cw, nw), u_s, h_s, acc_s, wu_ref, wd_ref, None)
+    mlp_block((cw, nw), u_s, h_s, acc_s, wu_ref, wd_ref, up_s)
 
     @pl.when(blk == n_blk - 1)
     def _():
@@ -275,15 +287,18 @@
     rest = rows - hi.astype(F32)
     mid = rest.astype(BF)
     low = (rest - mid.astype(F32)).astype(BF)
-    n, tok = slots_s.shape[0], rows.shape[0]
-    sel = (lax.broadcasted_iota(I32, (n, tok), 0) == slot_ref[...]).astype(BF)
+    sel = slot_pick(slots_s.shape[0], slot_ref)
     slots_s[...] = (dot(sel, hi) + dot(sel, mid)) + dot(sel, low)
+
+
+def slot_pick(n, slot_ref):
+    return (lax.broadcasted_iota(I32, (n, slot_ref.shape[1]), 0) == slot_ref[...]).astype(BF)
 
 
 def backward_kernel(cfg, cot_hbm, x1_hbm, saved_hbm, rows_in_ref, dgp_in_ref, slot_ref, gate0_ref,
                     up_ref, wu_ref, wd_ref, wg_ref, wp_ref, gate_ref, fet_ref,
-                    got_hbm, slots0_hbm,
-                    cot_s, x_s, acc_s, dup_s, dng_s, slots_s, rows_s, dgp_s, in_sem, x_sem, put_sem, send_sem, self_sem, recv_sem):
+                    got_hbm, gate_hbm, slots0_ref,
+                    cot_s, x_s, acc_s, dup_s, dh_s, dng_s, slots_s, gslots_s, rows_s, dgp_s, in_sem, x_sem, send_sem, self_sem, recv_sem):
     n_layers, n_blk, n_dp, n_emb, cap, cw, nw, slab = cfg
     i, blk = pl.program_id(0), pl.program_id(1)
     layer = n_layers - i
@@ -294,11 +309,16 @@
     peers = [peer_of(n_emb, lax.rem(me + k, n_dev)) for k in range(1, n_dev)]
     here = got_hbm.at[layer - 1, pl.ds(pl.multiple_of(me * cap, cap), cap), :]
 
-    def part(emb):
-        return slots_s.at[pl.ds(pl.multiple_of(emb * cap, cap), cap), :]
-
-    own = pltpu.make_async_copy(part(lax.axis_index('emb')), here, self_sem)
-    copies = [remote(part(peer['emb']), here, send_sem.at[k], recv_sem.at[i, k], peer) for k, peer in enumerate(peers)]
+    g_here = gate_hbm.at[pl.ds(pl.multiple_of(me * cap, cap), cap), :]
+
+    def part(ref, emb):
+        return ref.at[pl.ds(pl.multiple_of(emb * cap, cap), cap), :]
+
+    own = pltpu.make_async_copy(part(slots_s, lax.axis_index('emb')), here, self_sem.at[0])
+    copies = [remote(part(slots_s, peer['emb']), here, send_sem.at[0, k], recv_sem.at[i, k], peer) for k, peer in enumerate(peers)]
+    g_own = pltpu.make_async_copy(part(gslots_s, lax.axis_index('emb')), g_here, self_sem.at[1])
+    g_copies = [remote(part(gslots_s, peer['emb']), g_here, send_sem.at[1, k], recv_sem.at[n_layers, k], peer)
+                for k, peer in enumerate(peers)]
 
     @pl.when(blk == 0)
     def _():
@@ -335,13 +355,35 @@
         for copy in copies:
             copy.start()
 
+    @pl.when((blk == 2) & (i == 0))
+    def _():
+        to_slots(gelu(gate0_ref[0]), slot_ref, gslots_s)
+
+    @pl.when((blk == 3) & (i == 0))
+    def _():
+        g_own.start()
+        for copy in g_copies:
+            copy.start()
+
+    gw = 128
+
+    def act(c):
+        for g in range(cw // gw):
+            gs = slice(c * cw + g * gw, c * cw + (g + 1) * gw)
+            dup_s[:, gs] = (dh_s[:, gs].astype(F32) * gelu_slope(up_ref[0, :, gs])).astype(BF)
+
     for c in range(fb // cw):
         cs = slice(c * cw, (c + 1) * cw)
-        d_hid = dot_t(cot_s[...], wd_ref[0, cs, :]).astype(BF).astype(F32)
-        dup_s[:, cs] = (d_hid * gelu_slope(up_ref[0, :, cs])).astype(BF)
-    for n in range(dim // nw):
-        ns = slice(n * nw, (n + 1) * nw)
-        acc_s[:, ns] += dot_t(dup_s[...], wu_ref[0, ns, :])
+        dh_s[:, cs] = dot_t(cot_s[...], wd_ref[0, cs, :]).astype(BF)
+        if c > 0:
+            act(c - 1)
+    for c in range(fb // cw):
+        cs = slice(c * cw, (c + 1) * cw)
+        for n in range(dim // nw):
+            ns = slice(n * nw, (n + 1) * nw)
+            acc_s[:, ns] += dot_t(dup_s[:, cs], wu_ref[0, ns, cs])
+        if c == 0:
+            act(fb // cw - 1)
 
     @pl.when(blk == n_blk - 1)
     def _():
@@ -356,75 +398,110 @@
             cot_s[sl, :] = (cot_s[sl, :].astype(F32) + d_x).astype(BF)
 
         row_loop(tok, slab)(rows_back)
-        d_mixed = dot_t(cot_s[...], wp_ref[0]).astype(BF).astype(F32)
-        gate = jnp.where(i < n_layers - 1, gate_ref[0], gate0_ref[0])
-        gate_grads(gate, fet_ref[0], d_mixed, rows_s, dgp_s)
+        d_mixed = dot_t(cot_s[...], wp_ref[0]).astype(BF)
         own.wait()
         for copy in copies:
             copy.wait()
 
+        @pl.when(i == 0)
+        def _():
+            g_own.wait()
+            for copy in g_copies:
+                copy.wait()
+
+        @pl.when(i < n_layers - 1)
+        def _():
+            gate_grads(gate_ref[0], fet_ref[0], d_mixed.astype(F32), rows_s, dgp_s)
+
         @pl.when(i == n_layers - 1)
         def _():
-            to_slots(rows_s[...], slot_ref, slots_s)
-            puts = [pltpu.make_async_copy(slots_s, slots0_hbm.at[d], put_sem.at[d]) for d in range(n_dp)]
-            for put in puts:
-                put.start()
-            for put in puts:
-                put.wait()
-
-
-def scatter_kernel(cfg, keys_ref, meta_ref, rows_ref, dt_in, dt_out, sums, sem):
-    first_layer, slot_bits, unroll, bulk = cfg
+            slots = dot(slot_pick(slots_s.shape[0], slot_ref), d_mixed).astype(BF)
+            for d in range(n_dp):
+                slots0_ref[d] = slots
+
+
+def scatter_kernel(cfg, keys_ref, meta_ref, *refs):
+    first_layer, n_layers, slot_bits, unroll, window, bulk = cfg
+    if first_layer == 0:
+        gate_ref, mixed_ref, dt_in, dt_out, groups, spots, prod, sems = refs
+        n_rows = mixed_ref.shape[0]
+
+        def product(sl):
+            prod[0, sl, :] = gate_ref[sl, :] * mixed_ref[sl, :].astype(F32)
+
+        row_loop(n_rows, 64, 4)(product)
+        rows_ref = prod
+    else:
+        rows_ref, dt_in, dt_out, groups, spots, sems = refs
     count = meta_ref[0]
-    n_layers, _, e_dim = rows_ref.shape
-    trips = (count + (unroll - 1)) // unroll
-
-    def add(t, carry):
-        prev, accs = carry
-        for k in range(unroll):
-            j = t * unroll + k
-            key = keys_ref[j]
-            slot = jnp.bitwise_and(key, (1 << slot_bits) - 1)
-            row = jnp.right_shift(key, slot_bits)
-            same = row == prev
-            accs = tuple(jnp.where(same, acc, 0.0) + rows_ref[l, pl.ds(slot, 1), :] for l, acc in enumerate(accs))
-            for l in range(n_layers):
-                sums[l, pl.ds(j, 1), :] = accs[l]
-            prev = row
-        return prev, accs
-
-    lax.fori_loop(0, trips, add, (jnp.int32(-1), tuple(jnp.zeros((1, e_dim), F32) for _ in range(n_layers))))
-
-    def move(j, row, n):
-        return pltpu.make_async_copy(sums.at[:, pl.ds(j, n), :], dt_out.at[pl.ds(first_layer, n_layers), pl.ds(row, n), :], sem)
-
-    def put(t, carry):
-        n, row = carry
-        for k in range(unroll):
-            j = t * unroll + k
-            follow = jnp.right_shift(keys_ref[j + 1], slot_bits)
-            last = jnp.logical_and(row != follow, j < count)
-
-            @pl.when(last)
-            def _(j=j, row=row):
-                move(j, row, 1).start()
-
-            n = n + last.astype(I32)
-            row = follow
-        return n, row
-
-    n_rows, _ = lax.fori_loop(0, trips, put, (jnp.int32(0), jnp.right_shift(keys_ref[0], slot_bits)))
-
-    def drain_bulk(j, carry):
-        move(0, 0, bulk).wait()
-        return carry
-
-    def drain(j, carry):
-        move(0, 0, 1).wait()
-        return carry
-
-    lax.fori_loop(0, n_rows // bulk, drain_bulk, 0)
-    lax.fori_loop(0, lax.rem(n_rows, bulk), drain, 0)
+    e_dim = rows_ref.shape[2]
+    sub = 8
+    n_win = (count + (window - 1)) // window
+    lane_row = lax.broadcasted_iota(I32, (sub, e_dim), 0)
+    mask = (1 << slot_bits) - 1
+
+    def move(buf, spot, group, n):
+        return pltpu.make_async_copy(groups.at[buf, :, pl.ds(spot, n)],
+                                     dt_out.at[pl.ds(first_layer, n_layers), pl.ds(group, n)], sems.at[buf])
+
+    def settle(buf, n):
+        def drain_bulk(j, carry):
+            move(buf, 0, 0, bulk).wait()
+            return carry
+
+        def drain(j, carry):
+            move(buf, 0, 0, 1).wait()
+            return carry
+
+        lax.fori_loop(0, n // bulk, drain_bulk, 0)
+        lax.fori_loop(0, lax.rem(n, bulk), drain, 0)
+
+    def run_window(w, carry):
+        buf = lax.rem(w, 2)
+        prev, accs, older, old = carry
+        settle(buf, older)
+        stop = jnp.minimum(count, (w + 1) * window)
+        trips = (stop - w * window + (unroll - 1)) // unroll
+
+        def add(t, carry):
+            prev, n, accs = carry
+            for k in range(unroll):
+                key = keys_ref[w * window + t * unroll + k]
+                slot = jnp.bitwise_and(key, mask)
+                row = jnp.right_shift(key, slot_bits)
+                group = jnp.right_shift(row, 3)
+                same = group == prev
+                n = n + jnp.where(same, 0, 1)
+                spots[jnp.maximum(n, 0)] = group
+                here = lane_row == jnp.bitwise_and(row, sub - 1)
+                new = []
+                for l, acc in enumerate(accs):
+                    row_l = jnp.broadcast_to(rows_ref[l, pl.ds(slot, 1), :], (sub, e_dim))
+                    new.append(jnp.where(same, acc, 0.0) + jnp.where(here, row_l, 0.0))
+                    groups[buf, l, jnp.maximum(n, 0)] = new[l]
+                accs = tuple(new)
+                prev = group
+            return prev, n, accs
+
+        n0 = jnp.where(jnp.right_shift(keys_ref[w * window], slot_bits + 3) == prev, 0, -1)
+        prev, n, accs = lax.fori_loop(0, trips, add, (prev, n0, accs))
+        follow = jnp.right_shift(keys_ref[(w + 1) * window], slot_bits + 3)
+        padded = trips * unroll > stop - w * window
+        goes_on = jnp.logical_and(stop < count, follow == prev)
+        n_groups = n + 1 - jnp.where(jnp.logical_or(padded, goes_on), 1, 0)
+
+        def put(u, carry):
+            move(buf, u, spots[u], 1).start()
+            return carry
+
+        lax.fori_loop(0, n_groups, put, 0)
+        return prev, accs, old, n_groups
+
+    zero = jnp.int32(0)
+    accs = tuple(jnp.zeros((sub, e_dim), F32) for _ in range(n_layers))
+    _, _, older, old = lax.fori_loop(0, n_win, run_window, (jnp.int32(-1), accs, zero, zero))
+    settle(lax.rem(n_win, 2), older)
+    settle(lax.rem(n_win + 1, 2), old)
 
 
 def solution(mesh):
@@ -470,7 +547,7 @@
         slot_bits = (n_slots - 1).bit_length()
         slot_ids = jnp.arange(n_slots, dtype=I32).reshape(n_dev, CAP)
         keys = jnp.where(valid, recv_loc * (1 << slot_bits) + slot_ids, big)
-        skeys = jnp.concatenate([lax.sort(keys.reshape(-1)), jnp.full((16,), big, I32)])
+        skeys = jnp.concatenate([lax.sort(keys.reshape(-1)), jnp.full((128,), big, I32)])
         total = jnp.sum(counts).reshape(1)
 
         my_owner = tok_ids // range_rows
@@ -517,7 +594,7 @@
                       pl.BlockSpec((1, dim, fb), lambda f: (0, 0, f)), pl.BlockSpec((1, fb, dim), lambda f: (0, f, 0))],
             out_specs=[flat(tok, dim), flat(1, tok, e_dim), flat(n_layers, tok, e_dim)],
             scratch_shapes=[
-                pltpu.VMEM((tok, dim), BF), pltpu.VMEM((tok, dim), F32), pltpu.VMEM((tok, fb), BF),
+                pltpu.VMEM((tok, dim), BF), pltpu.VMEM((tok, dim), F32), pltpu.VMEM((tok, fb), BF), pltpu.VMEM((1, tok, fb), F32),
                 pltpu.VMEM((n_layers, n_serve, e_dim), BF), pltpu.SemaphoreType.DMA, pltpu.SemaphoreType.DMA,
                 pltpu.SemaphoreType.DMA((n_emb - 1,)), pltpu.SemaphoreType.DMA((n_emb - 1,)),
             ],
@@ -559,43 +636,51 @@
         def of_layer(off, *shape):
             return pl.BlockSpec((1,) + shape, lambda i, f: (jnp.maximum(n_back - i + off, 0), 0, 0))
 
-        got, slots0 = pl.pallas_call(
+        got, got_gate, slots0 = pl.pallas_call(
             functools.partial(backward_kernel, (n_back, n_blk, n_dp, n_emb, CAP, cw, nw, slab)),
             grid=(n_back, n_blk),
-            out_shape=[jax.ShapeDtypeStruct((n_back, n_slots, e_dim), F32), jax.ShapeDtypeStruct((n_dp, n_serve, e_dim), F32)],
+            out_shape=[jax.ShapeDtypeStruct((n_back, n_slots, e_dim), F32), jax.ShapeDtypeStruct((n_slots, e_dim), F32),
+                       jax.ShapeDtypeStruct((n_dp, n_serve, e_dim), BF)],
             in_specs=[hbm, hbm, hbm, flat(tok, e_dim), flat(tok, e_dim), flat(1, tok), flat(1, tok, e_dim),
                       pl.BlockSpec((1, tok, fb), lambda i, f: (n_back - 1 - i, 0, f)),
                       pl.BlockSpec((1, dim, fb), lambda i, f: (n_back - i, 0, f)), pl.BlockSpec((1, fb, dim), lambda i, f: (n_back - i, f, 0)),
                       of_layer(0, dim, e_dim), of_layer(-1, e_dim, dim), of_layer(-2, tok, e_dim), of_layer(-1, tok, e_dim)],
-            out_specs=[hbm, hbm],
+            out_specs=[hbm, hbm, flat(n_dp, n_serve, e_dim)],
             scratch_shapes=[
-                pltpu.VMEM((tok, dim), BF), pltpu.VMEM((tok, dim), BF), pltpu.VMEM((tok, dim), F32), pltpu.VMEM((tok, fb), BF),
-                pltpu.VMEM((tok, dim), BF), pltpu.VMEM((n_serve, e_dim), F32), pltpu.VMEM((tok, e_dim), F32), pltpu.VMEM((tok, e_dim), BF),
-                pltpu.SemaphoreType.DMA, pltpu.SemaphoreType.DMA, pltpu.SemaphoreType.DMA((n_dp,)),
-                pltpu.SemaphoreType.DMA((n_dev - 1,)), pltpu.SemaphoreType.DMA, pltpu.SemaphoreType.DMA((n_back, n_dev - 1)),
+                pltpu.VMEM((tok, dim), BF), pltpu.VMEM((tok, dim), BF), pltpu.VMEM((tok, dim), F32), pltpu.VMEM((tok, fb), BF), pltpu.VMEM((tok, fb), BF),
+                pltpu.VMEM((tok, dim), BF), pltpu.VMEM((n_serve, e_dim), F32), pltpu.VMEM((n_serve, e_dim), F32),
+                pltpu.VMEM((tok, e_dim), F32), pltpu.VMEM((tok, e_dim), BF),
+                pltpu.SemaphoreType.DMA, pltpu.SemaphoreType.DMA,
+                pltpu.SemaphoreType.DMA((2, n_dev - 1)), pltpu.SemaphoreType.DMA((2,)), pltpu.SemaphoreType.DMA((n_back + 1, n_dev - 1)),
             ],
             compiler_params=params(2, collective_id=2, has_side_effects=True),
             cost_estimate=pl.CostEstimate(flops=n_back * matmul_flops, bytes_accessed=400 << 20, transcendentals=0),
             name='backward',
         )(cot_out, x1, saved, rows, dgp, slot_of[None, :], gate0, ups, w_up, w_down, w_gate, w_proj, gates, fetched)
 
-        def scatter(first_layer, rows_in, dtab):
-            n = rows_in.shape[0]
+        window, sub = 512, 8
+
+        def scatter(first_layer, n, rows_in, dtab):
+            scratch = [pltpu.VMEM((2, n, window, sub, e_dim), F32), pltpu.SMEM((window,), I32)]
+            if first_layer == 0:
+                scratch.append(pltpu.VMEM((1, n_slots, e_dim), F32))
             return pl.pallas_call(
-                functools.partial(scatter_kernel, (first_layer, slot_bits, 8, 64)),
+                functools.partial(scatter_kernel, (first_layer, n, slot_bits, 8, window, 32)),
                 out_shape=jax.ShapeDtypeStruct(dtab.shape, F32),
-                in_specs=[sm, sm, vm, hbm],
+                in_specs=[sm, sm] + [vm] * len(rows_in) + [hbm],
                 out_specs=hbm,
-                input_output_aliases={3: 0},
-                scratch_shapes=[pltpu.VMEM((n, n_slots + 8, e_dim), F32), pltpu.SemaphoreType.DMA],
+                input_output_aliases={2 + len(rows_in): 0},
+                scratch_shapes=scratch + [pltpu.SemaphoreType.DMA((2,))],
                 compiler_params=params(0),
                 cost_estimate=pl.CostEstimate(flops=n * 20_000_000_000, bytes_accessed=n << 22, transcendentals=0),
                 name=f'scatter_{first_layer}',
-            )(skeys, total, rows_in, dtab)
-
-        got0 = lax.all_to_all(slots0.reshape(n_dev, CAP, e_dim), MESH_AXES, 0, 0, tiled=True).reshape(1, n_slots, e_dim)
-        dtab = scatter(1, got, dtab)
-        dtab = scatter(0, got0, dtab)
+            )(skeys, total, *rows_in, dtab)
+
+        mixed0 = lax.all_to_all(slots0.reshape(n_dev, CAP, e_dim), MESH_AXES, 0, 0, tiled=True).reshape(n_slots, e_dim)
+        dtab = dtab.reshape(n_layers, range_rows // sub, sub, e_dim)
+        dtab = scatter(1, n_back, (got,), dtab)
+        dtab = scatter(0, 1, (got_gate, mixed0), dtab)
+        dtab = dtab.reshape(n_layers, range_rows, e_dim)
         return out, dtab
 
     return jax.shard_map(device_body, mesh=mesh, in_specs=(tok_spec, act_spec, act_spec, table_spec, full_spec, full_spec, full_spec, full_spec), out_specs=(act_spec, table_spec), check_vma=False)

time: 601 us -> 574 us (0.955)
  Pallas kernels: 579 us -> 557 us
    pallas_call x2, Pallas kernels: 57.3 us -> 44.9 us  [scatter(): pl.pallas_call(functools.partial(scatter_kernel, (first_layer, n, slot_bi...]
    pallas_call x1, Pallas kernels: 221 us -> 211 us  [device_body(): pl.pallas_call(functools.partial(backward_kernel, (n_back, n_blk, n_dp, n...]
  transfers between devices with their start and end apart: 1 -> 1, of which waited for: 0 -> 0; matrix products, arithmetic and copies ran while one was open for 1% -> 1% of each run, Pallas kernels for 6% -> 4%
where the time goes in v3:
time: 574 us; the launch traced here: 576 us
  Pallas kernels  557 us (97%)
  other arithmetic  12.5 us (2%)
    pallas_call x1, Pallas kernels, device_body(): pl.pallas_call(functools.partial(backward_kernel, (n_back, n_blk, n_dp, n...  211 us
    pallas_call x1, Pallas kernels, device_body(): pl.pallas_call(functools.partial(forward_kernel, (n_back, n_blk, cw, nw,...  202 us
    pallas_call x1, Pallas kernels, device_body(): pl.pallas_call(functools.partial(first_kernel, (n_dp, n_emb, CAP, cw, nw,...  75.8 us
    pallas_call x2, Pallas kernels, scatter(): pl.pallas_call(functools.partial(scatter_kernel, (first_layer, n, slot_bi...  44.9 us
    pallas_call x1, Pallas kernels, device_body(): pl.pallas_call(functools.partial(gather_kernel, (n_layers, n_emb, CAP, pe...  15.3 us
  transfers between devices with their start and end apart: 1, of which 0 were waited for; matrix products, arithmetic and copies ran while one was open for 1% of the time, Pallas kernels for 4%

profile of v3, /device:TPU:0, one launch (start us, length us, event | category | flops | bytes accessed | tf_op | source)
XLA Modules:
  0.0 576.0 jit_solution(11993904625905907118)
XLA Ops:
  0.7 0.7 add_select_fusion.3
  1.4 0.2 convert_reduce_fusion.1
  1.7 0.7 multiply_add_fusion.1
  2.4 0.9 copy.18.slot_ref
  3.2 7.9 %all_ids.1 = s32[8,4,128]{2,1,0:T(4,128)} custom-call(s32[4,128]{1,0:T(4,128)} %bitcast.35), custom_call_target="tpu_custom_call" | custom-call | tf_op jit(solution)/shard_map/all_ids/pallas_call | solution.py:530
  11.1 0.8 fusion.6
  11.9 0.7 fusion.12
  12.6 0.9 convert_reduce_fusion.2
  13.6 0.6 dynamic_slice.7.counts_ref
  14.2 0.7 convert_reduce_fusion
  14.9 0.9 select_reduce_fusion
  15.9 0.6 copy.23
  16.5 0.2 copy.25
  16.7 0.9 fusion.2.pick_ref
  17.6 15.3 %table_rows.1.served_hbm = bf16[4,1024,256]{2,1,0:T(8,128)(2,1)} custom-call(s32[1024]{0:T(1024)} %bitcast.38, s32[4]{0:T(128)} %dynamic_slice.7.counts_ref, s32[1024,1]{1,0:T(8,128)} %fusion.2.pick_ref, bf16[4,32064,256]{2,1,0:T(8,128)(2,1)} %tables_hbm.1), custom_call_target="tpu_custom_call" | custom-call | tf_op jit(solution)/shard_map/table_rows/pallas_call | solution.py:562
  32.9 75.8 %first_layer.1 = (bf16[512,3072]{1,0:T(8,128)(2,1)}, f32[1,512,256]{2,1,0:T(8,128)}, bf16[4,512,256]{2,1,0:T(8,128)(2,1)}) custom-call(bf16[512,3072]{1,0:T(8,128)(2,1)} %x_hbm.1, s32[512,1]{1,0:T(8,128)} %copy.18.slot_ref, bf16[4,1024,256]{2,1,0:T(8,128)(2,1)} %table_rows.1.served_hbm, bf16[4,3072,256]{2,1,0:T(8,128)(2,1)} %wg_ref.5, ...), custom_call_target="tpu_custom_call" | custom-call | flops 51539607552 | bytes 104857600 | tf_op jit(solution)/shard_map/first_layer/pallas_call | solution.py:585
  108.7 202.1 %forward.1 = (bf16[512,3072]{1,0:T(8,128)(2,1)}, bf16[2,512,3072]{2,1,0:T(8,128)(2,1)}, f32[3,512,8192]{2,1,0:T(8,128)}, f32[3,512,256]{2,1,0:T(8,128)}, f32[512...) custom-call(bf16[512,3072]{1,0:T(8,128)(2,1)} %get-tuple-element.17.x_hbm.x1_hbm, ...), custom_call_target="tpu_custom_call" | custom-call | flops 154618822656 | bytes 419430400 | tf_op jit(solution)/shard_map/forward/pallas_call | solution.py:609
  310.8 210.7 %backward.1 = (f32[3,2048,256]{2,1,0:T(8,128)}, f32[2048,256]{1,0:T(8,128)}, bf16[2,1024,256]{2,1,0:T(8,128)(2,1)}) custom-call(bf16[512,3072]{1,0:T(8,128)(2,1)} %cot_hbm.3, bf16[512,3072]{1,0:T(8,128)(2,1)} %get-tuple-element.17.x_hbm.x1_hbm, bf16[2,512,3072]{2,1,0:T(8,128)(2,1)} %get-tuple-element.21.saved_hbm, f32[512,256]{1,0:T(8,128)} %get-tuple-element.22.rows_in_ref, ...), custom_call_target="tpu_custom_call" | custom-call | flops 154618822656 | bytes 419430400 | tf_op jit(solution)/shard_map/backward/pallas_call | solution.py:639
  521.5 3.0 all-to-all-start
  524.5 0.8 select_bitcast_fusion
  525.2 5.0 sort.14
  530.3 0.6 concatenate.3.keys_ref
  530.9 23.2 %scatter_1.1.refs_2_ = f32[4,4008,8,256]{3,2,1,0:T(8,128)} custom-call(s32[2176]{0:T(1024)} %concatenate.3.keys_ref, s32[1]{0:T(128)} %bitcast.2.meta_ref, f32[3,2048,256]{2,1,0:T(8,128)} %get-tuple-element.29.refs_0_, f32[4,4008,8,256]{3,2,1,0:T(8,128)} %bitcast.6.refs_1_), custom_call_target="tpu_custom_call", output_to_operand_aliasing={{}: (3, {})} | custom-call | flops 60000002048 | bytes 12582912 | tf_op jit(solution)/shard_map/scatter_1/pallas_call | solution.py:667
  554.1 21.7 %scatter_0.1 = f32[4,4008,8,256]{3,2,1,0:T(8,128)} custom-call(s32[2176]{0:T(1024)} %concatenate.3.keys_ref, s32[1]{0:T(128)} %bitcast.2.meta_ref, f32[2048,256]{1,0:T(8,128)} %get-tuple-element.27.refs_0_, bf16[2048,256]{1,0:T(8,128)(2,1)} %bitcast.5.refs_1_, f32[4,4008,8,256]{3,2,1,0:T(8,128)} %scatter_1.1.refs_2_), custom_call_target="tpu_custom_call", output_to_operand_aliasing={{}: (4, {})} | custom-call | flops 20000000000 | bytes 4194304 | tf_op jit(solution)/shard_map/scatter_0/pallas_call | solution.py:667
  (16 shorter events, 0.2 us)
Async XLA Ops:
  2.4 10.2 %copy-start.1 = (s32[512]{0:T(512)}, s32[512]{0:T(512)S(1)}, u32[]{:S(2)}) copy-start(s32[512]{0:T(512)S(1)} %multiply_add_fusion.1) | copy-start | bytes 6148
  13.5 3.0 copy-start.2
  15.8 0.6 copy-start
  521.5 32.7 %all-to-all-start = ((bf16[8,256,256]{2,1,0:T(8,128)(2,1)}), bf16[8,256,256]{2,1,0:T(8,128)(2,1)}, u32[]{:S(2)}, u32[]{:S(2)}) async-start(bf16[8,256,256]{2,1,0:T(8,128)(2,1)} %bitcast.32), calls=%async_computation | async-start | bytes 2097152 | tf_op jit(solution)/shard_map/all_to_all | solution.py:679

commit v4 on v3

--- a/solution.py
+++ b/solution.py
@@ -126,27 +126,47 @@
         lax.fori_loop(n_trips[d], cap // trip, blank, 0)
 
 
+def weight_copies(wu_hbm, wd_hbm, wu_s, wd_s, sems):
+    fb = wu_s.shape[2]
+
+    def copies(layer, blk, slot):
+        at = pl.multiple_of(blk * fb, fb)
+        return (pltpu.make_async_copy(wu_hbm.at[layer, :, pl.ds(at, fb)], wu_s.at[slot], sems.at[0, slot]),
+                pltpu.make_async_copy(wd_hbm.at[layer, pl.ds(at, fb), :], wd_s.at[slot], sems.at[1, slot]))
+
+    return copies
+
+
+def start(copies):
+    for copy in copies:
+        copy.start()
+
+
+def wait(copies):
+    for copy in copies:
+        copy.wait()
+
+
 def mlp_block(cfg, u_s, h_s, acc_s, wu_ref, wd_ref, up_ref):
     cw, nw = cfg
     gw = 128
-    fb = wu_ref.shape[2]
+    n_c = wu_ref.shape[1] // cw
 
     def act(c):
         for g in range(cw // gw):
             gs = slice(c * cw + g * gw, c * cw + (g + 1) * gw)
-            h_s[:, gs] = gelu(up_ref[0, :, gs]).astype(BF)
-
-    n_c = fb // cw
+            h_s[:, gs] = gelu(up_ref[:, gs]).astype(BF)
+
     for c in range(n_c):
         cs = slice(c * cw, (c + 1) * cw)
-        up_ref[0, :, cs] = dot(u_s[...], wu_ref[0, :, cs])
+        up_ref[:, cs] = dot(u_s[...], wu_ref[:, cs])
         if c > 0:
             act(c - 1)
     for c in range(n_c):
         cs = slice(c * cw, (c + 1) * cw)
         for n in range(acc_s.shape[1] // nw):
             ns = slice(n * nw, (n + 1) * nw)
-            acc_s[:, ns] += dot(h_s[:, cs], wd_ref[0, cs, ns])
+            acc_s[:, ns] += dot(h_s[:, cs], wd_ref[cs, ns])
         if c == 0:
             act(n_c - 1)
 
@@ -160,15 +180,13 @@
 def add_proj(nw, acc_s, mixed, wp_ref):
     for n in range(acc_s.shape[1] // nw):
         ns = slice(n * nw, (n + 1) * nw)
-        acc_s[:, ns] += dot(mixed, wp_ref[0, :, ns])
-
-
-def first_kernel(cfg, x_hbm, slot_ref, served_hbm, wg_ref, wp_ref, wu_ref, wd_ref,
+        acc_s[:, ns] += dot(mixed, wp_ref[:, ns])
+
+
+def first_kernel(cfg, x_hbm, slot_ref, served_hbm, wg_hbm, wp_hbm, wu_hbm, wd_hbm,
                  x_out_ref, gate_ref, fet_ref,
-                 u_s, acc_s, h_s, up_s, ret_s, in_sem, self_sem, send_sem, recv_sem):
-    n_dp, n_emb, cap, cw, nw, slab = cfg
-    n_blk = pl.num_programs(0)
-    blk = pl.program_id(0)
+                 u_s, acc_s, h_s, up_s, ret_s, wu_s, wd_s, wg_s, wp_s, in_sem, w_sem, self_sem, send_sem, recv_sem):
+    n_dp, n_emb, cap, n_blk, cw, nw, slab = cfg
     tok, dim = u_s.shape
     my_emb = lax.axis_index('emb')
     my_dp = lax.axis_index('dp')
@@ -177,76 +195,120 @@
     peers = [lax.rem(my_emb + k, n_emb) for k in range(1, n_emb)]
     copies = [remote(served_hbm.at[:, pl.ds(pl.multiple_of(p * cap, cap), cap), :], here,
                      send_sem.at[k], recv_sem.at[k], {'dp': my_dp, 'emb': p}) for k, p in enumerate(peers)]
-
-    @pl.when(blk == 0)
-    def _():
-        fetch = pltpu.make_async_copy(x_hbm, x_out_ref, in_sem)
-        fetch.start()
-        meet([{'dp': my_dp, 'emb': p} for p in peers])
-        own.start()
-        for copy in copies:
-            copy.start()
-        fetch.wait()
-        row_loop(tok, slab)(lambda sl: norm_rows(x_out_ref[sl, :].astype(F32), sl, u_s, acc_s))
-        gate_ref[0] = dot(u_s[...], wg_ref[0])
-
-    mlp_block((cw, nw), u_s, h_s, acc_s, wu_ref, wd_ref, up_s)
-
-    @pl.when(blk == n_blk - 1)
-    def _():
-        own.wait()
-        for copy in copies:
-            copy.wait()
-        sel = (lax.broadcasted_iota(I32, (tok, n_emb * cap), 1) == slot_ref[...]).astype(BF)
-        for l in range(fet_ref.shape[0]):
-            fet_ref[l] = dot(sel, ret_s[l]).astype(BF)
-        add_proj(nw, acc_s, (gelu(gate_ref[0]) * fet_ref[0].astype(F32)).astype(BF), wp_ref)
-
-        def finish(sl):
-            x_out_ref[sl, :] = acc_s[sl, :].astype(BF)
-
-        row_loop(tok, slab)(finish)
-
-
-def forward_kernel(cfg, x_hbm, cot_hbm, fet_ref, wg_ref, wp_ref, wu_ref, wd_ref,
-                   out_hbm, saved_hbm, up_ref, gate_ref, rows_ref, dgp_ref, dtab_hbm,
-                   x_s, u_s, acc_s, h_s, zero_s, in_sem, out_sem, z_sem):
+    weights = weight_copies(wu_hbm, wd_hbm, wu_s, wd_s, w_sem)
+    first = [pltpu.make_async_copy(x_hbm, x_out_ref, in_sem.at[0]),
+             pltpu.make_async_copy(wg_hbm.at[0], wg_s, in_sem.at[1]),
+             pltpu.make_async_copy(wp_hbm.at[0], wp_s, in_sem.at[2])]
+    start(first[:2])
+    start(weights(0, 0, 0))
+    start(first[2:])
+    meet([{'dp': my_dp, 'emb': p} for p in peers])
+    own.start()
+    start(copies)
+    first[0].wait()
+    row_loop(tok, slab)(lambda sl: norm_rows(x_out_ref[sl, :].astype(F32), sl, u_s, acc_s))
+    first[1].wait()
+    gate_ref[0] = dot(u_s[...], wg_s[...])
+
+    def block(f, carry):
+        slot = lax.rem(f, 2)
+
+        @pl.when(f + 1 < n_blk)
+        def _():
+            start(weights(0, f + 1, 1 - slot))
+
+        wait(weights(0, f, slot))
+        mlp_block((cw, nw), u_s, h_s, acc_s, wu_s.at[slot], wd_s.at[slot], up_s)
+        return carry
+
+    lax.fori_loop(0, n_blk, block, 0)
+    own.wait()
+    wait(copies)
+    first[2].wait()
+    sel = (lax.broadcasted_iota(I32, (tok, n_emb * cap), 1) == slot_ref[...]).astype(BF)
+    for l in range(fet_ref.shape[0]):
+        fet_ref[l] = dot(sel, ret_s[l]).astype(BF)
+    add_proj(nw, acc_s, (gelu(gate_ref[0]) * fet_ref[0].astype(F32)).astype(BF), wp_s)
+
+    def finish(sl):
+        x_out_ref[sl, :] = acc_s[sl, :].astype(BF)
+
+    row_loop(tok, slab)(finish)
+
+
+def forward_kernel(cfg, x_hbm, cot_hbm, fet_ref, wg_hbm, wp_hbm, wu_hbm, wd_hbm,
+                   out_hbm, saved_hbm, ups_hbm, gate_ref, rows_ref, dgp_ref, dtab_hbm,
+                   x_s, u_s, acc_s, h_s, up_s, zero_s, wu_s, wd_s, wg_s, wp_s, in_sem, w_sem, up_sem, out_sem, z_sem):
     n_layers, n_blk, cw, nw, slab, z_per, z_chunks = cfg
-    layer, blk = pl.program_id(0), pl.program_id(1)
     tok, dim = x_s.shape
-    step = layer * n_blk + blk
+    fb = wu_s.shape[2]
     z_rows = zero_s.shape[0]
-
-    def z_copy(j):
-        c = step * z_per + j
-        zl = c // z_chunks
-        zc = c - zl * z_chunks
-        return pltpu.make_async_copy(zero_s, dtab_hbm.at[zl, pl.ds(pl.multiple_of(zc * z_rows, 8), z_rows), :], z_sem.at[j])
-
-    @pl.when(step == 0)
-    def _():
-        fetch = pltpu.make_async_copy(x_hbm, x_s, in_sem)
-        fetch.start()
-        row_loop(z_rows, 8, 1)(lambda sl: zero_s.__setitem__((sl, slice(None)), jnp.zeros((8, zero_s.shape[1]), F32)))
-        fetch.wait()
-        row_loop(tok, slab)(lambda sl: norm_rows(x_s[sl, :].astype(F32), sl, u_s, acc_s))
-
-    for j in range(z_per):
-        @pl.when(step > 0)
-        def _():
-            z_copy(j).wait()
-
-        z_copy(j).start()
-
-    @pl.when(blk == 0)
-    def _():
-        gate_ref[0] = dot(u_s[...], wg_ref[0])
-
-    mlp_block((cw, nw), u_s, h_s, acc_s, wu_ref, wd_ref, up_ref)
-
-    @pl.when(blk == n_blk - 1)
-    def _():
-        add_proj(nw, acc_s, (gelu(gate_ref[0]) * fet_ref[0].astype(F32)).astype(BF), wp_ref)
+    n_steps = n_layers * n_blk
+    weights = weight_copies(wu_hbm, wd_hbm, wu_s, wd_s, w_sem)
+
+    def z_copies(step):
+        found = []
+        for j in range(z_per):
+            c = step * z_per + j
+            zl = c // z_chunks
+            zc = c - zl * z_chunks
+            found.append(pltpu.make_async_copy(
+                zero_s, dtab_hbm.at[zl, pl.ds(pl.multiple_of(zc * z_rows, 8), z_rows), :], z_sem.at[j]))
+        return found
+
+    def up_copy(layer, blk, slot):
+        return pltpu.make_async_copy(up_s.at[slot], ups_hbm.at[layer, :, pl.ds(pl.multiple_of(blk * fb, fb), fb)], up_sem.at[slot])
+
+    def gate_copy(layer):
+        return pltpu.make_async_copy(wg_hbm.at[layer + 1], wg_s, in_sem.at[1])
+
+    def proj_copy(layer):
+        return pltpu.make_async_copy(wp_hbm.at[layer + 1], wp_s, in_sem.at[2])
+
+    fetch = pltpu.make_async_copy(x_hbm, x_s, in_sem.at[0])
+    fetch.start()
+    gate_copy(0).start()
+    start(weights(1, 0, 0))
+    proj_copy(0).start()
+    row_loop(z_rows, 8, 1)(lambda sl: zero_s.__setitem__((sl, slice(None)), jnp.zeros((8, zero_s.shape[1]), F32)))
+    fetch.wait()
+    row_loop(tok, slab)(lambda sl: norm_rows(x_s[sl, :].astype(F32), sl, u_s, acc_s))
+
+    def one_layer(layer, carry):
+        gate_copy(layer).wait()
+        gate_ref[layer] = dot(u_s[...], wg_s[...])
+
+        @pl.when(layer + 1 < n_layers)
+        def _():
+            gate_copy(layer + 1).start()
+
+        def block(f, carry):
+            step = layer * n_blk + f
+            slot = lax.rem(step, 2)
+
+            @pl.when(step + 1 < n_steps)
+            def _():
+                nxt = step + 1
+                start(weights(1 + nxt // n_blk, lax.rem(nxt, n_blk), 1 - slot))
+
+            @pl.when(step > 0)
+            def _():
+                wait(z_copies(step - 1))
+
+            start(z_copies(step))
+
+            @pl.when(step > 1)
+            def _():
+                up_copy(layer, f, slot).wait()
+
+            wait(weights(1 + layer, f, slot))
+            mlp_block((cw, nw), u_s, h_s, acc_s, wu_s.at[slot], wd_s.at[slot], up_s.at[slot])
+            up_copy(layer, f, slot).start()
+            return carry
+
+        lax.fori_loop(0, n_blk, block, 0)
+        proj_copy(layer).wait()
+        add_proj(nw, acc_s, (gelu(gate_ref[layer]) * fet_ref[layer + 1].astype(F32)).astype(BF), wp_s)
 
         @pl.when(layer > 0)
         def _():
@@ -262,19 +324,22 @@
         @pl.when(layer < n_layers - 1)
         def _():
             pltpu.make_async_copy(x_s, saved_hbm.at[layer], out_sem).start()
-
-        @pl.when(layer == n_layers - 1)
-        def _():
-            put = pltpu.make_async_copy(x_s, out_hbm, out_sem)
-            put.start()
-            get = pltpu.make_async_copy(cot_hbm, u_s, in_sem)
-            get.start()
-            for j in range(z_per):
-                z_copy(j).wait()
-            get.wait()
-            d_mixed = dot_t(u_s[...], wp_ref[0]).astype(BF).astype(F32)
-            gate_grads(gate_ref[0], fet_ref[0], d_mixed, rows_ref, dgp_ref)
-            put.wait()
+            proj_copy(layer + 1).start()
+
+        return carry
+
+    lax.fori_loop(0, n_layers, one_layer, 0)
+    put = pltpu.make_async_copy(x_s, out_hbm, out_sem)
+    put.start()
+    get = pltpu.make_async_copy(cot_hbm, u_s, in_sem.at[0])
+    get.start()
+    wait(z_copies(n_steps - 1))
+    up_copy(0, 0, 0).wait()
+    up_copy(0, 0, 1).wait()
+    get.wait()
+    d_mixed = dot_t(u_s[...], wp_s[...]).astype(BF).astype(F32)
+    gate_grads(gate_ref[n_layers - 1], fet_ref[n_layers], d_mixed, rows_ref, dgp_ref)
+    put.wait()
 
 
 def gate_grads(gate_pre, fetched, d_mixed, rows_ref, dgp_ref):
@@ -295,129 +360,155 @@
     return (lax.broadcasted_iota(I32, (n, slot_ref.shape[1]), 0) == slot_ref[...]).astype(BF)
 
 
-def backward_kernel(cfg, cot_hbm, x1_hbm, saved_hbm, rows_in_ref, dgp_in_ref, slot_ref, gate0_ref,
-                    up_ref, wu_ref, wd_ref, wg_ref, wp_ref, gate_ref, fet_ref,
+def backward_kernel(cfg, cot_hbm, x1_hbm, saved_hbm, rows_in_ref, dgp_in_ref, slot_ref, gate0_ref, gate_ref, fet_ref,
+                    ups_hbm, wu_hbm, wd_hbm, wg_hbm, wp_hbm,
                     got_hbm, gate_hbm, slots0_ref,
-                    cot_s, x_s, acc_s, dup_s, dh_s, dng_s, slots_s, gslots_s, rows_s, dgp_s, in_sem, x_sem, send_sem, self_sem, recv_sem):
+                    cot_s, x_s, acc_s, dup_s, dh_s, dng_s, slots_s, gslots_s, rows_s, dgp_s, up_s, wu_s, wd_s, wg_s, wp_s,
+                    in_sem, w_sem, up_sem, send_sem, self_sem, recv_sem):
     n_layers, n_blk, n_dp, n_emb, cap, cw, nw, slab = cfg
-    i, blk = pl.program_id(0), pl.program_id(1)
-    layer = n_layers - i
     tok, dim = cot_s.shape
-    fb = wu_ref.shape[2]
+    fb = wu_s.shape[2]
+    gw = 128
     n_dev = n_dp * n_emb
-    me = lax.axis_index('dp') * n_emb + lax.axis_index('emb')
+    n_steps = n_layers * n_blk
+    my_emb = lax.axis_index('emb')
+    me = lax.axis_index('dp') * n_emb + my_emb
     peers = [peer_of(n_emb, lax.rem(me + k, n_dev)) for k in range(1, n_dev)]
-    here = got_hbm.at[layer - 1, pl.ds(pl.multiple_of(me * cap, cap), cap), :]
-
-    g_here = gate_hbm.at[pl.ds(pl.multiple_of(me * cap, cap), cap), :]
+    weights = weight_copies(wu_hbm, wd_hbm, wu_s, wd_s, w_sem)
 
     def part(ref, emb):
         return ref.at[pl.ds(pl.multiple_of(emb * cap, cap), cap), :]
 
-    own = pltpu.make_async_copy(part(slots_s, lax.axis_index('emb')), here, self_sem.at[0])
-    copies = [remote(part(slots_s, peer['emb']), here, send_sem.at[0, k], recv_sem.at[i, k], peer) for k, peer in enumerate(peers)]
-    g_own = pltpu.make_async_copy(part(gslots_s, lax.axis_index('emb')), g_here, self_sem.at[1])
-    g_copies = [remote(part(gslots_s, peer['emb']), g_here, send_sem.at[1, k], recv_sem.at[n_layers, k], peer)
-                for k, peer in enumerate(peers)]
-
-    @pl.when(blk == 0)
-    def _():
-        @pl.when(i == 0)
-        def _():
-            fetch = pltpu.make_async_copy(cot_hbm, cot_s, in_sem)
-            fetch.start()
-            rows_s[...] = rows_in_ref[...]
-            dgp_s[...] = dgp_in_ref[...]
-            meet(peers)
-            fetch.wait()
-
+    def sends(ref, there, which, got):
+        return [pltpu.make_async_copy(part(ref, my_emb), there, self_sem.at[which])] + [
+            remote(part(ref, peer['emb']), there, send_sem.at[which, k], recv_sem.at[got, k], peer) for k, peer in enumerate(peers)]
+
+    def row_sends(i):
+        return sends(slots_s, part(got_hbm.at[n_layers - 1 - i], me), 0, i)
+
+    gate_sends = sends(gslots_s, part(gate_hbm, me), 1, n_layers)
+
+    def up_copy(step, slot):
+        i = step // n_blk
+        blk = step - i * n_blk
+        return pltpu.make_async_copy(ups_hbm.at[n_layers - 1 - i, :, pl.ds(pl.multiple_of(blk * fb, fb), fb)], up_s.at[slot], up_sem.at[slot])
+
+    def load(step, slot):
+        i = step // n_blk
+        return weights(n_layers - i, step - i * n_blk, slot) + (up_copy(step, slot),)
+
+    def gate_copy(i):
+        return pltpu.make_async_copy(wg_hbm.at[n_layers - i], wg_s, in_sem.at[1])
+
+    def proj_copy(i):
+        return pltpu.make_async_copy(wp_hbm.at[n_layers - 1 - i], wp_s, in_sem.at[2])
+
+    def x_copy(i):
+        return pltpu.make_async_copy(saved_hbm.at[n_layers - 2 - i], x_s, in_sem.at[3])
+
+    fetch = pltpu.make_async_copy(cot_hbm, cot_s, in_sem.at[0])
+    gate_copy(0).start()
+    fetch.start()
+    start(load(0, 0))
+    proj_copy(0).start()
+    rows_s[...] = rows_in_ref[...]
+    dgp_s[...] = dgp_in_ref[...]
+
+    def clear(sl):
+        acc_s[sl, :] = jnp.zeros((slab, dim), F32)
+
+    row_loop(tok, slab)(clear)
+    meet(peers)
+    to_slots(gelu(gate0_ref[0]), slot_ref, gslots_s)
+
+    def one_layer(i, carry):
         @pl.when(i < n_layers - 1)
         def _():
-            pltpu.make_async_copy(saved_hbm.at[n_layers - 2 - i], x_s, x_sem).start()
+            x_copy(i).start()
 
         @pl.when(i == n_layers - 1)
         def _():
-            pltpu.make_async_copy(x1_hbm, x_s, x_sem).start()
+            pltpu.make_async_copy(x1_hbm, x_s, in_sem.at[3]).start()
 
         to_slots(rows_s[...], slot_ref, slots_s)
+        gate_copy(i).wait()
         for n in range(dim // nw):
             ns = slice(n * nw, (n + 1) * nw)
-            dng_s[:, ns] = dot_t(dgp_s[...], wg_ref[0, ns, :]).astype(BF)
-
-        def clear(sl):
-            acc_s[sl, :] = jnp.zeros((slab, dim), F32)
-
-        row_loop(tok, slab)(clear)
-
-    @pl.when(blk == 1)
-    def _():
-        own.start()
-        for copy in copies:
-            copy.start()
-
-    @pl.when((blk == 2) & (i == 0))
-    def _():
-        to_slots(gelu(gate0_ref[0]), slot_ref, gslots_s)
-
-    @pl.when((blk == 3) & (i == 0))
-    def _():
-        g_own.start()
-        for copy in g_copies:
-            copy.start()
-
-    gw = 128
-
-    def act(c):
-        for g in range(cw // gw):
-            gs = slice(c * cw + g * gw, c * cw + (g + 1) * gw)
-            dup_s[:, gs] = (dh_s[:, gs].astype(F32) * gelu_slope(up_ref[0, :, gs])).astype(BF)
-
-    for c in range(fb // cw):
-        cs = slice(c * cw, (c + 1) * cw)
-        dh_s[:, cs] = dot_t(cot_s[...], wd_ref[0, cs, :]).astype(BF)
-        if c > 0:
-            act(c - 1)
-    for c in range(fb // cw):
-        cs = slice(c * cw, (c + 1) * cw)
-        for n in range(dim // nw):
-            ns = slice(n * nw, (n + 1) * nw)
-            acc_s[:, ns] += dot_t(dup_s[:, cs], wu_ref[0, ns, cs])
-        if c == 0:
-            act(fb // cw - 1)
-
-    @pl.when(blk == n_blk - 1)
-    def _():
-        pltpu.make_async_copy(x1_hbm, x_s, x_sem).wait()
+            dng_s[:, ns] = dot_t(dgp_s[...], wg_s[ns, :]).astype(BF)
+        start(row_sends(i))
+
+        @pl.when(i < n_layers - 1)
+        def _():
+            gate_copy(i + 1).start()
+
+        @pl.when(i == 0)
+        def _():
+            start(gate_sends)
+            fetch.wait()
+
+        def block(f, carry):
+            step = i * n_blk + f
+            slot = lax.rem(step, 2)
+
+            @pl.when(step + 1 < n_steps)
+            def _():
+                start(load(step + 1, 1 - slot))
+
+            wait(load(step, slot))
+            wu_ref, wd_ref, up_ref = wu_s.at[slot], wd_s.at[slot], up_s.at[slot]
+
+            def act(c):
+                for g in range(cw // gw):
+                    gs = slice(c * cw + g * gw, c * cw + (g + 1) * gw)
+                    dup_s[:, gs] = (dh_s[:, gs].astype(F32) * gelu_slope(up_ref[:, gs])).astype(BF)
+
+            n_c = fb // cw
+            for c in range(n_c):
+                cs = slice(c * cw, (c + 1) * cw)
+                dh_s[:, cs] = dot_t(cot_s[...], wd_ref[cs, :]).astype(BF)
+                if c > 0:
+                    act(c - 1)
+            for c in range(n_c):
+                cs = slice(c * cw, (c + 1) * cw)
+                for n in range(dim // nw):
+                    ns = slice(n * nw, (n + 1) * nw)
+                    acc_s[:, ns] += dot_t(dup_s[:, cs], wu_ref[ns, cs])
+                if c == 0:
+                    act(n_c - 1)
+            return carry
+
+        lax.fori_loop(0, n_blk, block, 0)
+        pltpu.make_async_copy(x1_hbm, x_s, in_sem.at[3]).wait()
 
         def rows_back(sl):
             x = x_s[sl, :].astype(F32)
             scale = lax.rsqrt(jnp.mean(x * x, axis=-1, keepdims=True) + NORM_EPS)
             d_n = (acc_s[sl, :].astype(BF).astype(F32) + dng_s[sl, :].astype(F32)).astype(BF).astype(F32)
+            acc_s[sl, :] = jnp.zeros((slab, dim), F32)
             proj = jnp.mean(d_n * x, axis=-1, keepdims=True)
             d_x = d_n * scale - x * (proj * (scale * scale * scale))
             cot_s[sl, :] = (cot_s[sl, :].astype(F32) + d_x).astype(BF)
 
         row_loop(tok, slab)(rows_back)
-        d_mixed = dot_t(cot_s[...], wp_ref[0]).astype(BF)
-        own.wait()
-        for copy in copies:
-            copy.wait()
-
-        @pl.when(i == 0)
-        def _():
-            g_own.wait()
-            for copy in g_copies:
-                copy.wait()
+        proj_copy(i).wait()
+        d_mixed = dot_t(cot_s[...], wp_s[...]).astype(BF)
+        wait(row_sends(i))
 
         @pl.when(i < n_layers - 1)
         def _():
-            gate_grads(gate_ref[0], fet_ref[0], d_mixed.astype(F32), rows_s, dgp_s)
+            proj_copy(i + 1).start()
+            gate_grads(gate_ref[jnp.maximum(n_layers - 2 - i, 0)], fet_ref[n_layers - 1 - i], d_mixed.astype(F32), rows_s, dgp_s)
 
         @pl.when(i == n_layers - 1)
         def _():
             slots = dot(slot_pick(slots_s.shape[0], slot_ref), d_mixed).astype(BF)
             for d in range(n_dp):
                 slots0_ref[d] = slots
+
+        return carry
+
+    lax.fori_loop(0, n_layers, one_layer, 0)
+    wait(gate_sends)
 
 
 def scatter_kernel(cfg, keys_ref, meta_ref, *refs):
@@ -578,37 +669,29 @@
         z_per = n_layers * z_chunks // (n_back * n_blk)
         assert z_chunks * z_rows == range_rows and z_per * n_blk * n_back == z_chunks * n_layers
 
-        def flat(*shape):
-            return pl.BlockSpec(shape, lambda *_: (0,) * len(shape), pipeline_mode=pl.Buffered(1))
-
         matmul_flops = 4 * tok * dim * ffn
+        w_bufs = [pltpu.VMEM((2, dim, fb), BF), pltpu.VMEM((2, fb, dim), BF), pltpu.VMEM((dim, e_dim), BF), pltpu.VMEM((e_dim, dim), BF)]
+        dma = pltpu.SemaphoreType.DMA
         x1, gate0, fetched = pl.pallas_call(
-            functools.partial(first_kernel, (n_dp, n_emb, CAP, cw, nw, slab)),
-            grid=(n_blk,),
+            functools.partial(first_kernel, (n_dp, n_emb, CAP, n_blk, cw, nw, slab)),
             out_shape=[
                 jax.ShapeDtypeStruct((tok, dim), BF),
                 jax.ShapeDtypeStruct((1, tok, e_dim), F32),
                 jax.ShapeDtypeStruct((n_layers, tok, e_dim), BF),
             ],
-            in_specs=[hbm, flat(tok, 1), hbm, flat(1, dim, e_dim), flat(1, e_dim, dim),
-                      pl.BlockSpec((1, dim, fb), lambda f: (0, 0, f)), pl.BlockSpec((1, fb, dim), lambda f: (0, f, 0))],
-            out_specs=[flat(tok, dim), flat(1, tok, e_dim), flat(n_layers, tok, e_dim)],
+            in_specs=[hbm, vm, hbm, hbm, hbm, hbm, hbm],
+            out_specs=[vm, vm, vm],
             scratch_shapes=[
-                pltpu.VMEM((tok, dim), BF), pltpu.VMEM((tok, dim), F32), pltpu.VMEM((tok, fb), BF), pltpu.VMEM((1, tok, fb), F32),
-                pltpu.VMEM((n_layers, n_serve, e_dim), BF), pltpu.SemaphoreType.DMA, pltpu.SemaphoreType.DMA,
-                pltpu.SemaphoreType.DMA((n_emb - 1,)), pltpu.SemaphoreType.DMA((n_emb - 1,)),
+                pltpu.VMEM((tok, dim), BF), pltpu.VMEM((tok, dim), F32), pltpu.VMEM((tok, fb), BF), pltpu.VMEM((tok, fb), F32),
+                pltpu.VMEM((n_layers, n_serve, e_dim), BF), *w_bufs, dma((3,)), dma((2, 2)), dma, dma((n_emb - 1,)), dma((n_emb - 1,)),
             ],
-            compiler_params=params(1, collective_id=1, has_side_effects=True),
+            compiler_params=params(0, collective_id=1, has_side_effects=True),
             cost_estimate=pl.CostEstimate(flops=matmul_flops, bytes_accessed=100 << 20, transcendentals=0),
             name='first_layer',
         )(resid_in, slot_of[:, None], served, w_gate, w_proj, w_up, w_down)
 
-        def lsp(*shape):
-            return pl.BlockSpec((1,) + shape, lambda l, f: (l + 1, 0, 0))
-
         out, saved, ups, gates, rows, dgp, dtab = pl.pallas_call(
             functools.partial(forward_kernel, (n_back, n_blk, cw, nw, slab, z_per, z_chunks)),
-            grid=(n_back, n_blk),
             out_shape=[
                 jax.ShapeDtypeStruct((tok, dim), BF),
                 jax.ShapeDtypeStruct((n_back - 1, tok, dim), BF),
@@ -618,45 +701,34 @@
                 jax.ShapeDtypeStruct((tok, e_dim), BF),
                 jax.ShapeDtypeStruct((n_layers, range_rows, e_dim), F32),
             ],
-            in_specs=[hbm, hbm, lsp(tok, e_dim), lsp(dim, e_dim), lsp(e_dim, dim),
-                      pl.BlockSpec((1, dim, fb), lambda l, f: (l + 1, 0, f)), pl.BlockSpec((1, fb, dim), lambda l, f: (l + 1, f, 0))],
-            out_specs=[hbm, hbm,
-                       pl.BlockSpec((1, tok, fb), lambda l, f: (l, 0, f)),
-                       pl.BlockSpec((1, tok, e_dim), lambda l, f: (l, 0, 0)),
-                       flat(tok, e_dim), flat(tok, e_dim), hbm],
+            in_specs=[hbm, hbm, vm, hbm, hbm, hbm, hbm],
+            out_specs=[hbm, hbm, hbm, vm, vm, vm, hbm],
             scratch_shapes=[
                 pltpu.VMEM((tok, dim), BF), pltpu.VMEM((tok, dim), BF), pltpu.VMEM((tok, dim), F32), pltpu.VMEM((tok, fb), BF),
-                pltpu.VMEM((z_rows, e_dim), F32), pltpu.SemaphoreType.DMA, pltpu.SemaphoreType.DMA, pltpu.SemaphoreType.DMA((z_per,)),
+                pltpu.VMEM((2, tok, fb), F32), pltpu.VMEM((z_rows, e_dim), F32), *w_bufs,
+                dma((3,)), dma((2, 2)), dma((2,)), dma, dma((z_per,)),
             ],
-            compiler_params=params(2),
+            compiler_params=params(0),
             cost_estimate=pl.CostEstimate(flops=n_back * matmul_flops, bytes_accessed=400 << 20, transcendentals=0),
             name='forward',
         )(x1, cot_out, fetched, w_gate, w_proj, w_up, w_down)
 
-        def of_layer(off, *shape):
-            return pl.BlockSpec((1,) + shape, lambda i, f: (jnp.maximum(n_back - i + off, 0), 0, 0))
-
         got, got_gate, slots0 = pl.pallas_call(
             functools.partial(backward_kernel, (n_back, n_blk, n_dp, n_emb, CAP, cw, nw, slab)),
-            grid=(n_back, n_blk),
             out_shape=[jax.ShapeDtypeStruct((n_back, n_slots, e_dim), F32), jax.ShapeDtypeStruct((n_slots, e_dim), F32),
                        jax.ShapeDtypeStruct((n_dp, n_serve, e_dim), BF)],
-            in_specs=[hbm, hbm, hbm, flat(tok, e_dim), flat(tok, e_dim), flat(1, tok), flat(1, tok, e_dim),
-                      pl.BlockSpec((1, tok, fb), lambda i, f: (n_back - 1 - i, 0, f)),
-                      pl.BlockSpec((1, dim, fb), lambda i, f: (n_back - i, 0, f)), pl.BlockSpec((1, fb, dim), lambda i, f: (n_back - i, f, 0)),
-                      of_layer(0, dim, e_dim), of_layer(-1, e_dim, dim), of_layer(-2, tok, e_dim), of_layer(-1, tok, e_dim)],
-            out_specs=[hbm, hbm, flat(n_dp, n_serve, e_dim)],
+            in_specs=[hbm, hbm, hbm, vm, vm, vm, vm, vm, vm, hbm, hbm, hbm, hbm, hbm],
+            out_specs=[hbm, hbm, vm],
             scratch_shapes=[
                 pltpu.VMEM((tok, dim), BF), pltpu.VMEM((tok, dim), BF), pltpu.VMEM((tok, dim), F32), pltpu.VMEM((tok, fb), BF), pltpu.VMEM((tok, fb), BF),
                 pltpu.VMEM((tok, dim), BF), pltpu.VMEM((n_serve, e_dim), F32), pltpu.VMEM((n_serve, e_dim), F32),
-                pltpu.VMEM((tok, e_dim), F32), pltpu.VMEM((tok, e_dim), BF),
-                pltpu.SemaphoreType.DMA, pltpu.SemaphoreType.DMA,
-                pltpu.SemaphoreType.DMA((2, n_dev - 1)), pltpu.SemaphoreType.DMA((2,)), pltpu.SemaphoreType.DMA((n_back + 1, n_dev - 1)),
+                pltpu.VMEM((tok, e_dim), F32), pltpu.VMEM((tok, e_dim), BF), pltpu.VMEM((2, tok, fb), F32), *w_bufs,
+                dma((4,)), dma((2, 2)), dma((2,)), dma((2, n_dev - 1)), dma((2,)), dma((n_back + 1, n_dev - 1)),
             ],
-            compiler_params=params(2, collective_id=2, has_side_effects=True),
+            compiler_params=params(0, collective_id=2, has_side_effects=True),
             cost_estimate=pl.CostEstimate(flops=n_back * matmul_flops, bytes_accessed=400 << 20, transcendentals=0),
             name='backward',
-        )(cot_out, x1, saved, rows, dgp, slot_of[None, :], gate0, ups, w_up, w_down, w_gate, w_proj, gates, fetched)
+        )(cot_out, x1, saved, rows, dgp, slot_of[None, :], gate0, gates, fetched, ups, w_up, w_down, w_gate, w_proj)
 
         window, sub = 512, 8
 

time: 574 us -> 558 us (0.972)
  Pallas kernels: 557 us -> 537 us
    pallas_call x1, Pallas kernels: 211 us -> 202 us  [device_body(): pl.pallas_call(functools.partial(backward_kernel, (n_back, n_blk, n_dp, n...]
    pallas_call x1, Pallas kernels: 75.8 us -> 68.8 us  [device_body(): pl.pallas_call(functools.partial(first_kernel, (n_dp, n_emb, CAP, n_blk,...]
where the time goes in v4:
time: 558 us; the launch traced here: 556 us
  Pallas kernels  537 us (96%)
  other arithmetic  12.5 us (2%)
    pallas_call x1, Pallas kernels, device_body(): pl.pallas_call(functools.partial(backward_kernel, (n_back, n_blk, n_dp, n...  202 us
    pallas_call x1, Pallas kernels, device_body(): pl.pallas_call(functools.partial(forward_kernel, (n_back, n_blk, cw, nw,...  199 us
    pallas_call x1, Pallas kernels, device_body(): pl.pallas_call(functools.partial(first_kernel, (n_dp, n_emb, CAP, n_blk,...  68.8 us
    pallas_call x2, Pallas kernels, scatter(): pl.pallas_call(functools.partial(scatter_kernel, (first_layer, n, slot_bi...  45.1 us
    pallas_call x1, Pallas kernels, device_body(): pl.pallas_call(functools.partial(gather_kernel, (n_layers, n_emb, CAP, pe...  14.4 us
  transfers between devices with their start and end apart: 1, of which 0 were waited for; matrix products, arithmetic and copies ran while one was open for 1% of the time, Pallas kernels for 4%

profile of v4, /device:TPU:0, one launch (start us, length us, event | category | flops | bytes accessed | tf_op | source)
XLA Modules:
  0.0 556.5 jit_solution(13176896491033560963)
XLA Ops:
  0.7 0.7 add_select_fusion.3
  1.4 0.2 convert_reduce_fusion.1
  1.7 0.7 multiply_add_fusion.1
  2.4 0.9 copy.18.slot_ref
  3.2 7.9 %all_ids.1 = s32[8,4,128]{2,1,0:T(4,128)} custom-call(s32[4,128]{1,0:T(4,128)} %bitcast.35), custom_call_target="tpu_custom_call" | custom-call | tf_op jit(solution)/shard_map/all_ids/pallas_call | solution.py:621
  11.1 0.8 fusion.6
  11.9 0.7 fusion.12
  12.6 0.9 convert_reduce_fusion.2
  13.6 0.6 dynamic_slice.7.counts_ref
  14.2 0.7 convert_reduce_fusion
  14.9 0.9 select_reduce_fusion
  15.9 0.6 copy.23
  16.5 0.2 copy.25
  16.7 0.9 fusion.2.pick_ref
  17.6 14.4 %table_rows.1.served_hbm = bf16[4,1024,256]{2,1,0:T(8,128)(2,1)} custom-call(s32[1024]{0:T(1024)} %bitcast.38, s32[4]{0:T(128)} %dynamic_slice.7.counts_ref, s32[1024,1]{1,0:T(8,128)} %fusion.2.pick_ref, bf16[4,32064,256]{2,1,0:T(8,128)(2,1)} %tables_hbm.1), custom_call_target="tpu_custom_call" | custom-call | tf_op jit(solution)/shard_map/table_rows/pallas_call | solution.py:653
  32.0 68.8 %first_layer.1 = (bf16[512,3072]{1,0:T(8,128)(2,1)}, f32[1,512,256]{2,1,0:T(8,128)}, bf16[4,512,256]{2,1,0:T(8,128)(2,1)}) custom-call(bf16[512,3072]{1,0:T(8,128)(2,1)} %x_hbm.1, s32[512,1]{1,0:T(8,128)} %copy.18.slot_ref, bf16[4,1024,256]{2,1,0:T(8,128)(2,1)} %table_rows.1.served_hbm, bf16[4,3072,256]{2,1,0:T(8,128)(2,1)} %wg_hbm.5, ...), custom_call_target="tpu_custom_call" | custom-call | flops 51539607552 | bytes 104857600 | tf_op jit(solution)/shard_map/first_layer/pallas_call | solution.py:675
  100.9 198.6 %forward.1 = (bf16[512,3072]{1,0:T(8,128)(2,1)}, bf16[2,512,3072]{2,1,0:T(8,128)(2,1)}, f32[3,512,8192]{2,1,0:T(8,128)}, f32[3,512,256]{2,1,0:T(8,128)}, f32[512...) custom-call(bf16[512,3072]{1,0:T(8,128)(2,1)} %get-tuple-element.17.x_hbm.x1_hbm, ...), custom_call_target="tpu_custom_call" | custom-call | flops 154618822656 | bytes 419430400 | tf_op jit(solution)/shard_map/forward/pallas_call | solution.py:693
  299.5 202.3 %backward.1 = (f32[3,2048,256]{2,1,0:T(8,128)}, f32[2048,256]{1,0:T(8,128)}, bf16[2,1024,256]{2,1,0:T(8,128)(2,1)}) custom-call(bf16[512,3072]{1,0:T(8,128)(2,1)} %cot_hbm.3, bf16[512,3072]{1,0:T(8,128)(2,1)} %get-tuple-element.17.x_hbm.x1_hbm, bf16[2,512,3072]{2,1,0:T(8,128)(2,1)} %get-tuple-element.21.saved_hbm, f32[512,256]{1,0:T(8,128)} %get-tuple-element.22.rows_in_ref, ...), custom_call_target="tpu_custom_call" | custom-call | flops 154618822656 | bytes 419430400 | tf_op jit(solution)/shard_map/backward/pallas_call | solution.py:716
  501.8 3.0 all-to-all-start
  504.8 0.8 select_bitcast_fusion
  505.6 5.0 sort.14
  510.6 0.6 concatenate.3.keys_ref
  511.2 23.3 %scatter_1.1.refs_2_ = f32[4,4008,8,256]{3,2,1,0:T(8,128)} custom-call(s32[2176]{0:T(1024)} %concatenate.3.keys_ref, s32[1]{0:T(128)} %bitcast.2.meta_ref, f32[3,2048,256]{2,1,0:T(8,128)} %get-tuple-element.29.refs_0_, f32[4,4008,8,256]{3,2,1,0:T(8,128)} %bitcast.6.refs_1_), custom_call_target="tpu_custom_call", output_to_operand_aliasing={{}: (3, {})} | custom-call | flops 60000002048 | bytes 12582912 | tf_op jit(solution)/shard_map/scatter_1/pallas_call | solution.py:739
  534.6 21.7 %scatter_0.1 = f32[4,4008,8,256]{3,2,1,0:T(8,128)} custom-call(s32[2176]{0:T(1024)} %concatenate.3.keys_ref, s32[1]{0:T(128)} %bitcast.2.meta_ref, f32[2048,256]{1,0:T(8,128)} %get-tuple-element.27.refs_0_, bf16[2048,256]{1,0:T(8,128)(2,1)} %bitcast.5.refs_1_, f32[4,4008,8,256]{3,2,1,0:T(8,128)} %scatter_1.1.refs_2_), custom_call_target="tpu_custom_call", output_to_operand_aliasing={{}: (4, {})} | custom-call | flops 20000000000 | bytes 4194304 | tf_op jit(solution)/shard_map/scatter_0/pallas_call | solution.py:739
  (16 shorter events, 0.2 us)
Async XLA Ops:
  2.4 10.2 %copy-start.1 = (s32[512]{0:T(512)}, s32[512]{0:T(512)S(1)}, u32[]{:S(2)}) copy-start(s32[512]{0:T(512)S(1)} %multiply_add_fusion.1) | copy-start | bytes 6148
  13.5 3.0 copy-start.2
  15.8 0.6 copy-start
  501.8 32.8 %all-to-all-start = ((bf16[8,256,256]{2,1,0:T(8,128)(2,1)}), bf16[8,256,256]{2,1,0:T(8,128)(2,1)}, u32[]{:S(2)}, u32[]{:S(2)}) async-start(bf16[8,256,256]{2,1,0:T(8,128)(2,1)} %bitcast.32), calls=%async_computation | async-start | bytes 2097152 | tf_op jit(solution)/shard_map/all_to_all | solution.py:751

commit v5 on v4

--- a/solution.py
+++ b/solution.py
@@ -92,7 +92,7 @@
     for d in range(n_dest):
         def issue(i, carry, d=d):
             for k in range(8):
-                row_copy(d, d * cap + i * 8 + k).start()
+                row_copy(d, d * cap + i * 8 + k).start(priority=k % 2)
             return carry
 
         lax.fori_loop(0, n_trips[d] * (trip // 8), issue, 0)
@@ -352,8 +352,11 @@
     rest = rows - hi.astype(F32)
     mid = rest.astype(BF)
     low = (rest - mid.astype(F32)).astype(BF)
-    sel = slot_pick(slots_s.shape[0], slot_ref)
-    slots_s[...] = (dot(sel, hi) + dot(sel, mid)) + dot(sel, low)
+    n = slots_s.shape[0] * slots_s.shape[2]
+    sel = slot_pick(n, slot_ref)
+    slots = (dot(sel, hi) + dot(sel, mid)) + dot(sel, low)
+    for h in range(slots_s.shape[1]):
+        slots_s[:, h] = slots[:, h * 128:(h + 1) * 128].reshape(n // 8, 8, 128)
 
 
 def slot_pick(n, slot_ref):
@@ -377,7 +380,7 @@
     weights = weight_copies(wu_hbm, wd_hbm, wu_s, wd_s, w_sem)
 
     def part(ref, emb):
-        return ref.at[pl.ds(pl.multiple_of(emb * cap, cap), cap), :]
+        return ref.at[pl.ds(emb * (cap // 8), cap // 8)]
 
     def sends(ref, there, which, got):
         return [pltpu.make_async_copy(part(ref, my_emb), there, self_sem.at[which])] + [
@@ -501,7 +504,7 @@
 
         @pl.when(i == n_layers - 1)
         def _():
-            slots = dot(slot_pick(slots_s.shape[0], slot_ref), d_mixed).astype(BF)
+            slots = dot(slot_pick(n_emb * cap, slot_ref), d_mixed).astype(BF)
             for d in range(n_dp):
                 slots0_ref[d] = slots
 
@@ -511,88 +514,86 @@
     wait(gate_sends)
 
 
-def scatter_kernel(cfg, keys_ref, meta_ref, *refs):
-    first_layer, n_layers, slot_bits, unroll, window, bulk = cfg
-    if first_layer == 0:
-        gate_ref, mixed_ref, dt_in, dt_out, groups, spots, prod, sems = refs
-        n_rows = mixed_ref.shape[0]
-
-        def product(sl):
-            prod[0, sl, :] = gate_ref[sl, :] * mixed_ref[sl, :].astype(F32)
-
-        row_loop(n_rows, 64, 4)(product)
-        rows_ref = prod
-    else:
-        rows_ref, dt_in, dt_out, groups, spots, sems = refs
+def scatter_kernel(cfg, read_ref, write_ref, group_ref, meta_ref, rows_ref, gate_ref, mixed_ref, dt_in, dt_out, groups, prod, sems):
+    unroll, window, bulk = cfg
+    n_layers = groups.shape[1]
+    n_slots = mixed_ref.shape[0]
     count = meta_ref[0]
-    e_dim = rows_ref.shape[2]
-    sub = 8
-    n_win = (count + (window - 1)) // window
-    lane_row = lax.broadcasted_iota(I32, (sub, e_dim), 0)
-    mask = (1 << slot_bits) - 1
+
+    def product(i, carry):
+        step = 64
+        mixed = mixed_ref[pl.ds(pl.multiple_of(i * step, step), step), :].astype(F32)
+        for h in range(2):
+            at = pl.ds(i * (step // 8), step // 8)
+            prod[at, h] = gate_ref[at, h] * mixed[:, h * 128:(h + 1) * 128].reshape(step // 8, 8, 128)
+        return carry
+
+    lax.fori_loop(0, n_slots // 64, product, 0, unroll=4)
+    words = prod.reshape(n_slots * 2, 128)
+    sub_iota = lax.broadcasted_iota(I32, (8, 128), 0)
 
     def move(buf, spot, group, n):
-        return pltpu.make_async_copy(groups.at[buf, :, pl.ds(spot, n)],
-                                     dt_out.at[pl.ds(first_layer, n_layers), pl.ds(group, n)], sems.at[buf])
-
-    def settle(buf, n):
+        return pltpu.make_async_copy(groups.at[buf, :, pl.ds(spot, n)], dt_out.at[:, pl.ds(group, n)], sems.at[buf])
+
+    def settle(w):
+        n = meta_ref[1 + w]
+
         def drain_bulk(j, carry):
-            move(buf, 0, 0, bulk).wait()
+            move(w % 2, 0, 0, bulk).wait()
             return carry
 
         def drain(j, carry):
-            move(buf, 0, 0, 1).wait()
+            move(w % 2, 0, 0, 1).wait()
             return carry
 
         lax.fori_loop(0, n // bulk, drain_bulk, 0)
         lax.fori_loop(0, lax.rem(n, bulk), drain, 0)
 
-    def run_window(w, carry):
-        buf = lax.rem(w, 2)
-        prev, accs, older, old = carry
-        settle(buf, older)
-        stop = jnp.minimum(count, (w + 1) * window)
-        trips = (stop - w * window + (unroll - 1)) // unroll
-
-        def add(t, carry):
-            prev, n, accs = carry
+    n_win = n_slots // window
+    accs = tuple(jnp.zeros((8, 128), F32) for _ in range(2 * n_layers))
+    for w in range(n_win):
+        buf = w % 2
+        if w >= 2:
+            settle(w - 2)
+        left = jnp.clip(count - w * window, 0, window)
+        trips = (left + (unroll - 1)) // unroll
+
+        def add(t, accs, w=w, buf=buf):
             for k in range(unroll):
-                key = keys_ref[w * window + t * unroll + k]
-                slot = jnp.bitwise_and(key, mask)
-                row = jnp.right_shift(key, slot_bits)
-                group = jnp.right_shift(row, 3)
-                same = group == prev
-                n = n + jnp.where(same, 0, 1)
-                spots[jnp.maximum(n, 0)] = group
-                here = lane_row == jnp.bitwise_and(row, sub - 1)
+                j = w * window + t * unroll + k
+                word = read_ref[j]
+                at = jnp.bitwise_and(word, n_slots * 2 - 1)
+                sub = jnp.bitwise_and(jnp.right_shift(word, 12), 7)
+                same = word < 0
+                here = sub_iota == sub
+                spot = jnp.bitwise_and(write_ref[j], window - 1)
                 new = []
-                for l, acc in enumerate(accs):
-                    row_l = jnp.broadcast_to(rows_ref[l, pl.ds(slot, 1), :], (sub, e_dim))
-                    new.append(jnp.where(same, acc, 0.0) + jnp.where(here, row_l, 0.0))
-                    groups[buf, l, jnp.maximum(n, 0)] = new[l]
+                for l in range(n_layers):
+                    for h in range(2):
+                        src = words if l == 0 else rows_ref.at[l - 1]
+                        row = jnp.broadcast_to(src[pl.ds(at + 8 * h, 1), :], (8, 128))
+                        acc = jnp.where(same, accs[2 * l + h], 0.0) + jnp.where(here, row, 0.0)
+                        groups[buf, l, spot, :, h * 128:(h + 1) * 128] = acc
+                        new.append(acc)
                 accs = tuple(new)
-                prev = group
-            return prev, n, accs
-
-        n0 = jnp.where(jnp.right_shift(keys_ref[w * window], slot_bits + 3) == prev, 0, -1)
-        prev, n, accs = lax.fori_loop(0, trips, add, (prev, n0, accs))
-        follow = jnp.right_shift(keys_ref[(w + 1) * window], slot_bits + 3)
-        padded = trips * unroll > stop - w * window
-        goes_on = jnp.logical_and(stop < count, follow == prev)
-        n_groups = n + 1 - jnp.where(jnp.logical_or(padded, goes_on), 1, 0)
-
-        def put(u, carry):
-            move(buf, u, spots[u], 1).start()
-            return carry
-
-        lax.fori_loop(0, n_groups, put, 0)
-        return prev, accs, old, n_groups
-
-    zero = jnp.int32(0)
-    accs = tuple(jnp.zeros((sub, e_dim), F32) for _ in range(n_layers))
-    _, _, older, old = lax.fori_loop(0, n_win, run_window, (jnp.int32(-1), accs, zero, zero))
-    settle(lax.rem(n_win, 2), older)
-    settle(lax.rem(n_win + 1, 2), old)
+            return accs
+
+        accs = lax.fori_loop(0, trips, add, accs)
+
+        def put(t, carry, w=w, buf=buf):
+            for k in range(unroll):
+                j = w * window + t * unroll + k
+                word = write_ref[j]
+
+                @pl.when(word < 0)
+                def _(j=j, word=word):
+                    move(buf, jnp.bitwise_and(word, window - 1), group_ref[j], 1).start()
+
+            return carry
+
+        lax.fori_loop(0, trips, put, 0)
+    for w in range(max(n_win - 2, 0), n_win):
+        settle(w)
 
 
 def solution(mesh):
@@ -638,8 +639,26 @@
         slot_bits = (n_slots - 1).bit_length()
         slot_ids = jnp.arange(n_slots, dtype=I32).reshape(n_dev, CAP)
         keys = jnp.where(valid, recv_loc * (1 << slot_bits) + slot_ids, big)
-        skeys = jnp.concatenate([lax.sort(keys.reshape(-1)), jnp.full((128,), big, I32)])
-        total = jnp.sum(counts).reshape(1)
+        window, sub = 512, 8
+        skeys = lax.sort(keys.reshape(-1))
+        total = jnp.sum(counts)
+        order = jnp.arange(n_slots, dtype=I32)
+        live = order < total
+        slot = jnp.bitwise_and(skeys, (1 << slot_bits) - 1)
+        row = jnp.right_shift(skeys, slot_bits)
+        group = jnp.right_shift(row, 3)
+        edge = group[1:] != group[:-1]
+        one = jnp.ones((1,), jnp.bool_)
+        fresh = jnp.concatenate([one, edge])
+        last = jnp.concatenate([edge, one]) & live
+        place = jnp.cumsum(fresh.astype(I32)).reshape(-1, window)
+        place = (place - place[:, :1]).reshape(-1)
+        sign = jnp.int32(-(1 << 31))
+        read_word = jnp.right_shift(slot, 3) * 16 + jnp.bitwise_and(slot, 7) + jnp.left_shift(jnp.bitwise_and(row, 7), 12)
+        read_word = read_word + jnp.where(fresh, 0, sign)
+        write_word = place + jnp.where(last, sign, 0)
+        group_word = jnp.where(live, group, 0)
+        meta = jnp.concatenate([total.reshape(1), jnp.sum(last.reshape(-1, window).astype(I32), axis=1)])
 
         my_owner = tok_ids // range_rows
         rank = jnp.sum(((my_owner[None, :] == my_owner[:, None]) & before).astype(I32), axis=-1)
@@ -715,13 +734,13 @@
 
         got, got_gate, slots0 = pl.pallas_call(
             functools.partial(backward_kernel, (n_back, n_blk, n_dp, n_emb, CAP, cw, nw, slab)),
-            out_shape=[jax.ShapeDtypeStruct((n_back, n_slots, e_dim), F32), jax.ShapeDtypeStruct((n_slots, e_dim), F32),
+            out_shape=[jax.ShapeDtypeStruct((n_back, n_slots // 8, e_dim // 128, 8, 128), F32), jax.ShapeDtypeStruct((n_slots // 8, e_dim // 128, 8, 128), F32),
                        jax.ShapeDtypeStruct((n_dp, n_serve, e_dim), BF)],
             in_specs=[hbm, hbm, hbm, vm, vm, vm, vm, vm, vm, hbm, hbm, hbm, hbm, hbm],
             out_specs=[hbm, hbm, vm],
             scratch_shapes=[
                 pltpu.VMEM((tok, dim), BF), pltpu.VMEM((tok, dim), BF), pltpu.VMEM((tok, dim), F32), pltpu.VMEM((tok, fb), BF), pltpu.VMEM((tok, fb), BF),
-                pltpu.VMEM((tok, dim), BF), pltpu.VMEM((n_serve, e_dim), F32), pltpu.VMEM((n_serve, e_dim), F32),
+                pltpu.VMEM((tok, dim), BF), pltpu.VMEM((n_serve // 8, e_dim // 128, 8, 128), F32), pltpu.VMEM((n_serve // 8, e_dim // 128, 8, 128), F32),
                 pltpu.VMEM((tok, e_dim), F32), pltpu.VMEM((tok, e_dim), BF), pltpu.VMEM((2, tok, fb), F32), *w_bufs,
                 dma((4,)), dma((2, 2)), dma((2,)), dma((2, n_dev - 1)), dma((2,)), dma((n_back + 1, n_dev - 1)),
             ],
@@ -730,28 +749,18 @@
             name='backward',
         )(cot_out, x1, saved, rows, dgp, slot_of[None, :], gate0, gates, fetched, ups, w_up, w_down, w_gate, w_proj)
 
-        window, sub = 512, 8
-
-        def scatter(first_layer, n, rows_in, dtab):
-            scratch = [pltpu.VMEM((2, n, window, sub, e_dim), F32), pltpu.SMEM((window,), I32)]
-            if first_layer == 0:
-                scratch.append(pltpu.VMEM((1, n_slots, e_dim), F32))
-            return pl.pallas_call(
-                functools.partial(scatter_kernel, (first_layer, n, slot_bits, 8, window, 32)),
-                out_shape=jax.ShapeDtypeStruct(dtab.shape, F32),
-                in_specs=[sm, sm] + [vm] * len(rows_in) + [hbm],
-                out_specs=hbm,
-                input_output_aliases={2 + len(rows_in): 0},
-                scratch_shapes=scratch + [pltpu.SemaphoreType.DMA((2,))],
-                compiler_params=params(0),
-                cost_estimate=pl.CostEstimate(flops=n * 20_000_000_000, bytes_accessed=n << 22, transcendentals=0),
-                name=f'scatter_{first_layer}',
-            )(skeys, total, *rows_in, dtab)
-
         mixed0 = lax.all_to_all(slots0.reshape(n_dev, CAP, e_dim), MESH_AXES, 0, 0, tiled=True).reshape(n_slots, e_dim)
-        dtab = dtab.reshape(n_layers, range_rows // sub, sub, e_dim)
-        dtab = scatter(1, n_back, (got,), dtab)
-        dtab = scatter(0, 1, (got_gate, mixed0), dtab)
+        dtab = pl.pallas_call(
+            functools.partial(scatter_kernel, (8, window, 32)),
+            out_shape=jax.ShapeDtypeStruct((n_layers, range_rows // sub, sub, e_dim), F32),
+            in_specs=[sm, sm, sm, sm, vm, vm, vm, hbm],
+            out_specs=hbm,
+            input_output_aliases={7: 0},
+            scratch_shapes=[pltpu.VMEM((2, n_layers, window, sub, e_dim), F32), pltpu.VMEM((n_slots // 8, e_dim // 128, 8, 128), F32), dma((2,))],
+            compiler_params=params(0),
+            name='scatter',
+        )(read_word, write_word, group_word, meta, got.reshape(n_back, n_slots * 2, 128), got_gate, mixed0,
+          dtab.reshape(n_layers, range_rows // sub, sub, e_dim))
         dtab = dtab.reshape(n_layers, range_rows, e_dim)
         return out, dtab
 

time: 558 us -> 545 us (0.977); the launches traced: 556 us -> 550 us
  Pallas kernels: 537 us -> 522 us
    pallas_call x2 -> x1, Pallas kernels: 45.1 us -> 26.6 us  [device_body(): pl.pallas_call(functools.partial(scatter_kernel, (8, window, 32)), out_sh...]
  transfers between devices with their start and end apart: 1 -> 1, of which waited for: 0 -> 1; matrix products, arithmetic and copies ran while one was open for 1% -> 2% of each run, Pallas kernels for 4% -> 0%
where the time goes in v5:
time: 545 us; the launch traced here: 550 us
  Pallas kernels  522 us (96%)
  other arithmetic  17.7 us (3%)
    pallas_call x1, Pallas kernels, device_body(): pl.pallas_call(functools.partial(backward_kernel, (n_back, n_blk, n_dp, n...  204 us
    pallas_call x1, Pallas kernels, device_body(): pl.pallas_call(functools.partial(forward_kernel, (n_back, n_blk, cw, nw,...  199 us
    pallas_call x1, Pallas kernels, device_body(): pl.pallas_call(functools.partial(first_kernel, (n_dp, n_emb, CAP, n_blk,...  68.8 us
    pallas_call x1, Pallas kernels, device_body(): pl.pallas_call(functools.partial(scatter_kernel, (8, window, 32)), out_sh...  26.6 us
    pallas_call x1, Pallas kernels, device_body(): pl.pallas_call(functools.partial(gather_kernel, (n_layers, n_emb, CAP, pe...  15.9 us
  transfers between devices with their start and end apart: 1, of which 1 were waited for; matrix products, arithmetic and copies ran while one was open for 2% of the time, Pallas kernels for 0%

profile of v5, /device:TPU:0, one launch (start us, length us, event | category | flops | bytes accessed | tf_op | source)
XLA Modules:
  0.0 550.2 jit_solution(18215305276266294076)
XLA Ops:
  0.7 0.7 add_select_fusion.3
  1.7 0.7 multiply_add_fusion.1
  2.4 7.9 %all_ids.1 = s32[8,4,128]{2,1,0:T(4,128)} custom-call(s32[4,128]{1,0:T(4,128)} %bitcast.55), custom_call_target="tpu_custom_call" | custom-call | tf_op jit(solution)/shard_map/all_ids/pallas_call | solution.py:622
  10.3 0.8 fusion.6
  11.0 0.9 convert_reduce_fusion.2
  12.5 0.7 fusion.18
  13.3 0.9 copy.23.slot_ref
  14.2 0.7 convert_reduce_fusion
  14.9 0.9 select_reduce_fusion
  15.9 0.6 copy.32
  16.7 0.9 fusion.2.pick_ref
  17.6 15.9 %table_rows.1.served_hbm = bf16[4,1024,256]{2,1,0:T(8,128)(2,1)} custom-call(s32[1024]{0:T(1024)} %bitcast.58, s32[4]{0:T(128)} %dynamic_slice.7.counts_ref, s32[1024,1]{1,0:T(8,128)} %fusion.2.pick_ref, bf16[4,32064,256]{2,1,0:T(8,128)(2,1)} %tables_hbm.1), custom_call_target="tpu_custom_call" | custom-call | tf_op jit(solution)/shard_map/table_rows/pallas_call | solution.py:672
  33.4 68.8 %first_layer.1 = (bf16[512,3072]{1,0:T(8,128)(2,1)}, f32[1,512,256]{2,1,0:T(8,128)}, bf16[4,512,256]{2,1,0:T(8,128)(2,1)}) custom-call(bf16[512,3072]{1,0:T(8,128)(2,1)} %x_hbm.1, s32[512,1]{1,0:T(8,128)} %copy.23.slot_ref, bf16[4,1024,256]{2,1,0:T(8,128)(2,1)} %table_rows.1.served_hbm, bf16[4,3072,256]{2,1,0:T(8,128)(2,1)} %wg_hbm.5, ...), custom_call_target="tpu_custom_call" | custom-call | flops 51539607552 | bytes 104857600 | tf_op jit(solution)/shard_map/first_layer/pallas_call | solution.py:694
  102.3 198.6 %forward.1 = (bf16[512,3072]{1,0:T(8,128)(2,1)}, bf16[2,512,3072]{2,1,0:T(8,128)(2,1)}, f32[3,512,8192]{2,1,0:T(8,128)}, f32[3,512,256]{2,1,0:T(8,128)}, f32[512...) custom-call(bf16[512,3072]{1,0:T(8,128)(2,1)} %get-tuple-element.17.x_hbm.x1_hbm, ...), custom_call_target="tpu_custom_call" | custom-call | flops 154618822656 | bytes 419430400 | tf_op jit(solution)/shard_map/forward/pallas_call | solution.py:712
  300.9 204.2 %backward.1 = (f32[3,256,2,8,128]{4,3,2,1,0:T(8,128)}, f32[256,2,8,128]{3,2,1,0:T(8,128)}, bf16[2,1024,256]{2,1,0:T(8,128)(2,1)}) custom-call(bf16[512,3072]{1,0:T(8,128)(2,1)} %cot_hbm.3, bf16[512,3072]{1,0:T(8,128)(2,1)} %get-tuple-element.17.x_hbm.x1_hbm, bf16[2,512,3072]{2,1,0:T(8,128)(2,1)} %get-tuple-element.21.saved_hbm, ...), custom_call_target="tpu_custom_call" | custom-call | flops 154618822656 | bytes 419430400 | tf_op jit(solution)/shard_map/backward/pallas_call | solution.py:735
  505.1 3.0 all-to-all-start
  508.1 0.8 select_bitcast_fusion
  508.9 5.0 sort.14
  513.9 1.3 fusion.11
  516.3 0.8 convert_reduce_fusion.4
  517.1 1.3 pad_add_fusion.2.meta_ref
  518.5 1.4 fusion.10
  519.8 3.6 all-to-all-done
  523.4 26.6 %scatter.1 = f32[4,4008,8,256]{3,2,1,0:T(8,128)} custom-call(s32[2048]{0:T(1024)} %get-tuple-element.44.read_ref, s32[2048]{0:T(1024)} %get-tuple-element.43.write_ref, s32[2048]{0:T(1024)} %get-tuple-element.39.group_ref, s32[5]{0:T(128)} %pad_add_fusion.2.meta_ref, f32[3,4096,128]{2,1,0:T(8,128)} %bitcast.48, ...), custom_call_target="tpu_custom_call", output_to_operand_aliasing={{}: (7, {})} | custom-call | tf_op jit(solution)/shard_map/scatter/pallas_call | solution.py:753
  (35 shorter events, 2.4 us)
Async XLA Ops:
  2.4 12.5 %copy-start.1 = (s32[512]{0:T(512)}, s32[512]{0:T(512)S(1)}, u32[]{:S(2)}) copy-start(s32[512]{0:T(512)S(1)} %multiply_add_fusion.1) | copy-start | bytes 6148
  11.9 1.4 copy-start.2
  15.8 0.6 copy-start
  505.1 18.2 %all-to-all-start = ((bf16[8,256,256]{2,1,0:T(8,128)(2,1)}), bf16[8,256,256]{2,1,0:T(8,128)(2,1)}, u32[]{:S(2)}, u32[]{:S(2)}) async-start(bf16[8,256,256]{2,1,0:T(8,128)(2,1)} %bitcast.49), calls=%async_computation | async-start | bytes 2097152 | tf_op jit(solution)/shard_map/all_to_all | solution.py:752

commit v6 on v5

--- a/solution.py
+++ b/solution.py
@@ -65,38 +65,96 @@
     pl.semaphore_wait(barrier, len(devices))
 
 
-def ids_kernel(cfg, in_ref, out_ref, send_sem, recv_sem):
-    n_dp, n_emb = cfg
+def plan_kernel(cfg, in_ref, ids_ref, recv_ref, counts_ref, pick_ref, slot_row_ref, slot_col_ref, rank_s, send_sem, recv_sem):
+    n_dp, n_emb, cap, range_rows, per_dot = cfg
     n_dev = n_dp * n_emb
-    me = lax.axis_index('dp') * n_emb + lax.axis_index('emb')
+    my_dp, my_emb = lax.axis_index('dp'), lax.axis_index('emb')
+    me = my_dp * n_emb + my_emb
+    n_sub, lanes = in_ref.shape
+    tok = n_sub * lanes
     peers = [peer_of(n_emb, lax.rem(me + k, n_dev)) for k in range(1, n_dev)]
     meet(peers)
-    copies = [remote(in_ref, out_ref.at[me], send_sem.at[k], recv_sem.at[k], peer) for k, peer in enumerate(peers)]
-    for copy in copies:
-        copy.start()
-    out_ref[me] = in_ref[...]
-    for copy in copies:
-        copy.wait()
-
-
-def gather_kernel(cfg, loc_ref, counts_ref, pick_ref, tables_hbm, out_ref, buf, sems):
-    n_layers, n_dest, cap, per_dot, group = cfg
+    copies = [remote(in_ref, ids_ref.at[me], send_sem.at[k], recv_sem.at[k], peer) for k, peer in enumerate(peers)]
+    start(copies)
+    ids_ref[me] = in_ref[...]
+
+    def line(ref):
+        return jnp.concatenate([ref[..., j, :] for j in range(n_sub)], axis=-1)
+
+    def ones(cond):
+        return jnp.where(cond, 1.0, 0.0)
+
+    def digits(x):
+        return jnp.concatenate([jnp.right_shift(x, 8), jnp.bitwise_and(x, 255)], axis=0).astype(F32).astype(BF)
+
+    square = (tok, tok)
+    down, right = lax.broadcasted_iota(I32, square, 0), lax.broadcasted_iota(I32, square, 1)
+    earlier = ones(down < right).astype(BF)
+    own = jnp.broadcast_to(jnp.concatenate([in_ref[j:j + 1, :] for j in range(n_sub)], axis=-1), (8, tok))
+    owner = sum(jnp.where(own >= e * range_rows, 1, 0) for e in range(1, n_emb))
+    is_owner = owner == lax.broadcasted_iota(I32, (8, tok), 0)
+    own_rank = dot(ones(is_owner).astype(BF), earlier).astype(I32)
+    slot_row = jnp.sum(jnp.where(is_owner, own_rank + owner * cap, 0).astype(F32), axis=0, keepdims=True).astype(I32)
+    slot_row_ref[...] = slot_row
+    turned = dot_t(ones(down == right).astype(BF), digits(jnp.broadcast_to(slot_row, (8, tok))))
+    slot_col_ref[...] = (turned[:, 0:1] * 256.0 + turned[:, 8:9]).astype(I32)
+
+    wait(copies)
+    ids8 = line(ids_ref)
+    low = my_emb * range_rows
+    mine = jnp.logical_and(ids8 >= low, ids8 < low + range_rows)
+    mine_f = ones(mine)
+    rank_s[...] = jnp.where(mine, dot(mine_f.astype(BF), earlier), -1.0)
+    counts = jnp.sum(mine_f, axis=1, keepdims=True).astype(I32)
+    counts_ref[...] = jnp.broadcast_to(counts, counts_ref.shape)
+    loc = digits(jnp.where(mine, ids8 - low, 0))
+    c_iota = lax.broadcasted_iota(I32, (cap, tok), 0).astype(F32)
+    dev_iota = lax.broadcasted_iota(I32, (n_dev, cap), 0)
+    recv = jnp.zeros((n_dev, cap), F32)
+    for d in range(n_dev):
+        found = dot_t(loc, ones(rank_s[d:d + 1, :] == c_iota).astype(BF))
+        recv = jnp.where(dev_iota == d, found[:n_dev] * 256.0 + found[n_dev:], recv)
+    slot = dev_iota * cap + lax.broadcasted_iota(I32, (n_dev, cap), 1)
+    recv_ref[...] = jnp.where(slot - dev_iota * cap < counts, recv.astype(I32), slot * 8)
+    lane16 = lax.broadcasted_iota(I32, (cap, 2 * n_dev), 1)
+    row1 = lax.broadcasted_iota(I32, (cap, 1), 0)
+    for e in range(n_emb):
+        d = my_dp * n_emb + e
+        found = dot_t(ones(rank_s[pl.ds(d, 1), :] == c_iota).astype(BF), loc)
+        low8 = jnp.sum(jnp.where(lane16 == n_dev + d, found, 0.0), axis=1, keepdims=True).astype(I32)
+        pick_ref[e * cap:(e + 1) * cap, :] = jnp.bitwise_and(low8, 7) + 8 * jnp.bitwise_and(row1, per_dot - 1)
+
+
+def gather_kernel(cfg, loc_ref, counts_ref, pick_ref, tables_hbm, out_ref, dtab_hbm, buf, zero_s, sems, z_sem):
+    n_layers, n_dest, cap, per_dot, group, z_chunks = cfg
     trip = per_dot * group
-    n_trips = [(counts_ref[d] + (trip - 1)) // trip for d in range(n_dest)]
-
-    def row_copy(d, s):
-        base = pl.multiple_of(jnp.left_shift(jnp.right_shift(loc_ref[s], 3), 3), 8)
-        return pltpu.make_async_copy(
-            tables_hbm.at[:, pl.ds(base, 8), :], buf.at[:, pl.ds(pl.multiple_of(s * 8, 8), 8), :], sems.at[d])
+    z_rows = zero_s.shape[0]
+    first = lax.axis_index('dp') * n_dest
+    n_trips = [(counts_ref[first + d, 0] + (trip - 1)) // trip for d in range(n_dest)]
+
+    def row_copy(d, c):
+        base = pl.multiple_of(jnp.left_shift(jnp.right_shift(loc_ref[first + d, c], 3), 3), 8)
+        at = pl.multiple_of(d * cap * 8 + c * 8, 8)
+        return pltpu.make_async_copy(tables_hbm.at[:, pl.ds(base, 8), :], buf.at[:, pl.ds(at, 8), :], sems.at[d])
+
+    def z_copy(c):
+        return pltpu.make_async_copy(zero_s, dtab_hbm.at[0, pl.ds(pl.multiple_of(c * z_rows, 8), z_rows), :], z_sem)
 
     for d in range(n_dest):
         def issue(i, carry, d=d):
             for k in range(8):
-                row_copy(d, d * cap + i * 8 + k).start(priority=k % 2)
+                row_copy(d, i * 8 + k).start()
             return carry
 
         lax.fori_loop(0, n_trips[d] * (trip // 8), issue, 0)
 
+    clear_rows(zero_s)
+
+    def z_start(c, carry):
+        z_copy(c).start(priority=1)
+        return carry
+
+    lax.fori_loop(0, z_chunks, z_start, 0)
     for d in range(n_dest):
         def drain(i, carry, d=d):
             part = buf.at[:, pl.ds(pl.multiple_of((d * cap + i * trip) * 8, 8), trip * 8), :]
@@ -124,6 +182,16 @@
             return carry
 
         lax.fori_loop(n_trips[d], cap // trip, blank, 0)
+
+    def z_wait(c, carry):
+        z_copy(c).wait()
+        return carry
+
+    lax.fori_loop(0, z_chunks, z_wait, 0)
+
+
+def clear_rows(ref):
+    row_loop(ref.shape[0], 8, 1)(lambda sl: ref.__setitem__((sl, slice(None)), jnp.zeros((8, ref.shape[1]), F32)))
 
 
 def weight_copies(wu_hbm, wd_hbm, wu_s, wd_s, sems):
@@ -236,7 +304,7 @@
     row_loop(tok, slab)(finish)
 
 
-def forward_kernel(cfg, x_hbm, cot_hbm, fet_ref, wg_hbm, wp_hbm, wu_hbm, wd_hbm,
+def forward_kernel(cfg, x_hbm, cot_hbm, fet_ref, wg_hbm, wp_hbm, wu_hbm, wd_hbm, dt_in,
                    out_hbm, saved_hbm, ups_hbm, gate_ref, rows_ref, dgp_ref, dtab_hbm,
                    x_s, u_s, acc_s, h_s, up_s, zero_s, wu_s, wd_s, wg_s, wp_s, in_sem, w_sem, up_sem, out_sem, z_sem):
     n_layers, n_blk, cw, nw, slab, z_per, z_chunks = cfg
@@ -253,7 +321,7 @@
             zl = c // z_chunks
             zc = c - zl * z_chunks
             found.append(pltpu.make_async_copy(
-                zero_s, dtab_hbm.at[zl, pl.ds(pl.multiple_of(zc * z_rows, 8), z_rows), :], z_sem.at[j]))
+                zero_s, dtab_hbm.at[zl + 1, pl.ds(pl.multiple_of(zc * z_rows, 8), z_rows), :], z_sem.at[j]))
         return found
 
     def up_copy(layer, blk, slot):
@@ -270,7 +338,7 @@
     gate_copy(0).start()
     start(weights(1, 0, 0))
     proj_copy(0).start()
-    row_loop(z_rows, 8, 1)(lambda sl: zero_s.__setitem__((sl, slice(None)), jnp.zeros((8, zero_s.shape[1]), F32)))
+    clear_rows(zero_s)
     fetch.wait()
     row_loop(tok, slab)(lambda sl: norm_rows(x_s[sl, :].astype(F32), sl, u_s, acc_s))
 
@@ -295,7 +363,8 @@
             def _():
                 wait(z_copies(step - 1))
 
-            start(z_copies(step))
+            for copy in z_copies(step):
+                copy.start(priority=1)
 
             @pl.when(step > 1)
             def _():
@@ -433,8 +502,8 @@
         def _():
             pltpu.make_async_copy(x1_hbm, x_s, in_sem.at[3]).start()
 
+        gate_copy(i).wait()
         to_slots(rows_s[...], slot_ref, slots_s)
-        gate_copy(i).wait()
         for n in range(dim // nw):
             ns = slice(n * nw, (n + 1) * nw)
             dng_s[:, ns] = dot_t(dgp_s[...], wg_s[ns, :]).astype(BF)
@@ -486,7 +555,7 @@
         def rows_back(sl):
             x = x_s[sl, :].astype(F32)
             scale = lax.rsqrt(jnp.mean(x * x, axis=-1, keepdims=True) + NORM_EPS)
-            d_n = (acc_s[sl, :].astype(BF).astype(F32) + dng_s[sl, :].astype(F32)).astype(BF).astype(F32)
+            d_n = (acc_s[sl, :].astype(BF) + dng_s[sl, :]).astype(F32)
             acc_s[sl, :] = jnp.zeros((slab, dim), F32)
             proj = jnp.mean(d_n * x, axis=-1, keepdims=True)
             d_x = d_n * scale - x * (proj * (scale * scale * scale))
@@ -619,29 +688,25 @@
         my_emb, my_dp = lax.axis_index('emb'), lax.axis_index('dp')
 
         lanes = 128
-        ids8 = pl.pallas_call(
-            functools.partial(ids_kernel, (n_dp, n_emb)),
-            out_shape=jax.ShapeDtypeStruct((n_dev, tok // lanes, lanes), I32),
-            in_specs=[vm], out_specs=vm,
-            scratch_shapes=[pltpu.SemaphoreType.DMA((n_dev - 1,)), pltpu.SemaphoreType.DMA((n_dev - 1,))],
+        per_dot, dots = 32, 2
+        dma = pltpu.SemaphoreType.DMA
+        _, recv_loc, counts, pick, slot_row, slot_col = pl.pallas_call(
+            functools.partial(plan_kernel, (n_dp, n_emb, CAP, range_rows, per_dot)),
+            out_shape=[jax.ShapeDtypeStruct(shape, I32) for shape in (
+                (n_dev, tok // lanes, lanes), (n_dev, CAP), (n_dev, lanes), (n_serve, 1), (1, tok), (tok, 1))],
+            in_specs=[vm], out_specs=[vm] * 6,
+            scratch_shapes=[pltpu.VMEM((n_dev, tok), F32), dma((n_dev - 1,)), dma((n_dev - 1,))],
             compiler_params=pltpu.CompilerParams(collective_id=0, has_side_effects=True),
-            name='all_ids',
-        )(tok_ids.reshape(tok // lanes, lanes)).reshape(n_dev, tok)
-        mine = (ids8 // range_rows) == my_emb
-        t_iota = jnp.arange(tok, dtype=I32)
-        before = t_iota[None, :] < t_iota[:, None]
-        rank8 = jnp.sum((mine[:, None, :] & before[None]).astype(I32), axis=-1)
+            name='plan',
+        )(tok_ids.reshape(tok // lanes, lanes))
         c_iota = jnp.arange(CAP, dtype=I32)
-        hit = mine[:, None, :] & (rank8[:, None, :] == c_iota[None, :, None])
-        recv_loc = jnp.sum(jnp.where(hit, (ids8 - my_emb * range_rows)[:, None, :], 0), axis=-1)
-        counts = jnp.sum(mine.astype(I32), axis=-1)
-        valid = c_iota[None, :] < counts[:, None]
+        valid = c_iota[None, :] < counts[:, :1]
         slot_bits = (n_slots - 1).bit_length()
         slot_ids = jnp.arange(n_slots, dtype=I32).reshape(n_dev, CAP)
         keys = jnp.where(valid, recv_loc * (1 << slot_bits) + slot_ids, big)
         window, sub = 512, 8
         skeys = lax.sort(keys.reshape(-1))
-        total = jnp.sum(counts)
+        total = jnp.sum(counts[:, 0])
         order = jnp.arange(n_slots, dtype=I32)
         live = order < total
         slot = jnp.bitwise_and(skeys, (1 << slot_bits) - 1)
@@ -660,37 +725,26 @@
         group_word = jnp.where(live, group, 0)
         meta = jnp.concatenate([total.reshape(1), jnp.sum(last.reshape(-1, window).astype(I32), axis=1)])
 
-        my_owner = tok_ids // range_rows
-        rank = jnp.sum(((my_owner[None, :] == my_owner[:, None]) & before).astype(I32), axis=-1)
-        slot_of = my_owner * CAP + rank
-
-        spread = jnp.where(valid, recv_loc, lax.rem(slot_ids * 8, range_rows))
-        want = lax.dynamic_slice_in_dim(spread, my_dp * n_emb, n_emb, 0).reshape(-1)
-        n_want = lax.dynamic_slice_in_dim(counts, my_dp * n_emb, n_emb, 0)
-        per_dot, group = 32, 2
-        pick = (jnp.bitwise_and(want, 7) + 8 * (jnp.arange(n_serve, dtype=I32) % per_dot))[:, None]
-        served = pl.pallas_call(
-            functools.partial(gather_kernel, (n_layers, n_emb, CAP, per_dot, group)),
-            out_shape=jax.ShapeDtypeStruct((n_layers, n_serve, e_dim), BF),
+        z_rows = 1336
+        z_chunks = range_rows // z_rows
+        served, dtab = pl.pallas_call(
+            functools.partial(gather_kernel, (n_layers, n_emb, CAP, per_dot, dots, z_chunks)),
+            out_shape=[jax.ShapeDtypeStruct((n_layers, n_serve, e_dim), BF), jax.ShapeDtypeStruct((n_layers, range_rows, e_dim), F32)],
             in_specs=[sm, sm, vm, hbm],
-            out_specs=vm,
-            scratch_shapes=[pltpu.VMEM((n_layers, n_serve * 8, e_dim), BF), pltpu.SemaphoreType.DMA((n_emb,))],
+            out_specs=[vm, hbm],
+            scratch_shapes=[pltpu.VMEM((n_layers, n_serve * 8, e_dim), BF), pltpu.VMEM((z_rows, e_dim), F32), dma((n_emb,)), dma],
             compiler_params=params(0),
             name='table_rows',
-        )(want, n_want, pick, tables)
+        )(recv_loc, counts, pick, tables)
 
         fb = 1024
         n_blk = ffn // fb
         cw, nw, slab = 512, 512, 16
         n_back = n_layers - 1
-        z_rows = 1336
-        z_chunks = range_rows // z_rows
-        z_per = n_layers * z_chunks // (n_back * n_blk)
-        assert z_chunks * z_rows == range_rows and z_per * n_blk * n_back == z_chunks * n_layers
-
+        z_per = z_chunks // n_blk
+        assert z_chunks * z_rows == range_rows and z_per * n_blk == z_chunks
         matmul_flops = 4 * tok * dim * ffn
         w_bufs = [pltpu.VMEM((2, dim, fb), BF), pltpu.VMEM((2, fb, dim), BF), pltpu.VMEM((dim, e_dim), BF), pltpu.VMEM((e_dim, dim), BF)]
-        dma = pltpu.SemaphoreType.DMA
         x1, gate0, fetched = pl.pallas_call(
             functools.partial(first_kernel, (n_dp, n_emb, CAP, n_blk, cw, nw, slab)),
             out_shape=[
@@ -707,7 +761,7 @@
             compiler_params=params(0, collective_id=1, has_side_effects=True),
             cost_estimate=pl.CostEstimate(flops=matmul_flops, bytes_accessed=100 << 20, transcendentals=0),
             name='first_layer',
-        )(resid_in, slot_of[:, None], served, w_gate, w_proj, w_up, w_down)
+        )(resid_in, slot_col, served, w_gate, w_proj, w_up, w_down)
 
         out, saved, ups, gates, rows, dgp, dtab = pl.pallas_call(
             functools.partial(forward_kernel, (n_back, n_blk, cw, nw, slab, z_per, z_chunks)),
@@ -720,8 +774,9 @@
                 jax.ShapeDtypeStruct((tok, e_dim), BF),
                 jax.ShapeDtypeStruct((n_layers, range_rows, e_dim), F32),
             ],
-            in_specs=[hbm, hbm, vm, hbm, hbm, hbm, hbm],
+            in_specs=[hbm, hbm, vm, hbm, hbm, hbm, hbm, hbm],
             out_specs=[hbm, hbm, hbm, vm, vm, vm, hbm],
+            input_output_aliases={7: 6},
             scratch_shapes=[
                 pltpu.VMEM((tok, dim), BF), pltpu.VMEM((tok, dim), BF), pltpu.VMEM((tok, dim), F32), pltpu.VMEM((tok, fb), BF),
                 pltpu.VMEM((2, tok, fb), F32), pltpu.VMEM((z_rows, e_dim), F32), *w_bufs,
@@ -730,7 +785,7 @@
             compiler_params=params(0),
             cost_estimate=pl.CostEstimate(flops=n_back * matmul_flops, bytes_accessed=400 << 20, transcendentals=0),
             name='forward',
-        )(x1, cot_out, fetched, w_gate, w_proj, w_up, w_down)
+        )(x1, cot_out, fetched, w_gate, w_proj, w_up, w_down, dtab)
 
         got, got_gate, slots0 = pl.pallas_call(
             functools.partial(backward_kernel, (n_back, n_blk, n_dp, n_emb, CAP, cw, nw, slab)),
@@ -747,7 +802,7 @@
             compiler_params=params(0, collective_id=2, has_side_effects=True),
             cost_estimate=pl.CostEstimate(flops=n_back * matmul_flops, bytes_accessed=400 << 20, transcendentals=0),
             name='backward',
-        )(cot_out, x1, saved, rows, dgp, slot_of[None, :], gate0, gates, fetched, ups, w_up, w_down, w_gate, w_proj)
+        )(cot_out, x1, saved, rows, dgp, slot_row, gate0, gates, fetched, ups, w_up, w_down, w_gate, w_proj)
 
         mixed0 = lax.all_to_all(slots0.reshape(n_dev, CAP, e_dim), MESH_AXES, 0, 0, tiled=True).reshape(n_slots, e_dim)
         dtab = pl.pallas_call(

time: 545 us -> 530 us (0.972)
  Pallas kernels: 522 us -> 511 us
  other arithmetic: 17.7 us -> 11.9 us
    pallas_call x1, Pallas kernels: 199 us -> 192 us  [device_body(): pl.pallas_call(functools.partial(forward_kernel, (n_back, n_blk, cw, nw,...]
    pallas_call x1, Pallas kernels: 204 us -> 197 us  [device_body(): pl.pallas_call(functools.partial(backward_kernel, (n_back, n_blk, n_dp, n...]
where the time goes in v6:
time: 530 us
  Pallas kernels  511 us (96%)
  other arithmetic  11.9 us (2%)
    pallas_call x1, Pallas kernels, device_body(): pl.pallas_call(functools.partial(backward_kernel, (n_back, n_blk, n_dp, n...  197 us
    pallas_call x1, Pallas kernels, device_body(): pl.pallas_call(functools.partial(forward_kernel, (n_back, n_blk, cw, nw,...  192 us
    pallas_call x1, Pallas kernels, device_body(): pl.pallas_call(functools.partial(first_kernel, (n_dp, n_emb, CAP, n_blk,...  68.8 us
    pallas_call x1, Pallas kernels, device_body(): pl.pallas_call(functools.partial(scatter_kernel, (8, window, 32)), out_sh...  24.1 us
    pallas_call x1, Pallas kernels, device_body(): pl.pallas_call(functools.partial(gather_kernel, (n_layers, n_emb, CAP, pe...  20 us
  transfers between devices with their start and end apart: 1, of which 1 were waited for; matrix products, arithmetic and copies ran while one was open for 2% of the time, Pallas kernels for 0%

profile of v6, /device:TPU:0, one launch (start us, length us, event | category | flops | bytes accessed | tf_op | source)
XLA Modules:
  0.0 530.4 jit_solution(17409396289157146584)
XLA Ops:
  0.6 9.3 %plan.1 = (s32[8,4,128]{2,1,0:T(4,128)}, s32[8,256]{1,0:T(8,128)}, s32[8,128]{1,0:T(8,128)}, s32[1024,1]{1,0:T(8,128)}, s32[1,512]{1,0:T(1,128)}, /*index=5*/s32[512,1]{1,0:T(8,128)}) custom-call(s32[4,128]{1,0:T(4,128)} %bitcast.31), custom_call_target="tpu_custom_call" | custom-call | tf_op jit(solution)/shard_map/plan/pallas_call | solution.py:693
  9.9 20.0 %table_rows.1 = (bf16[4,1024,256]{2,1,0:T(8,128)(2,1)}, f32[4,32064,256]{2,1,0:T(8,128)}) custom-call(s32[8,256]{1,0:T(8,128)} %get-tuple-element.25.loc_ref, s32[8,128]{1,0:T(8,128)} %get-tuple-element.26.counts_ref, s32[1024,1]{1,0:T(8,128)} %get-tuple-element.27.pick_ref, bf16[4,32064,256]{2,1,0:T(8,128)(2,1)} %tables_hbm.1), custom_call_target="tpu_custom_call" | custom-call | tf_op jit(solution)/shard_map/table_rows/pallas_call | solution.py:730
  30.0 68.8 %first_layer.1 = (bf16[512,3072]{1,0:T(8,128)(2,1)}, f32[1,512,256]{2,1,0:T(8,128)}, bf16[4,512,256]{2,1,0:T(8,128)(2,1)}) custom-call(bf16[512,3072]{1,0:T(8,128)(2,1)} %x_hbm.1, s32[512,1]{1,0:T(8,128)} %get-tuple-element.24.slot_ref, bf16[4,1024,256]{2,1,0:T(8,128)(2,1)} %get-tuple-element.28.served_hbm, bf16[4,3072,256]{2,1,0:T(8,128)(2,1)} %wg_hbm.5, ...), custom_call_target="tpu_custom_call" | custom-call | flops 51539607552 | bytes 104857600 | tf_op jit(solution)/shard_map/first_layer/pallas_call | solution.py:748
  98.8 191.6 %forward.1 = (bf16[512,3072]{1,0:T(8,128)(2,1)}, bf16[2,512,3072]{2,1,0:T(8,128)(2,1)}, f32[3,512,8192]{2,1,0:T(8,128)}, f32[3,512,256]{2,1,0:T(8,128)}, f32[512...) custom-call(bf16[512,3072]{1,0:T(8,128)(2,1)} %get-tuple-element.29.x_hbm., ...), custom_call_target="tpu_custom_call", output_to_operand_aliasing={{6}: (7, {})} | custom-call | flops 154618822656 | bytes 419430400 | tf_op jit(solution)/shard_map/forward/pallas_call | solution.py:766
  290.4 197.4 %backward.1 = (f32[3,256,2,8,128]{4,3,2,1,0:T(8,128)}, f32[256,2,8,128]{3,2,1,0:T(8,128)}, bf16[2,1024,256]{2,1,0:T(8,128)(2,1)}) custom-call(bf16[512,3072]{1,0:T(8,128)(2,1)} %cot_hbm.3, bf16[512,3072]{1,0:T(8,128)(2,1)} %get-tuple-element.29.x_hbm.x1_hbm, bf16[2,512,3072]{2,1,0:T(8,128)(2,1)} %get-tuple-element.34.saved_hbm, ...), custom_call_target="tpu_custom_call" | custom-call | flops 154618822656 | bytes 419430400 | tf_op jit(solution)/shard_map/backward/pallas_call | solution.py:790
  487.9 3.0 all-to-all-start
  490.9 1.3 slice_reduce_fusion.1
  492.2 0.8 select_bitcast_fusion
  493.0 5.0 sort.14
  498.0 1.2 fusion.2
  499.2 0.1 slice_compare_fusion
  499.3 0.1 pad_add_fusion.1
  499.3 0.3 reduce-window.9
  499.6 0.1 slice.28
  499.7 0.1 slice_reduce_fusion
  499.9 0.1 reshape.74
  499.9 0.1 copy.18
  500.0 0.1 copy.19
  500.2 0.1 broadcast_bitcast_fusion
  500.3 0.7 convert_reduce_fusion
  500.9 1.2 pad_add_fusion.2.meta_ref
  502.2 1.2 fusion.1
  503.4 2.7 all-to-all-done
  506.1 24.1 %scatter.1 = f32[4,4008,8,256]{3,2,1,0:T(8,128)} custom-call(s32[2048]{0:T(1024)} %get-tuple-element.52.read_ref, s32[2048]{0:T(1024)} %get-tuple-element.51.write_ref, s32[2048]{0:T(1024)} %get-tuple-element.47.group_ref, s32[5]{0:T(128)} %pad_add_fusion.2.meta_ref, f32[3,4096,128]{2,1,0:T(8,128)} %bitcast.25, ...), custom_call_target="tpu_custom_call", output_to_operand_aliasing={{}: (7, {})} | custom-call | tf_op jit(solution)/shard_map/scatter/pallas_call | solution.py:808
  (10 shorter events, 0.2 us)
Async XLA Ops:
  487.9 18.2 %all-to-all-start = ((bf16[8,256,256]{2,1,0:T(8,128)(2,1)}), bf16[8,256,256]{2,1,0:T(8,128)(2,1)}, u32[]{:S(2)}, u32[]{:S(2)}) async-start(bf16[8,256,256]{2,1,0:T(8,128)(2,1)} %bitcast.26), calls=%async_computation | async-start | bytes 2097152 | tf_op jit(solution)/shard_map/all_to_all | solution.py:807

commit v7 on v6

--- a/solution.py
+++ b/solution.py
@@ -138,7 +138,7 @@
         return pltpu.make_async_copy(tables_hbm.at[:, pl.ds(base, 8), :], buf.at[:, pl.ds(at, 8), :], sems.at[d])
 
     def z_copy(c):
-        return pltpu.make_async_copy(zero_s, dtab_hbm.at[0, pl.ds(pl.multiple_of(c * z_rows, 8), z_rows), :], z_sem)
+        return pltpu.make_async_copy(zero_s, dtab_hbm.at[0, pl.ds(c * z_rows, z_rows)], z_sem)
 
     for d in range(n_dest):
         def issue(i, carry, d=d):
@@ -191,7 +191,11 @@
 
 
 def clear_rows(ref):
-    row_loop(ref.shape[0], 8, 1)(lambda sl: ref.__setitem__((sl, slice(None)), jnp.zeros((8, ref.shape[1]), F32)))
+    def clear(i, carry):
+        ref[i] = jnp.zeros(ref.shape[1:], F32)
+        return carry
+
+    lax.fori_loop(0, ref.shape[0], clear, 0)
 
 
 def weight_copies(wu_hbm, wd_hbm, wu_s, wd_s, sems):
@@ -307,21 +311,22 @@
 def forward_kernel(cfg, x_hbm, cot_hbm, fet_ref, wg_hbm, wp_hbm, wu_hbm, wd_hbm, dt_in,
                    out_hbm, saved_hbm, ups_hbm, gate_ref, rows_ref, dgp_ref, dtab_hbm,
                    x_s, u_s, acc_s, h_s, up_s, zero_s, wu_s, wd_s, wg_s, wp_s, in_sem, w_sem, up_sem, out_sem, z_sem):
-    n_layers, n_blk, cw, nw, slab, z_per, z_chunks = cfg
+    n_layers, n_blk, cw, nw, slab, z_per, z_chunks, z_first = cfg
+    z_total = (n_layers + 1) * z_chunks
     tok, dim = x_s.shape
     fb = wu_s.shape[2]
     z_rows = zero_s.shape[0]
     n_steps = n_layers * n_blk
     weights = weight_copies(wu_hbm, wd_hbm, wu_s, wd_s, w_sem)
 
+    z_steps = (z_total - z_first) // z_per
+
     def z_copies(step):
         found = []
         for j in range(z_per):
-            c = step * z_per + j
+            c = z_first + step * z_per + j
             zl = c // z_chunks
-            zc = c - zl * z_chunks
-            found.append(pltpu.make_async_copy(
-                zero_s, dtab_hbm.at[zl + 1, pl.ds(pl.multiple_of(zc * z_rows, 8), z_rows), :], z_sem.at[j]))
+            found.append(pltpu.make_async_copy(zero_s, dtab_hbm.at[zl, pl.ds((c - zl * z_chunks) * z_rows, z_rows)], z_sem.at[j]))
         return found
 
     def up_copy(layer, blk, slot):
@@ -359,12 +364,14 @@
                 nxt = step + 1
                 start(weights(1 + nxt // n_blk, lax.rem(nxt, n_blk), 1 - slot))
 
-            @pl.when(step > 0)
+            @pl.when((step > 0) & (step <= z_steps))
             def _():
                 wait(z_copies(step - 1))
 
-            for copy in z_copies(step):
-                copy.start(priority=1)
+            @pl.when(step < z_steps)
+            def _():
+                for copy in z_copies(step):
+                    copy.start(priority=1)
 
             @pl.when(step > 1)
             def _():
@@ -402,7 +409,8 @@
     put.start()
     get = pltpu.make_async_copy(cot_hbm, u_s, in_sem.at[0])
     get.start()
-    wait(z_copies(n_steps - 1))
+    if z_steps == n_steps:
+        wait(z_copies(n_steps - 1))
     up_copy(0, 0, 0).wait()
     up_copy(0, 0, 1).wait()
     get.wait()
@@ -583,11 +591,16 @@
     wait(gate_sends)
 
 
-def scatter_kernel(cfg, read_ref, write_ref, group_ref, meta_ref, rows_ref, gate_ref, mixed_ref, dt_in, dt_out, groups, prod, sems):
+def scatter_kernel(cfg, read_ref, write_ref, group_ref, meta_ref, rows_hbm, gate_hbm, mixed_hbm, dt_in, dt_out, rows_ref, gate_ref, mixed_ref, groups, prod, spots, sems, in_sem):
     unroll, window, bulk = cfg
     n_layers = groups.shape[1]
     n_slots = mixed_ref.shape[0]
+    n_win = n_slots // window
     count = meta_ref[0]
+    loads = [pltpu.make_async_copy(src, dst, in_sem.at[k]) for k, (src, dst) in enumerate(
+        ((gate_hbm, gate_ref), (mixed_hbm, mixed_ref), (rows_hbm, rows_ref)))]
+    start(loads)
+    wait(loads[:2])
 
     def product(i, carry):
         step = 64
@@ -598,12 +611,24 @@
         return carry
 
     lax.fori_loop(0, n_slots // 64, product, 0, unroll=4)
-    words = prod.reshape(n_slots * 2, 128)
-    sub_iota = lax.broadcasted_iota(I32, (8, 128), 0)
 
     def move(buf, spot, group, n):
         return pltpu.make_async_copy(groups.at[buf, :, pl.ds(spot, n)], dt_out.at[:, pl.ds(group, n)], sems.at[buf])
 
+    def each(n, k, body):
+        def trip(t, carry):
+            for i in range(k):
+                body(t * k + i)
+            return carry
+
+        def one(i, carry):
+            body(i)
+            return carry
+
+        full = n // k
+        lax.fori_loop(0, full, trip, 0)
+        lax.fori_loop(full * k, n, one, 0)
+
     def settle(w):
         n = meta_ref[1 + w]
 
@@ -618,49 +643,47 @@
         lax.fori_loop(0, n // bulk, drain_bulk, 0)
         lax.fori_loop(0, lax.rem(n, bulk), drain, 0)
 
-    n_win = n_slots // window
-    accs = tuple(jnp.zeros((8, 128), F32) for _ in range(2 * n_layers))
+    blank = jnp.zeros(groups.shape[3:], F32)
+    accs = tuple(jnp.zeros((2, 128), F32) for _ in range(n_layers))
     for w in range(n_win):
         buf = w % 2
         if w >= 2:
             settle(w - 2)
         left = jnp.clip(count - w * window, 0, window)
         trips = (left + (unroll - 1)) // unroll
-
-        def add(t, accs, w=w, buf=buf):
+        n_out = meta_ref[1 + w]
+
+        def clear(u, buf=buf):
+            for l in range(n_layers):
+                groups[buf, l, u] = blank
+
+        each(jnp.where(left > 0, jnp.minimum(n_out + 1, window), 0), 4, clear)
+        if w == 0:
+            wait(loads[2:])
+        else:
+            @pl.when(meta_ref[1 + 2 * n_win + w] > 0)
+            def _(w=w, buf=buf):
+                for l in range(n_layers):
+                    groups[buf, l, 0] = groups[1 - buf, l, meta_ref[n_win + w]]
+
+        sums = [groups.at[buf, l].reshape(window * 16, 128) for l in range(n_layers)]
+        rows = [prod.reshape(n_slots * 2, 128)] + [rows_ref.at[l] for l in range(n_layers - 1)]
+
+        def add(t, accs, w=w, sums=sums, rows=rows):
             for k in range(unroll):
                 j = w * window + t * unroll + k
                 word = read_ref[j]
                 at = jnp.bitwise_and(word, n_slots * 2 - 1)
-                sub = jnp.bitwise_and(jnp.right_shift(word, 12), 7)
                 same = word < 0
-                here = sub_iota == sub
-                spot = jnp.bitwise_and(write_ref[j], window - 1)
-                new = []
-                for l in range(n_layers):
-                    for h in range(2):
-                        src = words if l == 0 else rows_ref.at[l - 1]
-                        row = jnp.broadcast_to(src[pl.ds(at + 8 * h, 1), :], (8, 128))
-                        acc = jnp.where(same, accs[2 * l + h], 0.0) + jnp.where(here, row, 0.0)
-                        groups[buf, l, spot, :, h * 128:(h + 1) * 128] = acc
-                        new.append(acc)
-                accs = tuple(new)
+                to = write_ref[j]
+                spots[jnp.right_shift(to, 4)] = group_ref[j]
+                accs = tuple(jnp.where(same, acc, 0.0) + src[pl.ds(at, 2, stride=8), :] for acc, src in zip(accs, rows))
+                for acc, dst in zip(accs, sums):
+                    dst[pl.ds(to, 2, stride=8), :] = acc
             return accs
 
         accs = lax.fori_loop(0, trips, add, accs)
-
-        def put(t, carry, w=w, buf=buf):
-            for k in range(unroll):
-                j = w * window + t * unroll + k
-                word = write_ref[j]
-
-                @pl.when(word < 0)
-                def _(j=j, word=word):
-                    move(buf, jnp.bitwise_and(word, window - 1), group_ref[j], 1).start()
-
-            return carry
-
-        lax.fori_loop(0, trips, put, 0)
+        each(n_out, 4, lambda u, buf=buf: move(buf, u, spots[u], 1).start())
     for w in range(max(n_win - 2, 0), n_win):
         settle(w)
 
@@ -704,35 +727,38 @@
         slot_bits = (n_slots - 1).bit_length()
         slot_ids = jnp.arange(n_slots, dtype=I32).reshape(n_dev, CAP)
         keys = jnp.where(valid, recv_loc * (1 << slot_bits) + slot_ids, big)
-        window, sub = 512, 8
+        window, sub = 256, 8
+        n_win = n_slots // window
         skeys = lax.sort(keys.reshape(-1))
         total = jnp.sum(counts[:, 0])
-        order = jnp.arange(n_slots, dtype=I32)
-        live = order < total
+        live = jnp.arange(n_slots, dtype=I32) < total
         slot = jnp.bitwise_and(skeys, (1 << slot_bits) - 1)
         row = jnp.right_shift(skeys, slot_bits)
         group = jnp.right_shift(row, 3)
+        same_row = jnp.concatenate([jnp.zeros((1,), jnp.bool_), row[1:] == row[:-1]])
         edge = group[1:] != group[:-1]
         one = jnp.ones((1,), jnp.bool_)
         fresh = jnp.concatenate([one, edge])
         last = jnp.concatenate([edge, one]) & live
         place = jnp.cumsum(fresh.astype(I32)).reshape(-1, window)
-        place = (place - place[:, :1]).reshape(-1)
-        sign = jnp.int32(-(1 << 31))
-        read_word = jnp.right_shift(slot, 3) * 16 + jnp.bitwise_and(slot, 7) + jnp.left_shift(jnp.bitwise_and(row, 7), 12)
-        read_word = read_word + jnp.where(fresh, 0, sign)
-        write_word = place + jnp.where(last, sign, 0)
+        place = place - place[:, :1]
+        read_word = jnp.right_shift(slot, 3) * 16 + jnp.bitwise_and(slot, 7) + jnp.where(same_row, jnp.int32(-(1 << 31)), 0)
+        write_word = place.reshape(-1) * 16 + jnp.bitwise_and(row, 7)
         group_word = jnp.where(live, group, 0)
-        meta = jnp.concatenate([total.reshape(1), jnp.sum(last.reshape(-1, window).astype(I32), axis=1)])
-
-        z_rows = 1336
-        z_chunks = range_rows // z_rows
+        goes_on = jnp.logical_not(fresh) & live
+        meta = jnp.concatenate([total.reshape(1), jnp.sum(last.reshape(-1, window).astype(I32), axis=1), place[:, -1],
+                                goes_on.reshape(-1, window)[:, 0].astype(I32)])
+
+        tab_shape = (n_layers, range_rows // 8, e_dim // 128, 8, 128)
+        z_rows = 167
+        z_chunks = tab_shape[1] // z_rows
+        z_first, z_per = z_chunks // 2, 4
         served, dtab = pl.pallas_call(
-            functools.partial(gather_kernel, (n_layers, n_emb, CAP, per_dot, dots, z_chunks)),
-            out_shape=[jax.ShapeDtypeStruct((n_layers, n_serve, e_dim), BF), jax.ShapeDtypeStruct((n_layers, range_rows, e_dim), F32)],
+            functools.partial(gather_kernel, (n_layers, n_emb, CAP, per_dot, dots, z_first)),
+            out_shape=[jax.ShapeDtypeStruct((n_layers, n_serve, e_dim), BF), jax.ShapeDtypeStruct(tab_shape, F32)],
             in_specs=[sm, sm, vm, hbm],
             out_specs=[vm, hbm],
-            scratch_shapes=[pltpu.VMEM((n_layers, n_serve * 8, e_dim), BF), pltpu.VMEM((z_rows, e_dim), F32), dma((n_emb,)), dma],
+            scratch_shapes=[pltpu.VMEM((n_layers, n_serve * 8, e_dim), BF), pltpu.VMEM((z_rows,) + tab_shape[2:], F32), dma((n_emb,)), dma],
             compiler_params=params(0),
             name='table_rows',
         )(recv_loc, counts, pick, tables)
@@ -741,8 +767,7 @@
         n_blk = ffn // fb
         cw, nw, slab = 512, 512, 16
         n_back = n_layers - 1
-        z_per = z_chunks // n_blk
-        assert z_chunks * z_rows == range_rows and z_per * n_blk == z_chunks
+        assert z_chunks * z_rows == tab_shape[1] and (n_layers * z_chunks - z_first) % z_per == 0
         matmul_flops = 4 * tok * dim * ffn
         w_bufs = [pltpu.VMEM((2, dim, fb), BF), pltpu.VMEM((2, fb, dim), BF), pltpu.VMEM((dim, e_dim), BF), pltpu.VMEM((e_dim, dim), BF)]
         x1, gate0, fetched = pl.pallas_call(
@@ -764,7 +789,7 @@
         )(resid_in, slot_col, served, w_gate, w_proj, w_up, w_down)
 
         out, saved, ups, gates, rows, dgp, dtab = pl.pallas_call(
-            functools.partial(forward_kernel, (n_back, n_blk, cw, nw, slab, z_per, z_chunks)),
+            functools.partial(forward_kernel, (n_back, n_blk, cw, nw, slab, z_per, z_chunks, z_first)),
             out_shape=[
                 jax.ShapeDtypeStruct((tok, dim), BF),
                 jax.ShapeDtypeStruct((n_back - 1, tok, dim), BF),
@@ -772,14 +797,14 @@
                 jax.ShapeDtypeStruct((n_back, tok, e_dim), F32),
                 jax.ShapeDtypeStruct((tok, e_dim), F32),
                 jax.ShapeDtypeStruct((tok, e_dim), BF),
-                jax.ShapeDtypeStruct((n_layers, range_rows, e_dim), F32),
+                jax.ShapeDtypeStruct(tab_shape, F32),
             ],
             in_specs=[hbm, hbm, vm, hbm, hbm, hbm, hbm, hbm],
             out_specs=[hbm, hbm, hbm, vm, vm, vm, hbm],
             input_output_aliases={7: 6},
             scratch_shapes=[
                 pltpu.VMEM((tok, dim), BF), pltpu.VMEM((tok, dim), BF), pltpu.VMEM((tok, dim), F32), pltpu.VMEM((tok, fb), BF),
-                pltpu.VMEM((2, tok, fb), F32), pltpu.VMEM((z_rows, e_dim), F32), *w_bufs,
+                pltpu.VMEM((2, tok, fb), F32), pltpu.VMEM((z_rows,) + tab_shape[2:], F32), *w_bufs,
                 dma((3,)), dma((2, 2)), dma((2,)), dma, dma((z_per,)),
             ],
             compiler_params=params(0),
@@ -807,16 +832,17 @@
         mixed0 = lax.all_to_all(slots0.reshape(n_dev, CAP, e_dim), MESH_AXES, 0, 0, tiled=True).reshape(n_slots, e_dim)
         dtab = pl.pallas_call(
             functools.partial(scatter_kernel, (8, window, 32)),
-            out_shape=jax.ShapeDtypeStruct((n_layers, range_rows // sub, sub, e_dim), F32),
-            in_specs=[sm, sm, sm, sm, vm, vm, vm, hbm],
+            out_shape=jax.ShapeDtypeStruct(dtab.shape, F32),
+            in_specs=[sm, sm, sm, sm, hbm, hbm, hbm, hbm],
             out_specs=hbm,
             input_output_aliases={7: 0},
-            scratch_shapes=[pltpu.VMEM((2, n_layers, window, sub, e_dim), F32), pltpu.VMEM((n_slots // 8, e_dim // 128, 8, 128), F32), dma((2,))],
+            scratch_shapes=[pltpu.VMEM((n_back, n_slots * 2, 128), F32), pltpu.VMEM((n_slots // 8,) + tab_shape[2:], F32),
+                            pltpu.VMEM((n_slots, e_dim), BF), pltpu.VMEM((2, n_layers, window, e_dim // 128, sub, 128), F32),
+                            pltpu.VMEM((n_slots // 8, e_dim // 128, 8, 128), F32), pltpu.SMEM((window,), I32), dma((2,)), dma((3,))],
             compiler_params=params(0),
             name='scatter',
-        )(read_word, write_word, group_word, meta, got.reshape(n_back, n_slots * 2, 128), got_gate, mixed0,
-          dtab.reshape(n_layers, range_rows // sub, sub, e_dim))
-        dtab = dtab.reshape(n_layers, range_rows, e_dim)
+        )(read_word, write_word, group_word, meta, got.reshape(n_back, n_slots * 2, 128), got_gate, mixed0, dtab)
+        dtab = dtab.transpose(0, 1, 3, 2, 4).reshape(n_layers, range_rows, e_dim)
         return out, dtab
 
     return jax.shard_map(device_body, mesh=mesh, in_specs=(tok_spec, act_spec, act_spec, table_spec, full_spec, full_spec, full_spec, full_spec), out_specs=(act_spec, table_spec), check_vma=False)

time: 530 us -> 526 us (level)
  Pallas kernels: 511 us -> 503 us
    pallas_call x1, Pallas kernels: 24.1 us -> 15.9 us  [device_body(): pl.pallas_call(functools.partial(scatter_kernel, (8, window, 32)), out_sh...]
    pallas_call x1, Pallas kernels: 20 us -> 13.3 us  [device_body(): pl.pallas_call(functools.partial(gather_kernel, (n_layers, n_emb, CAP, pe...]
    pallas_call x1, Pallas kernels: 192 us -> 198 us  [device_body(): pl.pallas_call(functools.partial(forward_kernel, (n_back, n_blk, cw, nw,...]
  transfers between devices with their start and end apart: 1 -> 1, of which waited for: 1 -> 1; matrix products, arithmetic and copies ran while one was open for 2% -> 3% of each run, Pallas kernels for 0% -> 0%
where the time goes in v7:
time: 526 us; the launch traced here: 523 us
  Pallas kernels  503 us (96%)
  other arithmetic  12.6 us (2%)
    pallas_call x1, Pallas kernels, device_body(): pl.pallas_call(functools.partial(forward_kernel, (n_back, n_blk, cw, nw,...  198 us
    pallas_call x1, Pallas kernels, device_body(): pl.pallas_call(functools.partial(backward_kernel, (n_back, n_blk, n_dp, n...  197 us
    pallas_call x1, Pallas kernels, device_body(): pl.pallas_call(functools.partial(first_kernel, (n_dp, n_emb, CAP, n_blk,...  69.6 us
    pallas_call x1, Pallas kernels, device_body(): pl.pallas_call(functools.partial(scatter_kernel, (8, window, 32)), out_sh...  15.9 us
    pallas_call x1, Pallas kernels, device_body(): pl.pallas_call(functools.partial(gather_kernel, (n_layers, n_emb, CAP, pe...  13.3 us
  transfers between devices with their start and end apart: 1, of which 1 were waited for; matrix products, arithmetic and copies ran while one was open for 3% of the time, Pallas kernels for 0%

profile of v7, /device:TPU:0, one launch (start us, length us, event | category | flops | bytes accessed | tf_op | source)
XLA Modules:
  0.0 522.5 jit_solution(17521497957966995637)
XLA Ops:
  0.6 9.3 %plan.1 = (s32[8,4,128]{2,1,0:T(4,128)}, s32[8,256]{1,0:T(8,128)}, s32[8,128]{1,0:T(8,128)}, s32[1024,1]{1,0:T(8,128)}, s32[1,512]{1,0:T(1,128)}, /*index=5*/s32[512,1]{1,0:T(8,128)}) custom-call(s32[4,128]{1,0:T(4,128)} %bitcast.36), custom_call_target="tpu_custom_call" | custom-call | tf_op jit(solution)/shard_map/plan/pallas_call | solution.py:716
  9.9 13.3 %table_rows.1 = (bf16[4,1024,256]{2,1,0:T(8,128)(2,1)}, f32[4,4008,2,8,128]{4,3,2,1,0:T(8,128)}) custom-call(s32[8,256]{1,0:T(8,128)} %get-tuple-element.25.loc_ref, s32[8,128]{1,0:T(8,128)} %get-tuple-element.26.counts_ref, s32[1024,1]{1,0:T(8,128)} %get-tuple-element.27.pick_ref, bf16[4,32064,256]{2,1,0:T(8,128)(2,1)} %tables_hbm.1), custom_call_target="tpu_custom_call" | custom-call | tf_op jit(solution)/shard_map/table_rows/pallas_call | solution.py:756
  23.2 69.6 %first_layer.1 = (bf16[512,3072]{1,0:T(8,128)(2,1)}, f32[1,512,256]{2,1,0:T(8,128)}, bf16[4,512,256]{2,1,0:T(8,128)(2,1)}) custom-call(bf16[512,3072]{1,0:T(8,128)(2,1)} %x_hbm.1, s32[512,1]{1,0:T(8,128)} %get-tuple-element.24.slot_ref, bf16[4,1024,256]{2,1,0:T(8,128)(2,1)} %get-tuple-element.28.served_hbm, bf16[4,3072,256]{2,1,0:T(8,128)(2,1)} %wg_hbm.5, ...), custom_call_target="tpu_custom_call" | custom-call | flops 51539607552 | bytes 104857600 | tf_op jit(solution)/shard_map/first_layer/pallas_call | solution.py:773
  92.8 198.1 %forward.1 = (bf16[512,3072]{1,0:T(8,128)(2,1)}, bf16[2,512,3072]{2,1,0:T(8,128)(2,1)}, f32[3,512,8192]{2,1,0:T(8,128)}, f32[3,512,256]{2,1,0:T(8,128)}, f32[512...) custom-call(bf16[512,3072]{1,0:T(8,128)(2,1)} %get-tuple-element.29., ...), custom_call_target="tpu_custom_call", output_to_operand_aliasing={{6}: (7, {})} | custom-call | flops 154618822656 | bytes 419430400 | tf_op jit(solution)/shard_map/forward/pallas_call | solution.py:791
  291.0 197.2 %backward.1 = (f32[3,256,2,8,128]{4,3,2,1,0:T(8,128)}, f32[256,2,8,128]{3,2,1,0:T(8,128)}, bf16[2,1024,256]{2,1,0:T(8,128)(2,1)}) custom-call(bf16[512,3072]{1,0:T(8,128)(2,1)} %cot_hbm.3, bf16[512,3072]{1,0:T(8,128)(2,1)} %get-tuple-element.29.x_hbm.x1_hbm, bf16[2,512,3072]{2,1,0:T(8,128)(2,1)} %get-tuple-element.34.saved_hbm, ...), custom_call_target="tpu_custom_call" | custom-call | flops 154618822656 | bytes 419430400 | tf_op jit(solution)/shard_map/backward/pallas_call | solution.py:815
  488.2 3.0 all-to-all-start
  491.2 1.4 slice_reduce_fusion.1
  492.6 0.8 select_bitcast_fusion
  493.4 5.0 sort.14
  498.4 0.1 slice_compare_fusion
  498.5 0.1 pad_add_fusion.1
  498.6 0.3 reduce-window.9
  499.0 0.1 slice_reduce_fusion
  499.1 0.1 reshape.81
  499.2 0.1 copy.17
  499.3 0.1 copy.15
  499.5 0.7 fusion.3
  500.2 0.1 convert_reduce_fusion.1
  500.4 0.8 convert_reduce_fusion
  501.2 1.3 pad_add_fusion.2.meta_ref
  502.5 1.3 fusion.4
  503.9 0.7 select_add_fusion.read_ref
  504.6 1.9 all-to-all-done
  506.5 15.9 %scatter.1 = f32[4,4008,2,8,128]{4,3,2,1,0:T(8,128)} custom-call(s32[2048]{0:T(1024)} %select_add_fusion.read_ref, s32[2048]{0:T(1024)} %get-tuple-element.48.write_ref, s32[2048]{0:T(1024)} %get-tuple-element.47.group_ref, s32[25]{0:T(128)} %pad_add_fusion.2.meta_ref, f32[3,4096,128]{2,1,0:T(8,128)} %bitcast.31, ...), custom_call_target="tpu_custom_call", output_to_operand_aliasing={{}: (7, {})} | custom-call | tf_op jit(solution)/shard_map/scatter/pallas_call | solution.py:833
  (15 shorter events, 0.4 us)
Async XLA Ops:
  488.2 18.2 %all-to-all-start = ((bf16[8,256,256]{2,1,0:T(8,128)(2,1)}), bf16[8,256,256]{2,1,0:T(8,128)(2,1)}, u32[]{:S(2)}, u32[]{:S(2)}) async-start(bf16[8,256,256]{2,1,0:T(8,128)(2,1)} %bitcast.32), calls=%async_computation | async-start | bytes 2097152 | tf_op jit(solution)/shard_map/all_to_all | solution.py:832

commit v8 on v7

--- a/solution.py
+++ b/solution.py
@@ -138,7 +138,7 @@
         return pltpu.make_async_copy(tables_hbm.at[:, pl.ds(base, 8), :], buf.at[:, pl.ds(at, 8), :], sems.at[d])
 
     def z_copy(c):
-        return pltpu.make_async_copy(zero_s, dtab_hbm.at[0, pl.ds(c * z_rows, z_rows)], z_sem)
+        return pltpu.make_async_copy(zero_s, dtab_hbm.at[1, pl.ds(c * z_rows, z_rows)], z_sem)
 
     for d in range(n_dest):
         def issue(i, carry, d=d):
@@ -219,7 +219,7 @@
         copy.wait()
 
 
-def mlp_block(cfg, u_s, h_s, acc_s, wu_ref, wd_ref, up_ref):
+def mlp_block(cfg, u_s, h_s, acc_s, wu_ref, wd_ref, up_ref, second=None):
     cw, nw = cfg
     gw = 128
     n_c = wu_ref.shape[1] // cw
@@ -234,6 +234,8 @@
         up_ref[:, cs] = dot(u_s[...], wu_ref[:, cs])
         if c > 0:
             act(c - 1)
+    if second is not None:
+        second.wait()
     for c in range(n_c):
         cs = slice(c * cw, (c + 1) * cw)
         for n in range(acc_s.shape[1] // nw):
@@ -289,8 +291,9 @@
         def _():
             start(weights(0, f + 1, 1 - slot))
 
-        wait(weights(0, f, slot))
-        mlp_block((cw, nw), u_s, h_s, acc_s, wu_s.at[slot], wd_s.at[slot], up_s)
+        up_w, down_w = weights(0, f, slot)
+        up_w.wait()
+        mlp_block((cw, nw), u_s, h_s, acc_s, wu_s.at[slot], wd_s.at[slot], up_s, down_w)
         return carry
 
     lax.fori_loop(0, n_blk, block, 0)
@@ -311,23 +314,22 @@
 def forward_kernel(cfg, x_hbm, cot_hbm, fet_ref, wg_hbm, wp_hbm, wu_hbm, wd_hbm, dt_in,
                    out_hbm, saved_hbm, ups_hbm, gate_ref, rows_ref, dgp_ref, dtab_hbm,
                    x_s, u_s, acc_s, h_s, up_s, zero_s, wu_s, wd_s, wg_s, wp_s, in_sem, w_sem, up_sem, out_sem, z_sem):
-    n_layers, n_blk, cw, nw, slab, z_per, z_chunks, z_first = cfg
-    z_total = (n_layers + 1) * z_chunks
+    n_layers, n_blk, cw, nw, slab, z_pair, z_chunks, z_first = cfg
     tok, dim = x_s.shape
     fb = wu_s.shape[2]
     z_rows = zero_s.shape[0]
     n_steps = n_layers * n_blk
     weights = weight_copies(wu_hbm, wd_hbm, wu_s, wd_s, w_sem)
 
-    z_steps = (z_total - z_first) // z_per
-
-    def z_copies(step):
+    def z_copies(step, js):
         found = []
-        for j in range(z_per):
-            c = z_first + step * z_per + j
+        for j in js:
+            c = z_first + jnp.right_shift(step, 1) * z_pair + jnp.bitwise_and(step, 1) * (z_pair // 2) + j
             zl = c // z_chunks
-            found.append(pltpu.make_async_copy(zero_s, dtab_hbm.at[zl, pl.ds((c - zl * z_chunks) * z_rows, z_rows)], z_sem.at[j]))
+            found.append(pltpu.make_async_copy(zero_s, dtab_hbm.at[zl + 1, pl.ds((c - zl * z_chunks) * z_rows, z_rows)], z_sem.at[j]))
         return found
+
+    few, more = range(z_pair // 2), range(z_pair // 2, z_pair - z_pair // 2)
 
     def up_copy(layer, blk, slot):
         return pltpu.make_async_copy(up_s.at[slot], ups_hbm.at[layer, :, pl.ds(pl.multiple_of(blk * fb, fb), fb)], up_sem.at[slot])
@@ -364,13 +366,22 @@
                 nxt = step + 1
                 start(weights(1 + nxt // n_blk, lax.rem(nxt, n_blk), 1 - slot))
 
-            @pl.when((step > 0) & (step <= z_steps))
+            odd = jnp.bitwise_and(step, 1) == 1
+
+            @pl.when(step > 0)
             def _():
-                wait(z_copies(step - 1))
-
-            @pl.when(step < z_steps)
+                wait(z_copies(step - 1, few))
+
+            @pl.when((step > 0) & jnp.logical_not(odd))
             def _():
-                for copy in z_copies(step):
+                wait(z_copies(step - 1, more))
+
+            for copy in z_copies(step, few):
+                copy.start(priority=1)
+
+            @pl.when(odd)
+            def _():
+                for copy in z_copies(step, more):
                     copy.start(priority=1)
 
             @pl.when(step > 1)
@@ -409,8 +420,9 @@
     put.start()
     get = pltpu.make_async_copy(cot_hbm, u_s, in_sem.at[0])
     get.start()
-    if z_steps == n_steps:
-        wait(z_copies(n_steps - 1))
+    wait(z_copies(n_steps - 1, few))
+    if n_steps % 2 == 0:
+        wait(z_copies(n_steps - 1, more))
     up_copy(0, 0, 0).wait()
     up_copy(0, 0, 1).wait()
     get.wait()
@@ -591,15 +603,31 @@
     wait(gate_sends)
 
 
-def scatter_kernel(cfg, read_ref, write_ref, group_ref, meta_ref, rows_hbm, gate_hbm, mixed_hbm, dt_in, dt_out, rows_ref, gate_ref, mixed_ref, groups, prod, spots, sems, in_sem):
-    unroll, window, bulk = cfg
-    n_layers = groups.shape[1]
+def scatter_kernel(cfg, read_ref, write_ref, group_ref, meta_ref, rows_hbm, gate_hbm, mixed_hbm, dt_in, dt_out,
+                   rows_ref, gate_ref, mixed_ref, late, groups, prod, zero_s, spots, sems, in_sem, z_sem):
+    unroll, window, bulk, z_chunks = cfg
+    n_back = groups.shape[1]
     n_slots = mixed_ref.shape[0]
     n_win = n_slots // window
+    z_rows = zero_s.shape[0]
     count = meta_ref[0]
     loads = [pltpu.make_async_copy(src, dst, in_sem.at[k]) for k, (src, dst) in enumerate(
         ((gate_hbm, gate_ref), (mixed_hbm, mixed_ref), (rows_hbm, rows_ref)))]
     start(loads)
+    clear_rows(zero_s)
+
+    def z_copy(c):
+        return pltpu.make_async_copy(zero_s, dt_out.at[0, pl.ds(c * z_rows, z_rows)], z_sem)
+
+    def z_start(c, carry):
+        z_copy(c).start(priority=1)
+        return carry
+
+    def z_wait(c, carry):
+        z_copy(c).wait()
+        return carry
+
+    lax.fori_loop(0, z_chunks, z_start, 0)
     wait(loads[:2])
 
     def product(i, carry):
@@ -613,7 +641,10 @@
     lax.fori_loop(0, n_slots // 64, product, 0, unroll=4)
 
     def move(buf, spot, group, n):
-        return pltpu.make_async_copy(groups.at[buf, :, pl.ds(spot, n)], dt_out.at[:, pl.ds(group, n)], sems.at[buf])
+        return pltpu.make_async_copy(groups.at[buf, :, pl.ds(spot, n)], dt_out.at[pl.ds(1, n_back), pl.ds(group, n)], sems.at[buf])
+
+    def move_late(spot, group, n):
+        return pltpu.make_async_copy(late.at[pl.ds(spot, n)], dt_out.at[0, pl.ds(group, n)], sems.at[2])
 
     def each(n, k, body):
         def trip(t, carry):
@@ -629,32 +660,31 @@
         lax.fori_loop(0, full, trip, 0)
         lax.fori_loop(full * k, n, one, 0)
 
-    def settle(w):
-        n = meta_ref[1 + w]
-
+    def settle(n, copies):
         def drain_bulk(j, carry):
-            move(w % 2, 0, 0, bulk).wait()
+            copies(bulk).wait()
             return carry
 
         def drain(j, carry):
-            move(w % 2, 0, 0, 1).wait()
+            copies(1).wait()
             return carry
 
         lax.fori_loop(0, n // bulk, drain_bulk, 0)
         lax.fori_loop(0, lax.rem(n, bulk), drain, 0)
 
     blank = jnp.zeros(groups.shape[3:], F32)
-    accs = tuple(jnp.zeros((2, 128), F32) for _ in range(n_layers))
+    accs = tuple(jnp.zeros((2, 128), F32) for _ in range(1 + n_back))
     for w in range(n_win):
-        buf = w % 2
+        buf, base = w % 2, w * window
         if w >= 2:
-            settle(w - 2)
-        left = jnp.clip(count - w * window, 0, window)
+            settle(meta_ref[w - 1], lambda n, buf=buf: move(buf, 0, 0, n))
+        left = jnp.clip(count - base, 0, window)
         trips = (left + (unroll - 1)) // unroll
         n_out = meta_ref[1 + w]
 
-        def clear(u, buf=buf):
-            for l in range(n_layers):
+        def clear(u, buf=buf, base=base):
+            late[base + u] = blank
+            for l in range(n_back):
                 groups[buf, l, u] = blank
 
         each(jnp.where(left > 0, jnp.minimum(n_out + 1, window), 0), 4, clear)
@@ -662,30 +692,38 @@
             wait(loads[2:])
         else:
             @pl.when(meta_ref[1 + 2 * n_win + w] > 0)
-            def _(w=w, buf=buf):
-                for l in range(n_layers):
-                    groups[buf, l, 0] = groups[1 - buf, l, meta_ref[n_win + w]]
-
-        sums = [groups.at[buf, l].reshape(window * 16, 128) for l in range(n_layers)]
-        rows = [prod.reshape(n_slots * 2, 128)] + [rows_ref.at[l] for l in range(n_layers - 1)]
-
-        def add(t, accs, w=w, sums=sums, rows=rows):
+            def _(w=w, buf=buf, base=base):
+                last = meta_ref[n_win + w]
+                late[base] = late[base - window + last]
+                for l in range(n_back):
+                    groups[buf, l, 0] = groups[1 - buf, l, last]
+
+        sums = [late.at[pl.ds(base, window)].reshape(window * 16, 128)] + [groups.at[buf, l].reshape(window * 16, 128) for l in range(n_back)]
+        rows = [prod.reshape(n_slots * 2, 128)] + [rows_ref.at[l] for l in range(n_back)]
+
+        def add(t, accs, base=base, sums=sums, rows=rows):
             for k in range(unroll):
-                j = w * window + t * unroll + k
+                j = base + t * unroll + k
                 word = read_ref[j]
                 at = jnp.bitwise_and(word, n_slots * 2 - 1)
                 same = word < 0
                 to = write_ref[j]
-                spots[jnp.right_shift(to, 4)] = group_ref[j]
+                spots[base + jnp.right_shift(to, 4)] = group_ref[j]
                 accs = tuple(jnp.where(same, acc, 0.0) + src[pl.ds(at, 2, stride=8), :] for acc, src in zip(accs, rows))
                 for acc, dst in zip(accs, sums):
                     dst[pl.ds(to, 2, stride=8), :] = acc
             return accs
 
         accs = lax.fori_loop(0, trips, add, accs)
-        each(n_out, 4, lambda u, buf=buf: move(buf, u, spots[u], 1).start())
-    for w in range(max(n_win - 2, 0), n_win):
-        settle(w)
+        each(n_out, 4, lambda u, buf=buf, base=base: move(buf, u, spots[base + u], 1).start())
+    lax.fori_loop(0, z_chunks, z_wait, 0)
+    for w in range(n_win):
+        base = w * window
+        each(meta_ref[1 + w], 4, lambda u, base=base: move_late(base + u, spots[base + u], 1).start())
+    for w in range(n_win):
+        if w >= n_win - 2:
+            settle(meta_ref[1 + w], lambda n, w=w: move(w % 2, 0, 0, n))
+        settle(meta_ref[1 + w], lambda n: move_late(0, 0, n))
 
 
 def solution(mesh):
@@ -752,7 +790,7 @@
         tab_shape = (n_layers, range_rows // 8, e_dim // 128, 8, 128)
         z_rows = 167
         z_chunks = tab_shape[1] // z_rows
-        z_first, z_per = z_chunks // 2, 4
+        z_first = z_chunks // 2
         served, dtab = pl.pallas_call(
             functools.partial(gather_kernel, (n_layers, n_emb, CAP, per_dot, dots, z_first)),
             out_shape=[jax.ShapeDtypeStruct((n_layers, n_serve, e_dim), BF), jax.ShapeDtypeStruct(tab_shape, F32)],
@@ -767,7 +805,8 @@
         n_blk = ffn // fb
         cw, nw, slab = 512, 512, 16
         n_back = n_layers - 1
-        assert z_chunks * z_rows == tab_shape[1] and (n_layers * z_chunks - z_first) % z_per == 0
+        z_pair = 2 * (n_back * z_chunks - z_first) // (n_back * n_blk)
+        assert z_chunks * z_rows == tab_shape[1] and z_pair * n_back * n_blk == 2 * (n_back * z_chunks - z_first)
         matmul_flops = 4 * tok * dim * ffn
         w_bufs = [pltpu.VMEM((2, dim, fb), BF), pltpu.VMEM((2, fb, dim), BF), pltpu.VMEM((dim, e_dim), BF), pltpu.VMEM((e_dim, dim), BF)]
         x1, gate0, fetched = pl.pallas_call(
@@ -789,7 +828,7 @@
         )(resid_in, slot_col, served, w_gate, w_proj, w_up, w_down)
 
         out, saved, ups, gates, rows, dgp, dtab = pl.pallas_call(
-            functools.partial(forward_kernel, (n_back, n_blk, cw, nw, slab, z_per, z_chunks, z_first)),
+            functools.partial(forward_kernel, (n_back, n_blk, cw, nw, slab, z_pair, z_chunks, z_first)),
             out_shape=[
                 jax.ShapeDtypeStruct((tok, dim), BF),
                 jax.ShapeDtypeStruct((n_back - 1, tok, dim), BF),
@@ -805,7 +844,7 @@
             scratch_shapes=[
                 pltpu.VMEM((tok, dim), BF), pltpu.VMEM((tok, dim), BF), pltpu.VMEM((tok, dim), F32), pltpu.VMEM((tok, fb), BF),
                 pltpu.VMEM((2, tok, fb), F32), pltpu.VMEM((z_rows,) + tab_shape[2:], F32), *w_bufs,
-                dma((3,)), dma((2, 2)), dma((2,)), dma, dma((z_per,)),
+                dma((3,)), dma((2, 2)), dma((2,)), dma, dma((z_pair - z_pair // 2,)),
             ],
             compiler_params=params(0),
             cost_estimate=pl.CostEstimate(flops=n_back * matmul_flops, bytes_accessed=400 << 20, transcendentals=0),
@@ -831,14 +870,15 @@
 
         mixed0 = lax.all_to_all(slots0.reshape(n_dev, CAP, e_dim), MESH_AXES, 0, 0, tiled=True).reshape(n_slots, e_dim)
         dtab = pl.pallas_call(
-            functools.partial(scatter_kernel, (8, window, 32)),
+            functools.partial(scatter_kernel, (8, window, 32, z_chunks)),
             out_shape=jax.ShapeDtypeStruct(dtab.shape, F32),
             in_specs=[sm, sm, sm, sm, hbm, hbm, hbm, hbm],
             out_specs=hbm,
             input_output_aliases={7: 0},
             scratch_shapes=[pltpu.VMEM((n_back, n_slots * 2, 128), F32), pltpu.VMEM((n_slots // 8,) + tab_shape[2:], F32),
-                            pltpu.VMEM((n_slots, e_dim), BF), pltpu.VMEM((2, n_layers, window, e_dim // 128, sub, 128), F32),
-                            pltpu.VMEM((n_slots // 8, e_dim // 128, 8, 128), F32), pltpu.SMEM((window,), I32), dma((2,)), dma((3,))],
+                            pltpu.VMEM((n_slots, e_dim), BF), pltpu.VMEM((n_slots,) + tab_shape[2:], F32),
+                            pltpu.VMEM((2, n_back, window) + tab_shape[2:], F32), pltpu.VMEM((n_slots // 8,) + tab_shape[2:], F32),
+                            pltpu.VMEM((z_rows,) + tab_shape[2:], F32), pltpu.SMEM((n_slots,), I32), dma((3,)), dma((3,)), dma],
             compiler_params=params(0),
             name='scatter',
         )(read_word, write_word, group_word, meta, got.reshape(n_back, n_slots * 2, 128), got_gate, mixed0, dtab)

time: 526 us -> 529 us (level)
    pallas_call x1, Pallas kernels: 15.9 us -> 25.2 us  [device_body(): pl.pallas_call(functools.partial(scatter_kernel, (8, window, 32, z_chunks...]
    pallas_call x1, Pallas kernels: 198 us -> 191 us  [device_body(): pl.pallas_call(functools.partial(forward_kernel, (n_back, n_blk, cw, nw,...]
where the time goes in v8:
time: 529 us; the launch traced here: 525 us
  Pallas kernels  506 us (96%)
  other arithmetic  12.6 us (2%)
    pallas_call x1, Pallas kernels, device_body(): pl.pallas_call(functools.partial(backward_kernel, (n_back, n_blk, n_dp, n...  197 us
    pallas_call x1, Pallas kernels, device_body(): pl.pallas_call(functools.partial(forward_kernel, (n_back, n_blk, cw, nw,...  191 us
    pallas_call x1, Pallas kernels, device_body(): pl.pallas_call(functools.partial(first_kernel, (n_dp, n_emb, CAP, n_blk,...  69 us
    pallas_call x1, Pallas kernels, device_body(): pl.pallas_call(functools.partial(scatter_kernel, (8, window, 32, z_chunks...  25.2 us
    pallas_call x1, Pallas kernels, device_body(): pl.pallas_call(functools.partial(gather_kernel, (n_layers, n_emb, CAP, pe...  14.2 us
  transfers between devices with their start and end apart: 1, of which 1 were waited for; matrix products, arithmetic and copies ran while one was open for 3% of the time, Pallas kernels for 0%

profile of v8, /device:TPU:0, one launch (start us, length us, event | category | flops | bytes accessed | tf_op | source)
XLA Modules:
  0.0 524.7 jit_solution(4981149530540850508)
XLA Ops:
  0.6 9.3 %plan.1 = (s32[8,4,128]{2,1,0:T(4,128)}, s32[8,256]{1,0:T(8,128)}, s32[8,128]{1,0:T(8,128)}, s32[1024,1]{1,0:T(8,128)}, s32[1,512]{1,0:T(1,128)}, /*index=5*/s32[512,1]{1,0:T(8,128)}) custom-call(s32[4,128]{1,0:T(4,128)} %bitcast.36), custom_call_target="tpu_custom_call" | custom-call | tf_op jit(solution)/shard_map/plan/pallas_call | solution.py:754
  9.9 14.2 %table_rows.1 = (bf16[4,1024,256]{2,1,0:T(8,128)(2,1)}, f32[4,4008,2,8,128]{4,3,2,1,0:T(8,128)}) custom-call(s32[8,256]{1,0:T(8,128)} %get-tuple-element.25.loc_ref, s32[8,128]{1,0:T(8,128)} %get-tuple-element.26.counts_ref, s32[1024,1]{1,0:T(8,128)} %get-tuple-element.27.pick_ref, bf16[4,32064,256]{2,1,0:T(8,128)(2,1)} %tables_hbm.1), custom_call_target="tpu_custom_call" | custom-call | tf_op jit(solution)/shard_map/table_rows/pallas_call | solution.py:794
  24.2 69.0 %first_layer.1 = (bf16[512,3072]{1,0:T(8,128)(2,1)}, f32[1,512,256]{2,1,0:T(8,128)}, bf16[4,512,256]{2,1,0:T(8,128)(2,1)}) custom-call(bf16[512,3072]{1,0:T(8,128)(2,1)} %x_hbm.1, s32[512,1]{1,0:T(8,128)} %get-tuple-element.24.slot_ref, bf16[4,1024,256]{2,1,0:T(8,128)(2,1)} %get-tuple-element.28.served_hbm, bf16[4,3072,256]{2,1,0:T(8,128)(2,1)} %wg_hbm.5, ...), custom_call_target="tpu_custom_call" | custom-call | flops 51539607552 | bytes 104857600 | tf_op jit(solution)/shard_map/first_layer/pallas_call | solution.py:812
  93.2 190.6 %forward.1 = (bf16[512,3072]{1,0:T(8,128)(2,1)}, bf16[2,512,3072]{2,1,0:T(8,128)(2,1)}, f32[3,512,8192]{2,1,0:T(8,128)}, f32[3,512,256]{2,1,0:T(8,128)}, f32[512...) custom-call(bf16[512,3072]{1,0:T(8,128)(2,1)} %get-tuple-element.29., ...), custom_call_target="tpu_custom_call", output_to_operand_aliasing={{6}: (7, {})} | custom-call | flops 154618822656 | bytes 419430400 | tf_op jit(solution)/shard_map/forward/pallas_call | solution.py:830
  283.8 197.3 %backward.1 = (f32[3,256,2,8,128]{4,3,2,1,0:T(8,128)}, f32[256,2,8,128]{3,2,1,0:T(8,128)}, bf16[2,1024,256]{2,1,0:T(8,128)(2,1)}) custom-call(bf16[512,3072]{1,0:T(8,128)(2,1)} %cot_hbm.3, bf16[512,3072]{1,0:T(8,128)(2,1)} %get-tuple-element.29.x_hbm.x1_hbm, bf16[2,512,3072]{2,1,0:T(8,128)(2,1)} %get-tuple-element.34.saved_hbm, ...), custom_call_target="tpu_custom_call" | custom-call | flops 154618822656 | bytes 419430400 | tf_op jit(solution)/shard_map/backward/pallas_call | solution.py:854
  481.1 3.0 all-to-all-start
  484.1 1.4 slice_reduce_fusion.1
  485.5 0.8 select_bitcast_fusion
  486.3 5.0 sort.14
  491.3 0.1 slice_compare_fusion
  491.4 0.1 pad_add_fusion.1
  491.5 0.3 reduce-window.9
  491.9 0.1 slice_reduce_fusion
  492.0 0.1 reshape.81
  492.0 0.1 copy.17
  492.1 0.1 copy.15
  492.4 0.7 fusion.3
  493.1 0.1 convert_reduce_fusion.1
  493.2 0.8 convert_reduce_fusion
  494.1 1.3 pad_add_fusion.2.meta_ref
  495.4 1.3 fusion.4
  496.8 0.7 select_add_fusion.read_ref
  497.4 1.9 all-to-all-done
  499.3 25.2 %scatter.1 = f32[4,4008,2,8,128]{4,3,2,1,0:T(8,128)} custom-call(s32[2048]{0:T(1024)} %select_add_fusion.read_ref, s32[2048]{0:T(1024)} %get-tuple-element.48.write_ref, s32[2048]{0:T(1024)} %get-tuple-element.47.group_ref, s32[25]{0:T(128)} %pad_add_fusion.2.meta_ref, f32[3,4096,128]{2,1,0:T(8,128)} %bitcast.31, ...), custom_call_target="tpu_custom_call", output_to_operand_aliasing={{}: (7, {})} | custom-call | tf_op jit(solution)/shard_map/scatter/pallas_call | solution.py:872
  (15 shorter events, 0.4 us)
Async XLA Ops:
  481.1 18.2 %all-to-all-start = ((bf16[8,256,256]{2,1,0:T(8,128)(2,1)}), bf16[8,256,256]{2,1,0:T(8,128)(2,1)}, u32[]{:S(2)}, u32[]{:S(2)}) async-start(bf16[8,256,256]{2,1,0:T(8,128)(2,1)} %bitcast.32), calls=%async_computation | async-start | bytes 2097152 | tf_op jit(solution)/shard_map/all_to_all | solution.py:871

commit v9 on v8

--- a/solution.py
+++ b/solution.py
@@ -125,8 +125,9 @@
         pick_ref[e * cap:(e + 1) * cap, :] = jnp.bitwise_and(low8, 7) + 8 * jnp.bitwise_and(row1, per_dot - 1)
 
 
-def gather_kernel(cfg, loc_ref, counts_ref, pick_ref, tables_hbm, out_ref, dtab_hbm, buf, zero_s, sems, z_sem):
-    n_layers, n_dest, cap, per_dot, group, z_chunks = cfg
+def gather_kernel(cfg, loc_ref, counts_ref, recv_ref, tally_ref, pick_ref, tables_hbm,
+                  out_ref, dtab_hbm, read_ref, write_ref, group_ref, meta_ref, buf, zero_s, sems, z_sem):
+    n_layers, n_dest, cap, per_dot, group, z_chunks, slot_bits = cfg
     trip = per_dot * group
     z_rows = zero_s.shape[0]
     first = lax.axis_index('dp') * n_dest
@@ -155,6 +156,7 @@
         return carry
 
     lax.fori_loop(0, z_chunks, z_start, 0)
+    order_rows(recv_ref, tally_ref, slot_bits, read_ref, write_ref, group_ref, meta_ref)
     for d in range(n_dest):
         def drain(i, carry, d=d):
             part = buf.at[:, pl.ds(pl.multiple_of((d * cap + i * trip) * 8, 8), trip * 8), :]
@@ -454,8 +456,8 @@
 
 def backward_kernel(cfg, cot_hbm, x1_hbm, saved_hbm, rows_in_ref, dgp_in_ref, slot_ref, gate0_ref, gate_ref, fet_ref,
                     ups_hbm, wu_hbm, wd_hbm, wg_hbm, wp_hbm,
-                    got_hbm, gate_hbm, slots0_ref,
-                    cot_s, x_s, acc_s, dup_s, dh_s, dng_s, slots_s, gslots_s, rows_s, dgp_s, up_s, wu_s, wd_s, wg_s, wp_s,
+                    got_hbm, gate_hbm, mixed_hbm,
+                    cot_s, x_s, acc_s, dup_s, dh_s, dng_s, slots_s, gslots_s, dslots_s, rows_s, dgp_s, up_s, wu_s, wd_s, wg_s, wp_s,
                     in_sem, w_sem, up_sem, send_sem, self_sem, recv_sem):
     n_layers, n_blk, n_dp, n_emb, cap, cw, nw, slab = cfg
     tok, dim = cot_s.shape
@@ -479,6 +481,13 @@
         return sends(slots_s, part(got_hbm.at[n_layers - 1 - i], me), 0, i)
 
     gate_sends = sends(gslots_s, part(gate_hbm, me), 1, n_layers)
+
+    def flat(ref, dev):
+        return ref.at[pl.ds(pl.multiple_of(dev * cap, cap), cap), :]
+
+    mixed_sends = [pltpu.make_async_copy(flat(dslots_s, my_emb), flat(mixed_hbm, me), self_sem.at[2])] + [
+        remote(flat(dslots_s, peer['emb']), flat(mixed_hbm, me), send_sem.at[2, k], recv_sem.at[n_layers + 1, k], peer)
+        for k, peer in enumerate(peers)]
 
     def up_copy(step, slot):
         i = step // n_blk
@@ -584,6 +593,11 @@
         row_loop(tok, slab)(rows_back)
         proj_copy(i).wait()
         d_mixed = dot_t(cot_s[...], wp_s[...]).astype(BF)
+
+        @pl.when(i == n_layers - 1)
+        def _():
+            dslots_s[...] = dot(slot_pick(n_emb * cap, slot_ref), d_mixed).astype(BF)
+
         wait(row_sends(i))
 
         @pl.when(i < n_layers - 1)
@@ -591,36 +605,88 @@
             proj_copy(i + 1).start()
             gate_grads(gate_ref[jnp.maximum(n_layers - 2 - i, 0)], fet_ref[n_layers - 1 - i], d_mixed.astype(F32), rows_s, dgp_s)
 
-        @pl.when(i == n_layers - 1)
-        def _():
-            slots = dot(slot_pick(n_emb * cap, slot_ref), d_mixed).astype(BF)
-            for d in range(n_dp):
-                slots0_ref[d] = slots
-
         return carry
 
     lax.fori_loop(0, n_layers, one_layer, 0)
+    start(mixed_sends)
     wait(gate_sends)
+    wait(mixed_sends)
+
+
+def order_rows(recv_ref, counts_ref, slot_bits, read_ref, write_ref, group_ref, meta_ref):
+    n_dev, cap = recv_ref.shape
+    shape = (n_dev, cap)
+    square = (cap, cap)
+    dev, lane = lax.broadcasted_iota(I32, shape, 0), lax.broadcasted_iota(I32, shape, 1)
+    down, right = lax.broadcasted_iota(I32, square, 0), lax.broadcasted_iota(I32, square, 1)
+    counts = counts_ref[:, 0:1]
+    key = jnp.where(lane < counts, jnp.left_shift(recv_ref[...], slot_bits), 1 << 30) + dev * cap + lane
+
+    def ones(cond):
+        return jnp.where(cond, 1.0, 0.0)
+
+    def digit(k):
+        return jnp.bitwise_and(jnp.right_shift(key, 8 * k), 255).astype(F32).astype(BF)
+
+    digits = [digit(k) for k in range(4)]
+    same = ones(down == right).astype(BF)
+    turned = sum(jnp.left_shift(dot_t(same, d).astype(I32), 8 * k) for k, d in enumerate(digits))
+    rows = jnp.concatenate([d[None] for d in digits], axis=0)
+    found = [jnp.zeros((8, cap), F32) for _ in range(n_dev)]
+    for d in range(n_dev):
+        column = turned[:, d:d + 1]
+        smaller = sum(ones(key[e:e + 1, :] < column) for e in range(n_dev))
+        rank = jnp.sum(smaller, axis=1, keepdims=True)
+        mine = jnp.concatenate([rows[k, d:d + 1, :] for k in range(4)] * 2, axis=0)
+        for w in range(n_dev):
+            found[w] = found[w] + dot(mine, ones(rank - (w * cap) == right.astype(F32)).astype(BF))
+    merged = [sum(jnp.left_shift(f[k:k + 1].astype(I32), 8 * k) for k in range(4)) for f in found]
+    ordered = jnp.concatenate(merged, axis=0)
+
+    before = pltpu.roll(ordered, 1, 1)
+    before = jnp.where(lane == 0, pltpu.roll(before, 1, 0), before)
+    after = pltpu.roll(ordered, cap - 1, 1)
+    after = jnp.where(lane == cap - 1, pltpu.roll(after, n_dev - 1, 0), after)
+    total = jnp.sum(counts_ref[...].astype(F32), axis=0, keepdims=True).astype(I32)
+    place_in = dev * cap + lane
+    live = place_in < total[:, 0:1]
+    slot = jnp.bitwise_and(ordered, (1 << slot_bits) - 1)
+    row = jnp.right_shift(ordered, slot_bits)
+    group = jnp.right_shift(ordered, slot_bits + 3)
+    begin, end = place_in == 0, place_in == n_dev * cap - 1
+    same_row = jnp.logical_and(row == jnp.right_shift(before, slot_bits), jnp.logical_not(begin))
+    fresh = jnp.logical_or(group != jnp.right_shift(before, slot_bits + 3), begin)
+    last = jnp.logical_and(jnp.logical_or(group != jnp.right_shift(after, slot_bits + 3), end), live)
+    place = dot(ones(fresh).astype(BF), ones(down <= right).astype(BF)).astype(I32)
+    place = place - place[:, 0:1]
+    read_ref[...] = jnp.right_shift(slot, 3) * 16 + jnp.bitwise_and(slot, 7) + jnp.where(same_row, -(1 << 31), 0)
+    write_ref[...] = place * 16 + jnp.bitwise_and(row, 7)
+    group_ref[...] = jnp.where(live, group, 0)
+    n_out = jnp.sum(ones(last), axis=1, keepdims=True).astype(I32)
+    goes_on = jnp.where(jnp.logical_and(jnp.logical_not(fresh), live), 1, 0)[:, 0:1]
+    meta_lane = lax.broadcasted_iota(I32, meta_ref.shape, 1)
+    meta = jnp.where(meta_lane == 0, n_out, jnp.where(meta_lane == 1, place[:, cap - 1:cap], goes_on))
+    meta_ref[...] = jnp.where(meta_lane == 3, total, meta)
 
 
 def scatter_kernel(cfg, read_ref, write_ref, group_ref, meta_ref, rows_hbm, gate_hbm, mixed_hbm, dt_in, dt_out,
-                   rows_ref, gate_ref, mixed_ref, late, groups, prod, zero_s, spots, sems, in_sem, z_sem):
-    unroll, window, bulk, z_chunks = cfg
-    n_back = groups.shape[1]
+                   rows_ref, gate_ref, mixed_ref, groups, prod, zero_s, spots, sems, in_sem, z_sem):
+    unroll, bulk, z_chunks = cfg
+    n_layers, window = groups.shape[1:3]
     n_slots = mixed_ref.shape[0]
     n_win = n_slots // window
     z_rows = zero_s.shape[0]
-    count = meta_ref[0]
+    count = meta_ref[0, 3]
     loads = [pltpu.make_async_copy(src, dst, in_sem.at[k]) for k, (src, dst) in enumerate(
         ((gate_hbm, gate_ref), (mixed_hbm, mixed_ref), (rows_hbm, rows_ref)))]
     start(loads)
     clear_rows(zero_s)
 
     def z_copy(c):
-        return pltpu.make_async_copy(zero_s, dt_out.at[0, pl.ds(c * z_rows, z_rows)], z_sem)
+        return pltpu.make_async_copy(zero_s, dt_out.at[0, pl.ds(c * z_rows, z_rows)], z_sem.at[c])
 
     def z_start(c, carry):
-        z_copy(c).start(priority=1)
+        z_copy(c).start()
         return carry
 
     def z_wait(c, carry):
@@ -641,10 +707,7 @@
     lax.fori_loop(0, n_slots // 64, product, 0, unroll=4)
 
     def move(buf, spot, group, n):
-        return pltpu.make_async_copy(groups.at[buf, :, pl.ds(spot, n)], dt_out.at[pl.ds(1, n_back), pl.ds(group, n)], sems.at[buf])
-
-    def move_late(spot, group, n):
-        return pltpu.make_async_copy(late.at[pl.ds(spot, n)], dt_out.at[0, pl.ds(group, n)], sems.at[2])
+        return pltpu.make_async_copy(groups.at[buf, :, pl.ds(spot, n)], dt_out.at[:, pl.ds(group, n)], sems.at[buf])
 
     def each(n, k, body):
         def trip(t, carry):
@@ -660,70 +723,69 @@
         lax.fori_loop(0, full, trip, 0)
         lax.fori_loop(full * k, n, one, 0)
 
-    def settle(n, copies):
+    def settle(w):
+        n = meta_ref[w, 0]
+
         def drain_bulk(j, carry):
-            copies(bulk).wait()
+            move(w % 2, 0, 0, bulk).wait()
             return carry
 
         def drain(j, carry):
-            copies(1).wait()
+            move(w % 2, 0, 0, 1).wait()
             return carry
 
         lax.fori_loop(0, n // bulk, drain_bulk, 0)
         lax.fori_loop(0, lax.rem(n, bulk), drain, 0)
 
     blank = jnp.zeros(groups.shape[3:], F32)
-    accs = tuple(jnp.zeros((2, 128), F32) for _ in range(1 + n_back))
+    accs = tuple(jnp.zeros((2, 128), F32) for _ in range(n_layers))
+    z_done = jnp.int32(0)
     for w in range(n_win):
-        buf, base = w % 2, w * window
+        buf = w % 2
         if w >= 2:
-            settle(meta_ref[w - 1], lambda n, buf=buf: move(buf, 0, 0, n))
-        left = jnp.clip(count - base, 0, window)
+            settle(w - 2)
+        left = jnp.clip(count - w * window, 0, window)
         trips = (left + (unroll - 1)) // unroll
-        n_out = meta_ref[1 + w]
-
-        def clear(u, buf=buf, base=base):
-            late[base + u] = blank
-            for l in range(n_back):
+        n_out = meta_ref[w, 0]
+
+        def clear(u, buf=buf):
+            for l in range(n_layers):
                 groups[buf, l, u] = blank
 
         each(jnp.where(left > 0, jnp.minimum(n_out + 1, window), 0), 4, clear)
         if w == 0:
             wait(loads[2:])
         else:
-            @pl.when(meta_ref[1 + 2 * n_win + w] > 0)
-            def _(w=w, buf=buf, base=base):
-                last = meta_ref[n_win + w]
-                late[base] = late[base - window + last]
-                for l in range(n_back):
-                    groups[buf, l, 0] = groups[1 - buf, l, last]
-
-        sums = [late.at[pl.ds(base, window)].reshape(window * 16, 128)] + [groups.at[buf, l].reshape(window * 16, 128) for l in range(n_back)]
-        rows = [prod.reshape(n_slots * 2, 128)] + [rows_ref.at[l] for l in range(n_back)]
-
-        def add(t, accs, base=base, sums=sums, rows=rows):
+            @pl.when(meta_ref[w, 2] > 0)
+            def _(w=w, buf=buf):
+                for l in range(n_layers):
+                    groups[buf, l, 0] = groups[1 - buf, l, meta_ref[w - 1, 1]]
+
+        sums = [groups.at[buf, l].reshape(window * 16, 128) for l in range(n_layers)]
+        rows = [prod.reshape(n_slots * 2, 128)] + [rows_ref.at[l] for l in range(n_layers - 1)]
+
+        def add(t, accs, w=w, sums=sums, rows=rows):
             for k in range(unroll):
-                j = base + t * unroll + k
-                word = read_ref[j]
+                j = t * unroll + k
+                word = read_ref[w, j]
                 at = jnp.bitwise_and(word, n_slots * 2 - 1)
                 same = word < 0
-                to = write_ref[j]
-                spots[base + jnp.right_shift(to, 4)] = group_ref[j]
+                to = write_ref[w, j]
+                spots[jnp.right_shift(to, 4)] = group_ref[w, j]
                 accs = tuple(jnp.where(same, acc, 0.0) + src[pl.ds(at, 2, stride=8), :] for acc, src in zip(accs, rows))
                 for acc, dst in zip(accs, sums):
                     dst[pl.ds(to, 2, stride=8), :] = acc
             return accs
 
         accs = lax.fori_loop(0, trips, add, accs)
-        each(n_out, 4, lambda u, buf=buf, base=base: move(buf, u, spots[base + u], 1).start())
-    lax.fori_loop(0, z_chunks, z_wait, 0)
-    for w in range(n_win):
-        base = w * window
-        each(meta_ref[1 + w], 4, lambda u, base=base: move_late(base + u, spots[base + u], 1).start())
-    for w in range(n_win):
-        if w >= n_win - 2:
-            settle(meta_ref[1 + w], lambda n, w=w: move(w % 2, 0, 0, n))
-        settle(meta_ref[1 + w], lambda n: move_late(0, 0, n))
+        need = jnp.where(n_out > 0, spots[jnp.maximum(n_out - 1, 0)] // z_rows + 1, z_done)
+        need = jnp.maximum(need, z_done)
+        lax.fori_loop(z_done, need, z_wait, 0)
+        z_done = need
+        each(n_out, 4, lambda u, buf=buf: move(buf, u, spots[u], 1).start())
+    lax.fori_loop(z_done, z_chunks, z_wait, 0)
+    for w in range(max(n_win - 2, 0), n_win):
+        settle(w)
 
 
 def solution(mesh):
@@ -760,46 +822,21 @@
             compiler_params=pltpu.CompilerParams(collective_id=0, has_side_effects=True),
             name='plan',
         )(tok_ids.reshape(tok // lanes, lanes))
-        c_iota = jnp.arange(CAP, dtype=I32)
-        valid = c_iota[None, :] < counts[:, :1]
         slot_bits = (n_slots - 1).bit_length()
-        slot_ids = jnp.arange(n_slots, dtype=I32).reshape(n_dev, CAP)
-        keys = jnp.where(valid, recv_loc * (1 << slot_bits) + slot_ids, big)
-        window, sub = 256, 8
-        n_win = n_slots // window
-        skeys = lax.sort(keys.reshape(-1))
-        total = jnp.sum(counts[:, 0])
-        live = jnp.arange(n_slots, dtype=I32) < total
-        slot = jnp.bitwise_and(skeys, (1 << slot_bits) - 1)
-        row = jnp.right_shift(skeys, slot_bits)
-        group = jnp.right_shift(row, 3)
-        same_row = jnp.concatenate([jnp.zeros((1,), jnp.bool_), row[1:] == row[:-1]])
-        edge = group[1:] != group[:-1]
-        one = jnp.ones((1,), jnp.bool_)
-        fresh = jnp.concatenate([one, edge])
-        last = jnp.concatenate([edge, one]) & live
-        place = jnp.cumsum(fresh.astype(I32)).reshape(-1, window)
-        place = place - place[:, :1]
-        read_word = jnp.right_shift(slot, 3) * 16 + jnp.bitwise_and(slot, 7) + jnp.where(same_row, jnp.int32(-(1 << 31)), 0)
-        write_word = place.reshape(-1) * 16 + jnp.bitwise_and(row, 7)
-        group_word = jnp.where(live, group, 0)
-        goes_on = jnp.logical_not(fresh) & live
-        meta = jnp.concatenate([total.reshape(1), jnp.sum(last.reshape(-1, window).astype(I32), axis=1), place[:, -1],
-                                goes_on.reshape(-1, window)[:, 0].astype(I32)])
-
         tab_shape = (n_layers, range_rows // 8, e_dim // 128, 8, 128)
         z_rows = 167
         z_chunks = tab_shape[1] // z_rows
         z_first = z_chunks // 2
-        served, dtab = pl.pallas_call(
-            functools.partial(gather_kernel, (n_layers, n_emb, CAP, per_dot, dots, z_first)),
-            out_shape=[jax.ShapeDtypeStruct((n_layers, n_serve, e_dim), BF), jax.ShapeDtypeStruct(tab_shape, F32)],
-            in_specs=[sm, sm, vm, hbm],
-            out_specs=[vm, hbm],
+        words = [jax.ShapeDtypeStruct((n_dev, CAP), I32)] * 3 + [jax.ShapeDtypeStruct((n_dev, lanes), I32)]
+        served, dtab, read_word, write_word, group_word, meta = pl.pallas_call(
+            functools.partial(gather_kernel, (n_layers, n_emb, CAP, per_dot, dots, z_first, slot_bits)),
+            out_shape=[jax.ShapeDtypeStruct((n_layers, n_serve, e_dim), BF), jax.ShapeDtypeStruct(tab_shape, F32)] + words,
+            in_specs=[sm, sm, vm, vm, vm, hbm],
+            out_specs=[vm, hbm, vm, vm, vm, vm],
             scratch_shapes=[pltpu.VMEM((n_layers, n_serve * 8, e_dim), BF), pltpu.VMEM((z_rows,) + tab_shape[2:], F32), dma((n_emb,)), dma],
             compiler_params=params(0),
             name='table_rows',
-        )(recv_loc, counts, pick, tables)
+        )(recv_loc, counts, recv_loc, counts, pick, tables)
 
         fb = 1024
         n_blk = ffn // fb
@@ -851,34 +888,33 @@
             name='forward',
         )(x1, cot_out, fetched, w_gate, w_proj, w_up, w_down, dtab)
 
-        got, got_gate, slots0 = pl.pallas_call(
+        got, got_gate, mixed0 = pl.pallas_call(
             functools.partial(backward_kernel, (n_back, n_blk, n_dp, n_emb, CAP, cw, nw, slab)),
             out_shape=[jax.ShapeDtypeStruct((n_back, n_slots // 8, e_dim // 128, 8, 128), F32), jax.ShapeDtypeStruct((n_slots // 8, e_dim // 128, 8, 128), F32),
-                       jax.ShapeDtypeStruct((n_dp, n_serve, e_dim), BF)],
+                       jax.ShapeDtypeStruct((n_slots, e_dim), BF)],
             in_specs=[hbm, hbm, hbm, vm, vm, vm, vm, vm, vm, hbm, hbm, hbm, hbm, hbm],
-            out_specs=[hbm, hbm, vm],
+            out_specs=[hbm, hbm, hbm],
             scratch_shapes=[
                 pltpu.VMEM((tok, dim), BF), pltpu.VMEM((tok, dim), BF), pltpu.VMEM((tok, dim), F32), pltpu.VMEM((tok, fb), BF), pltpu.VMEM((tok, fb), BF),
                 pltpu.VMEM((tok, dim), BF), pltpu.VMEM((n_serve // 8, e_dim // 128, 8, 128), F32), pltpu.VMEM((n_serve // 8, e_dim // 128, 8, 128), F32),
-                pltpu.VMEM((tok, e_dim), F32), pltpu.VMEM((tok, e_dim), BF), pltpu.VMEM((2, tok, fb), F32), *w_bufs,
-                dma((4,)), dma((2, 2)), dma((2,)), dma((2, n_dev - 1)), dma((2,)), dma((n_back + 1, n_dev - 1)),
+                pltpu.VMEM((n_serve, e_dim), BF), pltpu.VMEM((tok, e_dim), F32), pltpu.VMEM((tok, e_dim), BF), pltpu.VMEM((2, tok, fb), F32), *w_bufs,
+                dma((4,)), dma((2, 2)), dma((2,)), dma((3, n_dev - 1)), dma((3,)), dma((n_back + 2, n_dev - 1)),
             ],
             compiler_params=params(0, collective_id=2, has_side_effects=True),
             cost_estimate=pl.CostEstimate(flops=n_back * matmul_flops, bytes_accessed=400 << 20, transcendentals=0),
             name='backward',
         )(cot_out, x1, saved, rows, dgp, slot_row, gate0, gates, fetched, ups, w_up, w_down, w_gate, w_proj)
 
-        mixed0 = lax.all_to_all(slots0.reshape(n_dev, CAP, e_dim), MESH_AXES, 0, 0, tiled=True).reshape(n_slots, e_dim)
         dtab = pl.pallas_call(
-            functools.partial(scatter_kernel, (8, window, 32, z_chunks)),
+            functools.partial(scatter_kernel, (8, 32, z_chunks)),
             out_shape=jax.ShapeDtypeStruct(dtab.shape, F32),
             in_specs=[sm, sm, sm, sm, hbm, hbm, hbm, hbm],
             out_specs=hbm,
             input_output_aliases={7: 0},
             scratch_shapes=[pltpu.VMEM((n_back, n_slots * 2, 128), F32), pltpu.VMEM((n_slots // 8,) + tab_shape[2:], F32),
-                            pltpu.VMEM((n_slots, e_dim), BF), pltpu.VMEM((n_slots,) + tab_shape[2:], F32),
-                            pltpu.VMEM((2, n_back, window) + tab_shape[2:], F32), pltpu.VMEM((n_slots // 8,) + tab_shape[2:], F32),
-                            pltpu.VMEM((z_rows,) + tab_shape[2:], F32), pltpu.SMEM((n_slots,), I32), dma((3,)), dma((3,)), dma],
+                            pltpu.VMEM((n_slots, e_dim), BF), pltpu.VMEM((2, n_layers, CAP) + tab_shape[2:], F32),
+                            pltpu.VMEM((n_slots // 8,) + tab_shape[2:], F32), pltpu.VMEM((z_rows,) + tab_shape[2:], F32),
+                            pltpu.SMEM((CAP,), I32), dma((2,)), dma((3,)), dma((z_chunks,))],
             compiler_params=params(0),
             name='scatter',
         )(read_word, write_word, group_word, meta, got.reshape(n_back, n_slots * 2, 128), got_gate, mixed0, dtab)

time: 529 us -> 521 us (0.985)
  other arithmetic: 12.6 us -> 0 us
  Pallas kernels: 506 us -> 518 us
    pallas_call x1, Pallas kernels: 197 us -> 208 us  [device_body(): pl.pallas_call(functools.partial(backward_kernel, (n_back, n_blk, n_dp, n...]
  transfers between devices with their start and end apart: 1 -> 0, of which waited for: 1 -> 0; matrix products, arithmetic and copies ran while one was open for 3% -> 0% of each run, Pallas kernels for 0% -> 0%
where the time goes in v9:
time: 521 us; the launch traced here: 519 us
  Pallas kernels  518 us (99%)
    pallas_call x1, Pallas kernels, device_body(): pl.pallas_call(functools.partial(backward_kernel, (n_back, n_blk, n_dp, n...  208 us
    pallas_call x1, Pallas kernels, device_body(): pl.pallas_call(functools.partial(forward_kernel, (n_back, n_blk, cw, nw,...  191 us
    pallas_call x1, Pallas kernels, device_body(): pl.pallas_call(functools.partial(first_kernel, (n_dp, n_emb, CAP, n_blk,...  69 us
    pallas_call x1, Pallas kernels, device_body(): pl.pallas_call(functools.partial(scatter_kernel, (8, 32, z_chunks)), out_...  24.7 us
    pallas_call x1, Pallas kernels, device_body(): pl.pallas_call(functools.partial(gather_kernel, (n_layers, n_emb, CAP, pe...  16.4 us

profile of v9, /device:TPU:0, one launch (start us, length us, event | category | flops | bytes accessed | tf_op | source)
XLA Modules:
  0.0 518.8 jit_solution(10804375378668773520)
XLA Ops:
  0.6 9.3 %plan.1 = (s32[8,4,128]{2,1,0:T(4,128)}, s32[8,256]{1,0:T(8,128)}, s32[8,128]{1,0:T(8,128)}, s32[1024,1]{1,0:T(8,128)}, s32[1,512]{1,0:T(1,128)}, /*index=5*/s32[512,1]{1,0:T(8,128)}) custom-call(s32[4,128]{1,0:T(4,128)} %bitcast.6), custom_call_target="tpu_custom_call" | custom-call | tf_op jit(solution)/shard_map/plan/pallas_call | solution.py:816
  9.9 16.4 %table_rows.1 = (bf16[4,1024,256]{2,1,0:T(8,128)(2,1)}, f32[4,4008,2,8,128]{4,3,2,1,0:T(8,128)}, s32[8,256]{1,0:T(8,128)}, s32[8,256]{1,0:T(8,128)}, s32[8,256]{1,0:T(8,128)}, /*index=5*/s32[8,128]{1,0:T(8,128)}) custom-call(s32[8,256]{1,0:T(8,128)} %get-tuple-element.27.loc_ref.recv_ref, s32[8,128]{1,0:T(8,128)} %get-tuple-element.28.counts_ref.tally_ref, ...), custom_call_target="tpu_custom_call" | custom-call | tf_op jit(solution)/shard_map/table_rows/pallas_call | solution.py:831
  26.3 69.0 %first_layer.1 = (bf16[512,3072]{1,0:T(8,128)(2,1)}, f32[1,512,256]{2,1,0:T(8,128)}, bf16[4,512,256]{2,1,0:T(8,128)(2,1)}) custom-call(bf16[512,3072]{1,0:T(8,128)(2,1)} %x_hbm.1, s32[512,1]{1,0:T(8,128)} %get-tuple-element.26.slot_ref, bf16[4,1024,256]{2,1,0:T(8,128)(2,1)} %get-tuple-element.30.served_hbm, bf16[4,3072,256]{2,1,0:T(8,128)(2,1)} %wg_hbm.5, ...), custom_call_target="tpu_custom_call" | custom-call | flops 51539607552 | bytes 104857600 | tf_op jit(solution)/shard_map/first_layer/pallas_call | solution.py:849
  95.3 190.7 %forward.1 = (bf16[512,3072]{1,0:T(8,128)(2,1)}, bf16[2,512,3072]{2,1,0:T(8,128)(2,1)}, f32[3,512,8192]{2,1,0:T(8,128)}, f32[3,512,256]{2,1,0:T(8,128)}, f32[512...) custom-call(bf16[512,3072]{1,0:T(8,128)(2,1)} %get-tuple-element.31., ...), custom_call_target="tpu_custom_call", output_to_operand_aliasing={{6}: (7, {})} | custom-call | flops 154618822656 | bytes 419430400 | tf_op jit(solution)/shard_map/forward/pallas_call | solution.py:867
  286.0 207.9 %backward.1 = (f32[3,256,2,8,128]{4,3,2,1,0:T(8,128)}, f32[256,2,8,128]{3,2,1,0:T(8,128)}, bf16[2048,256]{1,0:T(8,128)(2,1)}) custom-call(bf16[512,3072]{1,0:T(8,128)(2,1)} %cot_hbm.3, bf16[512,3072]{1,0:T(8,128)(2,1)} %get-tuple-element.31.x_hbm.x1_hbm, bf16[2,512,3072]{2,1,0:T(8,128)(2,1)} %get-tuple-element.39.saved_hbm, ...), custom_call_target="tpu_custom_call" | custom-call | flops 154618822656 | bytes 419430400 | tf_op jit(solution)/shard_map/backward/pallas_call | solution.py:891
  493.9 24.7 %scatter.1 = f32[4,4008,2,8,128]{4,3,2,1,0:T(8,128)} custom-call(s32[8,256]{1,0:T(8,128)} %get-tuple-element.35.read_ref, s32[8,256]{1,0:T(8,128)} %get-tuple-element.36.write_ref, s32[8,256]{1,0:T(8,128)} %get-tuple-element.37.group_ref, s32[8,128]{1,0:T(8,128)} %get-tuple-element.38.meta_ref, ...), custom_call_target="tpu_custom_call", output_to_operand_aliasing={{}: (7, {})} | custom-call | tf_op jit(solution)/shard_map/scatter/pallas_call | solution.py:908
